TPU v7x, 128 devices: a whole 4x4x4 slice. The times are simulated.
128 devices in a mesh: flow: 128 (over y, z, x, core).
Axes of the slice: x: 4, y: 4, z: 4, core: 2. Of those that a mesh axis runs over, the one named last changes fastest.
Arguments:
- forcing: float32 [2, 12, 3072, 1024], P(None, None, 'flow'), may hold values from -1000 to 1000
- viscosity: float32 [3072, 1024], P('flow'), may hold values from 0.5 to 4
- friction: float32 [3072, 1024], P('flow'), may hold values from 1 to 30
- rotation: float32 [3072, 1024], P('flow'), may hold values from -2 to 2
- vertical: float32 [11, 3072, 1024], P(None, 'flow'), may hold values from 2 to 20
- ice_mask: int32 [3072, 1024], P('flow'), may hold values 0 or 1
- grounded: int32 [3072, 1024], P('flow'), may hold values 0 or 1
Outputs:
- solution: float32 [2, 12, 3072, 1024], P(None, None, 'flow')
- residual: float32 [2, 12, 3072, 1024], P(None, None, 'flow')
All inputs are finite; a program needn't handle non-finite values. No bound on the sum of `ice_mask` or of `grounded` on one device may be relied on, other than what follows from the above.
Results may differ from a plain program's by a relative error of at most 0.0003.
Values sent between devices are 32-bit elements; how exact they have to be, the bound alone decides.
No kernel may reach another device: no remote copies, remote signals or barrier semaphores. Data moves between devices by JAX's collectives and lax.ppermute only.
A program may use at most 192 MiB of HBM per device.

v0:
```python
import jax
import jax.numpy as jnp
from jax import lax
from jax.sharding import Mesh
from jax.sharding import PartitionSpec as P

ITERS = 3
FLOW = ("flow_0", "flow_1", "flow_2", "flow_3")


epsilon = 1e-06
relaxation = 0.5
reach_weights = (1.0, 0.6, 0.35, 0.2)


def sent_to_all(value, axis):
    copies = jnp.broadcast_to(value, (lax.axis_size(axis), *value.shape))
    return lax.all_to_all(copies, axis, split_axis=0, concat_axis=0, tiled=True)


def of_everyone(value, axis):
    return sent_to_all(value, axis).sum(axis=0)


def by_axis(value, axes):
    far, near = axes
    nearer = of_everyone(value, near)
    return of_everyone(nearer, far)


def extended(block, sides, width):
    for axis, dim in sides:
        count = lax.axis_size(axis)
        forward = [(i, i + 1) for i in range(count - 1)]
        backward = [(target, source) for source, target in forward]
        low = lax.ppermute(
            lax.slice_in_dim(block, block.shape[dim] - width, None, axis=dim), axis, forward
        )
        high = lax.ppermute(lax.slice_in_dim(block, 0, width, axis=dim), axis, backward)
        block = jnp.concatenate([low, block, high], axis=dim)
    return block


def layer_coefs(basal_drag, vertical):
    zero_plane = jnp.zeros_like(vertical[:1])
    upper_coef = jnp.concatenate([vertical, zero_plane], 0)
    lower_coef = jnp.concatenate([zero_plane, vertical], 0)
    bottom = jnp.concatenate([basal_drag[None], jnp.zeros_like(vertical)], 0)
    return (upper_coef, lower_coef, bottom)


def stencil_apply(padded, viscosity, basal_drag, rotation, ice_cover, vertical):
    row_count = padded.shape[2] - 8
    values = padded[:, :, 4 : 4 + row_count]
    horizontal = jnp.zeros_like(values)
    for order, weight in enumerate(reach_weights):
        offset = order + 1
        forward_cells = padded[:, :, 4 + offset : 4 + offset + row_count]
        backward_cells = padded[:, :, 4 - offset : 4 - offset + row_count]
        horizontal = horizontal + weight * (2.0 * values - forward_cells - backward_cells)
    padded_cross = jnp.pad(values, ((0, 0), (0, 0), (0, 0), (1, 1)))
    horizontal = horizontal + (2.0 * values - padded_cross[..., 2:] - padded_cross[..., :-2])
    upper_coef, lower_coef, bottom = layer_coefs(basal_drag, vertical)
    diagonal = upper_coef + lower_coef + bottom + relaxation * viscosity
    shifted_up = jnp.concatenate([values[:, 1:], jnp.zeros_like(values[:, :1])], 1)
    shifted_down = jnp.concatenate([jnp.zeros_like(values[:, :1]), values[:, :-1]], 1)
    turned = jnp.stack([values[1], -values[0]])
    stencil = (
        diagonal * values
        - upper_coef * shifted_up
        - lower_coef * shifted_down
        + rotation * turned
        + viscosity * horizontal
    )
    return jnp.where(ice_cover > 0.5, stencil, values)


def precondition(vector, viscosity, basal_drag, rotation, ice_cover, vertical):
    active = ice_cover > 0.5
    horiz_total = 2.0 * sum(reach_weights) + 2.0
    upper_coef, lower_coef, bottom = layer_coefs(basal_drag, vertical)
    real_part = upper_coef + lower_coef + bottom + relaxation * viscosity + horiz_total * viscosity
    real_part = jnp.where(active, real_part, jnp.ones_like(real_part))
    imag_part = jnp.where(active, rotation, jnp.zeros_like(rotation))
    coupling = jnp.where(active, vertical, jnp.zeros_like(vertical))
    layer_total = vector.shape[1]
    inv_real, inv_imag, carry_former, carry_latter = ([], [], [], [])
    for layer in range(layer_total):
        pivot_real = real_part[layer]
        pivot_imag = imag_part
        source_former = vector[0, layer]
        source_latter = vector[1, layer]
        if layer > 0:
            link = coupling[layer - 1]
            pivot_real = pivot_real - link * link * inv_real[layer - 1]
            pivot_imag = pivot_imag - link * link * inv_imag[layer - 1]
            source_former = source_former + link * carry_former[layer - 1]
            source_latter = source_latter + link * carry_latter[layer - 1]
        inverse_det = 1.0 / (pivot_real * pivot_real + pivot_imag * pivot_imag)
        entry_real = pivot_real * inverse_det
        entry_imag = -pivot_imag * inverse_det
        inv_real.append(entry_real)
        inv_imag.append(entry_imag)
        carry_former.append(entry_real * source_former + entry_imag * source_latter)
        carry_latter.append(entry_real * source_latter - entry_imag * source_former)
    result_former = [None] * layer_total
    result_latter = [None] * layer_total
    result_former[layer_total - 1] = carry_former[layer_total - 1]
    result_latter[layer_total - 1] = carry_latter[layer_total - 1]
    for layer in range(layer_total - 2, -1, -1):
        link = coupling[layer]
        pushed_former = link * result_former[layer + 1]
        pushed_latter = link * result_latter[layer + 1]
        result_former[layer] = (
            carry_former[layer] + inv_real[layer] * pushed_former + inv_imag[layer] * pushed_latter
        )
        result_latter[layer] = (
            carry_latter[layer] + inv_real[layer] * pushed_latter - inv_imag[layer] * pushed_former
        )
    solved = jnp.stack([jnp.stack(result_former), jnp.stack(result_latter)])
    return jnp.where(active, solved, vector)


def least_squares(columns, start):
    count_cols = len(columns)
    givens_rhs = [start] + [start * 0.0 for index in range(count_cols)]
    cosines, sines, upper_cols = ([], [], [])
    for column_index, column_in in enumerate(columns):
        column = list(column_in)
        for row_index in range(column_index):
            rotated_a = (
                cosines[row_index] * column[row_index] + sines[row_index] * column[row_index + 1]
            )
            rotated_b = (
                -sines[row_index] * column[row_index] + cosines[row_index] * column[row_index + 1]
            )
            column[row_index] = rotated_a
            column[row_index + 1] = rotated_b
        radius = jnp.sqrt(
            column[column_index] * column[column_index]
            + column[column_index + 1] * column[column_index + 1]
        )
        cosine = column[column_index] / radius
        sine_value = column[column_index + 1] / radius
        column[column_index] = radius
        cosines.append(cosine)
        sines.append(sine_value)
        upper_cols.append(column)
        next_rhs = -sine_value * givens_rhs[column_index]
        givens_rhs[column_index] = cosine * givens_rhs[column_index]
        givens_rhs[column_index + 1] = next_rhs
    factors = [None] * count_cols
    for column_index in range(count_cols - 1, -1, -1):
        accum = givens_rhs[column_index]
        for later in range(column_index + 1, count_cols):
            accum = accum - upper_cols[later][column_index] * factors[later]
        factors[column_index] = accum / upper_cols[column_index][column_index]
    return factors


def body(forcing, viscosity, friction, rotation, vertical, ice_mask, grounded):
    ice_cover = jnp.where(ice_mask > 0, jnp.ones_like(viscosity), jnp.zeros_like(viscosity))
    basal_drag = jnp.where(grounded > 0, friction, jnp.zeros_like(friction))
    squares_total = by_axis(jnp.sum(forcing * forcing), (("flow_0", "flow_1", "flow_2"), "flow_3"))
    load_norm = jnp.sqrt(squares_total + epsilon)
    local_coefs = (viscosity, basal_drag, rotation, ice_cover, vertical)
    halo_depth = 0

    def product(search):
        padded = extended(search, ((FLOW, 2),), 4)
        return (stencil_apply(padded, *local_coefs), 0)

    krylov = [(forcing / load_norm, halo_depth)]
    searches = []
    columns = []
    for iteration in range(ITERS):
        current, depth_from = krylov[iteration]
        search = precondition(current, *local_coefs)
        searches.append((search, depth_from))
        image, depth_to = product(search)
        aligned = [krylov[index][0] for index in range(iteration + 1)]
        column = []
        centre_image = image
        local_terms = [jnp.sum(centre_image * vector) for vector in aligned]
        local_terms.append(jnp.sum(centre_image * centre_image))
        products = by_axis(jnp.stack(local_terms), (("flow_0", "flow_1", "flow_2"), "flow_3"))
        remaining = products[len(aligned)]
        for index, vector in enumerate(aligned):
            image = image - products[index] * vector
            remaining = remaining - products[index] * products[index]
            column.append(products[index])
        new_norm = jnp.sqrt(jnp.maximum(remaining, 0.0) + epsilon)
        column.append(new_norm)
        columns.append(column)
        if iteration + 1 < ITERS:
            krylov.append((image / new_norm, depth_to))
    factors = least_squares(columns, load_norm)
    solution = factors[0] * searches[0][0]
    for index in range(1, ITERS):
        solution = solution + factors[index] * searches[index][0]
    applied, applied_depth = product(solution)
    residual = forcing - applied
    return (solution, residual)


def solution(mesh):
    finer = Mesh(mesh.devices.reshape(4, 4, 4, 2), ("flow_0", "flow_1", "flow_2", "flow_3"))
    return jax.shard_map(
        body,
        mesh=finer,
        in_specs=(
            P(None, None, FLOW, None),
            P(FLOW, None),
            P(FLOW, None),
            P(FLOW, None),
            P(None, FLOW, None),
            P(FLOW, None),
            P(FLOW, None),
        ),
        out_specs=(P(None, None, FLOW, None), P(None, None, FLOW, None)),
        check_vma=False,
    )
```

profile of v0, /device:TPU:8, one launch (start us, length us, event | category | flops | bytes accessed | tf_op | source)
XLA Modules:
  0.0 239.4 jit_solution(10713103777908790851)
XLA Ops:
  0.7 3.0 %multiply_reduce_fusion.9 = f32[]{:T(128)} fusion(f32[2,12,24,1024]{3,2,1,0:T(8,128)} %param.7), kind=kLoop, calls=%fused_computation.192 | loop fusion | flops 1179647 | bytes 2359300 | tf_op jit(solution)/shard_map/reduce_sum | solution.py:164
  3.7 0.6 broadcast_in_dim.43
  4.3 3.7 %all_to_all.48 = f32[2,1,1]{2,1,0:T(1,128)S(1)} all-to-all(f32[2,1,1]{2,1,0:T(1,128)S(1)} %broadcast_in_dim.43), channel_id=1, replica_groups=mesh['flow_0'=4,'flow_1'=4,'flow_2'=4,'flow_3'=2] {'flow_3'}, dimensions={0} | all-to-all | bytes 16 | tf_op jit(solution)/shard_map/all_to_all | solution.py:18
  8.0 0.6 reduce_sum.163
  8.6 1.3 broadcast_in_dim.44
  9.9 11.6 %all-to-all-start.1 = ((f32[64,1,1]{2,1,0:T(1,128)}), f32[64,1,1]{2,1,0:T(1,128)}, u32[]{:S(2)}, u32[]{:S(2)}) async-start(f32[64,1,1]{2,1,0:T(1,128)} %broadcast_in_dim.44), calls=%async_computation.1 | async-start | bytes 65536 | tf_op jit(solution)/shard_map/all_to_all | solution.py:18
  21.8 2.0 add_add_fusion
  23.8 1.0 copy-done.80
  24.9 1.0 fusion.161
  25.9 4.3 %all-to-all-done.1 = f32[64,1,1]{2,1,0:T(1,128)} async-done(((f32[64,1,1]{2,1,0:T(1,128)}), f32[64,1,1]{2,1,0:T(1,128)}, u32[]{:S(2)}, u32[]{:S(2)}) %all-to-all-start.1) | async-done | bytes 288 | tf_op jit(solution)/shard_map/all_to_all | solution.py:18
  30.1 1.4 reduce_sum.164
  33.8 0.6 fusion.147
  34.6 1.5 constant_dynamic-update-slice_fusion.11
  38.2 0.5 maximum_select_fusion
  39.9 3.0 %collective-permute-start = (f32[2,12,4,1024]{3,1,2,0:T(8,128)S(1)}, f32[2,12,4,1024]{3,1,2,0:T(8,128)S(1)}, u32[]{:S(2)}, u32[]{:S(2)}) collective-permute-start(f32[2,12,4,1024]{3,1,2,0:T(8,128)S(1)} %copy.148), channel_id=1, source_target_pairs={{1,0},{2,1},{3,2},{4,3},{5,4},{6,5},{7,6},{8,7},{9,8},{10,9},{11,1... | collective-permute-start | bytes 1179656 | tf_op jit(solution)/shard_map/ppermute | solution.py:39
  43.1 1.9 collective-permute-start.1
  45.4 0.6 fusion.251
  46.0 3.5 %collective-permute-done = f32[2,12,4,1024]{3,1,2,0:T(8,128)S(1)} collective-permute-done((f32[2,12,4,1024]{3,1,2,0:T(8,128)S(1)}, f32[2,12,4,1024]{3,1,2,0:T(8,128)S(1)}, u32[]{:S(2)}, u32[]{:S(2)}) %collective-permute-start) | collective-permute-done | bytes 393248 | tf_op jit(solution)/shard_map/ppermute | solution.py:39
  49.8 8.0 %collective-permute-done.1 = f32[2,12,4,1024]{3,1,2,0:T(8,128)S(1)} collective-permute-done((f32[2,12,4,1024]{3,1,2,0:T(8,128)S(1)}, f32[2,12,4,1024]{3,1,2,0:T(8,128)S(1)}, u32[]{:S(2)}, u32[]{:S(2)}) %collective-permute-start.1) | collective-permute-done | bytes 393248 | tf_op jit(solution)/shard_map/ppermute | solution.py:36
  58.2 6.8 %multiply_reduce_fusion.8 = (f32[]{:T(128)}, f32[]{:T(128)}, f32[2,12,24,1024]{3,2,1,0:T(8,128)}) fusion(f32[2,12,24,1024]{3,2,1,0:T(8,128)S(1)} %maximum_select_fusion, f32[2,12,4,1024]{3,2,1,0:T(4,128)S(1)} %copy.151, f32[2,12,4,1024]{3,2,1,0:T(4,128)S(1)} %copy.149, f32[24,1024]{1,0:T(8,128)S(1)} %copy-done.100, ...), kind=kLoop, calls=%fused_computation.191 | loop fusion | flops 24772608 | bytes 18309132 | tf_op jit(solution)/shard_map/reduce_sum | solution.py:184
  65.0 1.4 pad_maximum_fusion.8
  66.4 3.7 %all_to_all.49 = f32[2,1,2]{2,1,0:T(1,128)S(1)} all-to-all(f32[2,1,2]{2,1,0:T(1,128)S(1)} %broadcast_in_dim.46), channel_id=1, replica_groups=mesh['flow_0'=4,'flow_1'=4,'flow_2'=4,'flow_3'=2] {'flow_3'}, dimensions={0} | all-to-all | bytes 32 | tf_op jit(solution)/shard_map/all_to_all | solution.py:18
  70.1 13.0 %all_to_all.50 = f32[64,1,2]{2,1,0:T(1,128)} all-to-all(f32[64,1,2]{2,1,0:T(1,128)S(1)} %broadcast_in_dim.47), channel_id=1, replica_groups=mesh['flow_0'=4,'flow_1'=4,'flow_2'=4,'flow_3'=2] {'flow_0','flow_1','fl..., dimensions={0} | all-to-all | bytes 1024 | tf_op jit(solution)/shard_map/all_to_all | solution.py:18
  83.1 0.8 reduce_sum.168
  84.0 0.6 fusion.256
  86.7 3.0 %subtract_divide_fusion.1 = f32[2,12,24,1024]{3,2,1,0:T(8,128)S(1)} fusion(f32[2,12,24,1024]{3,2,1,0:T(8,128)} %get-tuple-element.62, f32[]{:T(128)S(6)} %sqrt.22, f32[]{:T(128)} %bitcast.77, f32[2,12,24,1024]{3,2,1,0:T(8,128)S(1)} %copy-done, f32[]{:T(128)S(6)} %sqrt.21), kind=kLoop, calls=%fused_computation.189 | loop fusion | flops 2359296 | bytes 7077900 | tf_op jit(solution)/shard_map/div | solution.py:196
  91.7 0.8 constant_dynamic-update-slice_fusion.35
  94.5 0.5 maximum_select_fusion.1
  96.2 2.8 %collective-permute-start.2 = (f32[2,12,4,1024]{3,1,2,0:T(8,128)S(1)}, f32[2,12,4,1024]{3,1,2,0:T(8,128)S(1)}, u32[]{:S(2)}, u32[]{:S(2)}) collective-permute-start(f32[2,12,4,1024]{3,1,2,0:T(8,128)S(1)} %copy.154), channel_id=1, source_target_pairs={{1,0},{2,1},{3,2},{4,3},{5,4},{6,5},{7,6},{8,7},{9,8},{10,9},{11,1... | collective-permute-start | bytes 1179656 | tf_op jit(solution)/shard_map/ppermute | solution.py:39
  99.3 1.9 collective-permute-start.3
  101.6 0.6 fusion.248
  102.2 3.5 %collective-permute-done.2 = f32[2,12,4,1024]{3,1,2,0:T(8,128)S(1)} collective-permute-done((f32[2,12,4,1024]{3,1,2,0:T(8,128)S(1)}, f32[2,12,4,1024]{3,1,2,0:T(8,128)S(1)}, u32[]{:S(2)}, u32[]{:S(2)}) %collective-permute-start.2) | collective-permute-done | bytes 393248 | tf_op jit(solution)/shard_map/ppermute | solution.py:39
  106.0 8.0 %collective-permute-done.3 = f32[2,12,4,1024]{3,1,2,0:T(8,128)S(1)} collective-permute-done((f32[2,12,4,1024]{3,1,2,0:T(8,128)S(1)}, f32[2,12,4,1024]{3,1,2,0:T(8,128)S(1)}, u32[]{:S(2)}, u32[]{:S(2)}) %collective-permute-start.3) | collective-permute-done | bytes 393248 | tf_op jit(solution)/shard_map/ppermute | solution.py:36
  114.3 7.0 %multiply_reduce_fusion.6 = (f32[]{:T(128)}, f32[]{:T(128)}, f32[]{:T(128)}, f32[2,12,24,1024]{3,2,1,0:T(8,128)}) fusion(f32[2,12,24,1024]{3,2,1,0:T(8,128)S(1)} %subtract_divide_fusion.1, f32[2,12,24,1024]{3,2,1,0:T(8,128)S(1)} %maximum_select_fusion.1, f32[2,12,4,1024]{3,2,1,0:T(4,128)S(1)} %copy.157, f32[2,12,4,1024]{3,2,1,0:T(4,128)S(1)} %copy.155, ...), kind=kLoop, calls=%fused_computation.188 | loop fusion | flops 25952256 | bytes 20668432 | tf_op jit(solution)/shard_map/reduce_sum | solution.py:184
  121.3 2.0 pad_maximum_fusion.9
  123.3 3.7 %all_to_all.51 = f32[2,1,3]{2,1,0:T(1,128)S(1)} all-to-all(f32[2,1,3]{2,1,0:T(1,128)S(1)} %broadcast_in_dim.48), channel_id=1, replica_groups=mesh['flow_0'=4,'flow_1'=4,'flow_2'=4,'flow_3'=2] {'flow_3'}, dimensions={0} | all-to-all | bytes 48 | tf_op jit(solution)/shard_map/all_to_all | solution.py:18
  127.0 0.6 broadcast_in_dim.49
  127.6 5.1 %all-to-all-start.5 = ((f32[64,1,3]{2,1,0:T(1,128)}), f32[64,1,3]{2,1,0:T(1,128)}, u32[]{:S(2)}, u32[]{:S(2)}) async-start(f32[64,1,3]{2,1,0:T(1,128)} %broadcast_in_dim.49), calls=%async_computation.5 | async-start | bytes 65536 | tf_op jit(solution)/shard_map/all_to_all | solution.py:18
  132.8 8.1 %all-to-all-done.5 = f32[64,1,3]{2,1,0:T(1,128)} async-done(((f32[64,1,3]{2,1,0:T(1,128)}), f32[64,1,3]{2,1,0:T(1,128)}, u32[]{:S(2)}, u32[]{:S(2)}) %all-to-all-start.5) | async-done | bytes 800 | tf_op jit(solution)/shard_map/all_to_all | solution.py:18
  140.9 0.8 reduce_sum.173
  141.7 0.7 fusion.255
  145.7 4.6 %subtract_divide_fusion = f32[2,12,24,1024]{3,2,1,0:T(8,128)S(1)} fusion(f32[2,12,24,1024]{3,2,1,0:T(8,128)} %copy-done.1, f32[2,12,24,1024]{3,2,1,0:T(8,128)} %get-tuple-element.39, f32[]{:T(128)S(6)} %sqrt.24, f32[]{:T(128)} %bitcast.134, f32[]{:T(128)} %bitcast.133, f32[2,12,24,1024]{3,2,1,0:T(8,128)S(1)} %copy-done, f32[]{:T(128)S(6)} %sqrt.21), kind=kLoop, calls=%fused_computation.185 | loop fusion | flops 3538944 | bytes 9437200 | tf_op jit(solution)/shard_map/div | solution.py:196
  150.5 0.5 fusion.99
  152.0 0.8 constant_dynamic-update-slice_fusion.59
  154.7 0.5 maximum_select_fusion.2
  156.3 3.0 %collective-permute-start.4 = (f32[2,12,4,1024]{3,1,2,0:T(8,128)S(1)}, f32[2,12,4,1024]{3,1,2,0:T(8,128)S(1)}, u32[]{:S(2)}, u32[]{:S(2)}) collective-permute-start(f32[2,12,4,1024]{3,1,2,0:T(8,128)S(1)} %copy.160), channel_id=1, source_target_pairs={{1,0},{2,1},{3,2},{4,3},{5,4},{6,5},{7,6},{8,7},{9,8},{10,9},{11,1... | collective-permute-start | bytes 1179656 | tf_op jit(solution)/shard_map/ppermute | solution.py:39
  159.5 1.9 collective-permute-start.5
  161.8 0.6 fusion.245
  162.4 3.5 %collective-permute-done.4 = f32[2,12,4,1024]{3,1,2,0:T(8,128)S(1)} collective-permute-done((f32[2,12,4,1024]{3,1,2,0:T(8,128)S(1)}, f32[2,12,4,1024]{3,1,2,0:T(8,128)S(1)}, u32[]{:S(2)}, u32[]{:S(2)}) %collective-permute-start.4) | collective-permute-done | bytes 393248 | tf_op jit(solution)/shard_map/ppermute | solution.py:39
  166.2 8.0 %collective-permute-done.5 = f32[2,12,4,1024]{3,1,2,0:T(8,128)S(1)} collective-permute-done((f32[2,12,4,1024]{3,1,2,0:T(8,128)S(1)}, f32[2,12,4,1024]{3,1,2,0:T(8,128)S(1)}, u32[]{:S(2)}, u32[]{:S(2)}) %collective-permute-start.5) | collective-permute-done | bytes 393248 | tf_op jit(solution)/shard_map/ppermute | solution.py:36
  174.5 6.3 %multiply_reduce_fusion.3 = (f32[]{:T(128)}, f32[]{:T(128)}, f32[]{:T(128)}, f32[]{:T(128)}) fusion(f32[2,12,24,1024]{3,2,1,0:T(8,128)S(1)} %subtract_divide_fusion, f32[2,12,24,1024]{3,2,1,0:T(8,128)S(1)} %copy-done.2, f32[2,12,24,1024]{3,2,1,0:T(8,128)S(1)} %maximum_select_fusion.2, f32[2,12,4,1024]{3,2,1,0:T(4,128)S(1)} %copy.163, ...), kind=kLoop, calls=%fused_computation.184 | loop fusion | flops 27131904 | bytes 20668436 | tf_op jit(solution)/shard_map/reduce_sum | solution.py:184
  180.8 2.5 %pad_maximum_fusion.10 = f32[4]{0:T(128)S(1)} fusion(f32[1]{0:T(128)} %bitcast.189, f32[1]{0:T(128)} %bitcast.188, f32[1]{0:T(128)} %bitcast.187, f32[1]{0:T(128)} %bitcast.186), kind=kLoop, calls=%fused_computation.631 | loop fusion | flops 12 | bytes 32 | tf_op jit(solution)/shard_map/stack | solution.py:186
  183.3 3.7 %all_to_all.52 = f32[2,1,4]{2,1,0:T(1,128)S(1)} all-to-all(f32[2,1,4]{2,1,0:T(1,128)S(1)} %broadcast_in_dim.50), channel_id=1, replica_groups=mesh['flow_0'=4,'flow_1'=4,'flow_2'=4,'flow_3'=2] {'flow_3'}, dimensions={0} | all-to-all | bytes 64 | tf_op jit(solution)/shard_map/all_to_all | solution.py:18
  187.0 0.6 broadcast_in_dim.96
  187.6 4.7 %all-to-all-start.7 = ((f32[64,1,4]{2,1,0:T(1,128)}), f32[64,1,4]{2,1,0:T(1,128)S(1)}, u32[]{:S(2)}, u32[]{:S(2)}) async-start(f32[64,1,4]{2,1,0:T(1,128)} %broadcast_in_dim.96), calls=%async_computation.7 | async-start | bytes 65536 | tf_op jit(solution)/shard_map/all_to_all | solution.py:18
  195.6 5.4 %all-to-all-done.7 = f32[64,1,4]{2,1,0:T(1,128)S(1)} async-done(((f32[64,1,4]{2,1,0:T(1,128)}), f32[64,1,4]{2,1,0:T(1,128)S(1)}, u32[]{:S(2)}, u32[]{:S(2)}) %all-to-all-start.7) | async-done | bytes 1056 | tf_op jit(solution)/shard_map/all_to_all | solution.py:18
  201.0 0.6 fusion.254
  209.8 4.9 %multiply_add_fusion = f32[2,12,24,1024]{3,2,1,0:T(8,128)S(1)} fusion(f32[]{:T(128)S(6)} %div.125, f32[]{:T(128)S(6)} %div.126, f32[]{:T(128)S(6)} %div.127, f32[2,12,24,1024]{3,2,1,0:T(8,128)} %copy-done.3, f32[1,12,24,1024]{3,2,1,0:T(8,128)} %bitcast.1895, f32[1,12,24,1024]{3,2,1,0:T(8,128)} %bitcast.1903, pred[24,1024]{1,0:T(8,128)(4,1)} %copy-done.89, ...), kind=kLoop, calls=%fused_computation.180 | loop fusion | flops 7077888 | bytes 16539664 | tf_op jit(solution)/shard_map/add | solution.py:200
  215.1 3.0 %collective-permute-start.6 = (f32[2,12,4,1024]{3,1,2,0:T(8,128)S(1)}, f32[2,12,4,1024]{3,1,2,0:T(8,128)S(1)}, u32[]{:S(2)}, u32[]{:S(2)}) collective-permute-start(f32[2,12,4,1024]{3,1,2,0:T(8,128)S(1)} %copy.166), channel_id=1, source_target_pairs={{1,0},{2,1},{3,2},{4,3},{5,4},{6,5},{7,6},{8,7},{9,8},{10,9},{11,1... | collective-permute-start | bytes 1179656 | tf_op jit(solution)/shard_map/ppermute | solution.py:39
  218.3 2.2 collective-permute-start.7
  220.9 0.6 fusion.242
  221.5 3.3 %collective-permute-done.6 = f32[2,12,4,1024]{3,1,2,0:T(8,128)S(1)} collective-permute-done((f32[2,12,4,1024]{3,1,2,0:T(8,128)S(1)}, f32[2,12,4,1024]{3,1,2,0:T(8,128)S(1)}, u32[]{:S(2)}, u32[]{:S(2)}) %collective-permute-start.6) | collective-permute-done | bytes 393248 | tf_op jit(solution)/shard_map/ppermute | solution.py:39
  225.0 8.0 %collective-permute-done.7 = f32[2,12,4,1024]{3,1,2,0:T(8,128)S(1)} collective-permute-done((f32[2,12,4,1024]{3,1,2,0:T(8,128)S(1)}, f32[2,12,4,1024]{3,1,2,0:T(8,128)S(1)}, u32[]{:S(2)}, u32[]{:S(2)}) %collective-permute-start.7) | collective-permute-done | bytes 393248 | tf_op jit(solution)/shard_map/ppermute | solution.py:36
  233.4 6.0 %fusion.24 = f32[2,12,24,1024]{3,2,1,0:T(8,128)} fusion(f32[2,12,24,1024]{3,2,1,0:T(8,128)S(1)} %copy-done, f32[2,12,24,1024]{3,2,1,0:T(8,128)S(1)} %multiply_add_fusion, f32[2,12,4,1024]{3,2,1,0:T(4,128)S(1)} %copy.169, f32[2,12,4,1024]{3,2,1,0:T(4,128)S(1)} %copy.167, f32[1,12,24,1024]{3,2,1,0:T(8,128)S(1)} %get-tuple-element.148, ...), kind=kLoop, calls=%fused_computation.80 | loop fusion | flops 22413312 | bytes 18309120 | tf_op jit(solution)/shard_map/sub | solution.py:202
  (314 shorter events, 18.7 us)
Async XLA Ops:
  0.6 20.9 %copy-start.109 = (s32[24,1024]{1,0:T(8,128)S(1)}, s32[24,1024]{1,0:T(8,128)}, u32[]{:S(2)}) copy-start(s32[24,1024]{1,0:T(8,128)} %param.12) | copy-start | bytes 294916
  0.6 20.9 %copy-start.99 = (f32[24,1024]{1,0:T(8,128)S(1)}, f32[24,1024]{1,0:T(8,128)}, u32[]{:S(2)}) copy-start(f32[24,1024]{1,0:T(8,128)} %param.8) | copy-start | bytes 294916
  0.7 20.9 %copy-start.82 = (f32[11,24,1024]{2,1,0:T(8,128)S(1)}, f32[11,24,1024]{2,1,0:T(8,128)}, u32[]{:S(2)}) copy-start(f32[11,24,1024]{2,1,0:T(8,128)} %param.11) | copy-start | bytes 3244036
  0.7 21.1 %copy-start.113 = (s32[24,1024]{1,0:T(8,128)S(1)}, s32[24,1024]{1,0:T(8,128)}, u32[]{:S(2)}) copy-start(s32[24,1024]{1,0:T(8,128)} %param.13) | copy-start | bytes 294916
  0.7 21.1 %copy-start.112 = (f32[24,1024]{1,0:T(8,128)S(1)}, f32[24,1024]{1,0:T(8,128)}, u32[]{:S(2)}) copy-start(f32[24,1024]{1,0:T(8,128)} %param.9) | copy-start | bytes 294916
  9.9 20.3 %all-to-all-start.1 = ((f32[64,1,1]{2,1,0:T(1,128)}), f32[64,1,1]{2,1,0:T(1,128)}, u32[]{:S(2)}, u32[]{:S(2)}) async-start(f32[64,1,1]{2,1,0:T(1,128)} %broadcast_in_dim.44), calls=%async_computation.1 | async-start | bytes 65536 | tf_op jit(solution)/shard_map/all_to_all | solution.py:18
  23.8 8.3 %copy-start = (f32[2,12,24,1024]{3,2,1,0:T(8,128)S(1)}, f32[2,12,24,1024]{3,2,1,0:T(8,128)}, u32[]{:S(2)}) copy-start(f32[2,12,24,1024]{3,2,1,0:T(8,128)} %param.7) | copy-start | bytes 7077892
  39.9 9.7 %collective-permute-start = (f32[2,12,4,1024]{3,1,2,0:T(8,128)S(1)}, f32[2,12,4,1024]{3,1,2,0:T(8,128)S(1)}, u32[]{:S(2)}, u32[]{:S(2)}) collective-permute-start(f32[2,12,4,1024]{3,1,2,0:T(8,128)S(1)} %copy.148), channel_id=1, source_target_pairs={{1,0},{2,1},{3,2},{4,3},{5,4},{6,5},{7,6},{8,7},{9,8},{10,9},{11,1... | collective-permute-start | bytes 1179656 | tf_op jit(solution)/shard_map/ppermute | solution.py:39
  43.1 14.7 %collective-permute-start.1 = (f32[2,12,4,1024]{3,1,2,0:T(8,128)S(1)}, f32[2,12,4,1024]{3,1,2,0:T(8,128)S(1)}, u32[]{:S(2)}, u32[]{:S(2)}) collective-permute-start(f32[2,12,4,1024]{3,1,2,0:T(8,128)S(1)} %copy.150), channel_id=1, source_target_pairs={{0,1},{1,2},{2,3},{3,4},{4,5},{5,6},{6,7},{7,8},{8,9},{9,10},{10,1... | collective-permute-start | bytes 1179656 | tf_op jit(solution)/shard_map/ppermute | solution.py:36
  45.4 12.7 %copy-start.30 = (f32[12,24,1024]{2,1,0:T(8,128)S(1)}, f32[12,24,1024]{2,1,0:T(8,128)}, u32[]{:S(2)}) copy-start(f32[12,24,1024]{2,1,0:T(8,128)} %get-tuple-element.174) | copy-start | bytes 3538948
  45.4 12.7 %copy-start.34 = (f32[12,24,1024]{2,1,0:T(8,128)S(1)}, f32[12,24,1024]{2,1,0:T(8,128)}, u32[]{:S(2)}) copy-start(f32[12,24,1024]{2,1,0:T(8,128)} %get-tuple-element.175) | copy-start | bytes 3538948
  45.4 12.7 %copy-start.95 = (f32[24,1024]{1,0:T(8,128)S(1)}, f32[24,1024]{1,0:T(8,128)}, u32[]{:S(2)}) copy-start(f32[24,1024]{1,0:T(8,128)} %param.10) | copy-start | bytes 294916
  45.4 12.7 %copy-start.100 = (f32[24,1024]{1,0:T(8,128)S(1)}, f32[24,1024]{1,0:T(8,128)}, u32[]{:S(2)}) copy-start(f32[24,1024]{1,0:T(8,128)} %param.8) | copy-start | bytes 294916
  46.0 12.1 %copy-start.26 = (f32[12,24,1024]{2,1,0:T(8,128)S(1)}, f32[12,24,1024]{2,1,0:T(8,128)}, u32[]{:S(2)}) copy-start(f32[12,24,1024]{2,1,0:T(8,128)} %get-tuple-element.169) | copy-start | bytes 3538948
  86.5 3.2 %copy-start.6 = (f32[24,1024]{1,0:T(8,128)S(1)}, f32[24,1024]{1,0:T(8,128)}, u32[]{:S(2)}) copy-start(f32[24,1024]{1,0:T(8,128)} %get-tuple-element.101) | copy-start | bytes 294916
  86.5 3.2 %copy-start.9 = (f32[24,1024]{1,0:T(8,128)S(1)}, f32[24,1024]{1,0:T(8,128)}, u32[]{:S(2)}) copy-start(f32[24,1024]{1,0:T(8,128)} %get-tuple-element.102) | copy-start | bytes 294916
  86.5 3.2 %copy-start.12 = (f32[24,1024]{1,0:T(8,128)S(1)}, f32[24,1024]{1,0:T(8,128)}, u32[]{:S(2)}) copy-start(f32[24,1024]{1,0:T(8,128)} %get-tuple-element.103) | copy-start | bytes 294916
  89.9 24.4 %copy-start.1 = (f32[2,12,24,1024]{3,2,1,0:T(8,128)}, f32[2,12,24,1024]{3,2,1,0:T(8,128)S(1)}, u32[]{:S(2)}) copy-start(f32[2,12,24,1024]{3,2,1,0:T(8,128)S(1)} %subtract_divide_fusion.1) | copy-start | bytes 7077892
  96.2 9.5 %collective-permute-start.2 = (f32[2,12,4,1024]{3,1,2,0:T(8,128)S(1)}, f32[2,12,4,1024]{3,1,2,0:T(8,128)S(1)}, u32[]{:S(2)}, u32[]{:S(2)}) collective-permute-start(f32[2,12,4,1024]{3,1,2,0:T(8,128)S(1)} %copy.154), channel_id=1, source_target_pairs={{1,0},{2,1},{3,2},{4,3},{5,4},{6,5},{7,6},{8,7},{9,8},{10,9},{11,1... | collective-permute-start | bytes 1179656 | tf_op jit(solution)/shard_map/ppermute | solution.py:39
  99.3 14.7 %collective-permute-start.3 = (f32[2,12,4,1024]{3,1,2,0:T(8,128)S(1)}, f32[2,12,4,1024]{3,1,2,0:T(8,128)S(1)}, u32[]{:S(2)}, u32[]{:S(2)}) collective-permute-start(f32[2,12,4,1024]{3,1,2,0:T(8,128)S(1)} %copy.156), channel_id=1, source_target_pairs={{0,1},{1,2},{2,3},{3,4},{4,5},{5,6},{6,7},{7,8},{8,9},{9,10},{10,1... | collective-permute-start | bytes 1179656 | tf_op jit(solution)/shard_map/ppermute | solution.py:36
  101.5 12.8 %copy-start.31 = (f32[12,24,1024]{2,1,0:T(8,128)S(1)}, f32[12,24,1024]{2,1,0:T(8,128)}, u32[]{:S(2)}) copy-start(f32[12,24,1024]{2,1,0:T(8,128)} %get-tuple-element.174) | copy-start | bytes 3538948
  101.6 12.8 %copy-start.35 = (f32[12,24,1024]{2,1,0:T(8,128)S(1)}, f32[12,24,1024]{2,1,0:T(8,128)}, u32[]{:S(2)}) copy-start(f32[12,24,1024]{2,1,0:T(8,128)} %get-tuple-element.175) | copy-start | bytes 3538948
  101.6 12.8 %copy-start.96 = (f32[24,1024]{1,0:T(8,128)S(1)}, f32[24,1024]{1,0:T(8,128)}, u32[]{:S(2)}) copy-start(f32[24,1024]{1,0:T(8,128)} %param.10) | copy-start | bytes 294916
  101.6 12.7 %copy-start.101 = (f32[24,1024]{1,0:T(8,128)S(1)}, f32[24,1024]{1,0:T(8,128)}, u32[]{:S(2)}) copy-start(f32[24,1024]{1,0:T(8,128)} %param.8) | copy-start | bytes 294916
  102.2 12.2 %copy-start.27 = (f32[12,24,1024]{2,1,0:T(8,128)S(1)}, f32[12,24,1024]{2,1,0:T(8,128)}, u32[]{:S(2)}) copy-start(f32[12,24,1024]{2,1,0:T(8,128)} %get-tuple-element.169) | copy-start | bytes 3538948
  127.6 13.3 %all-to-all-start.5 = ((f32[64,1,3]{2,1,0:T(1,128)}), f32[64,1,3]{2,1,0:T(1,128)}, u32[]{:S(2)}, u32[]{:S(2)}) async-start(f32[64,1,3]{2,1,0:T(1,128)} %broadcast_in_dim.49), calls=%async_computation.5 | async-start | bytes 65536 | tf_op jit(solution)/shard_map/all_to_all | solution.py:18
  145.5 4.8 %copy-start.7 = (f32[24,1024]{1,0:T(8,128)S(1)}, f32[24,1024]{1,0:T(8,128)}, u32[]{:S(2)}) copy-start(f32[24,1024]{1,0:T(8,128)} %get-tuple-element.101) | copy-start | bytes 294916
  145.5 4.8 %copy-start.10 = (f32[24,1024]{1,0:T(8,128)S(1)}, f32[24,1024]{1,0:T(8,128)}, u32[]{:S(2)}) copy-start(f32[24,1024]{1,0:T(8,128)} %get-tuple-element.102) | copy-start | bytes 294916
  145.5 4.8 %copy-start.13 = (f32[24,1024]{1,0:T(8,128)S(1)}, f32[24,1024]{1,0:T(8,128)}, u32[]{:S(2)}) copy-start(f32[24,1024]{1,0:T(8,128)} %get-tuple-element.103) | copy-start | bytes 294916
  145.5 4.8 %copy-start.16 = (f32[24,1024]{1,0:T(8,128)S(1)}, f32[24,1024]{1,0:T(8,128)}, u32[]{:S(2)}) copy-start(f32[24,1024]{1,0:T(8,128)} %copy-done.14) | copy-start | bytes 294916
  145.5 4.8 %copy-start.19 = (f32[24,1024]{1,0:T(8,128)S(1)}, f32[24,1024]{1,0:T(8,128)}, u32[]{:S(2)}) copy-start(f32[24,1024]{1,0:T(8,128)} %copy-done.17) | copy-start | bytes 294916
  145.6 4.8 %copy-start.22 = (f32[24,1024]{1,0:T(8,128)S(1)}, f32[24,1024]{1,0:T(8,128)}, u32[]{:S(2)}) copy-start(f32[24,1024]{1,0:T(8,128)} %copy-done.20) | copy-start | bytes 294916
  145.6 4.8 %copy-start.25 = (f32[24,1024]{1,0:T(8,128)S(1)}, f32[24,1024]{1,0:T(8,128)}, u32[]{:S(2)}) copy-start(f32[24,1024]{1,0:T(8,128)} %copy-done.23) | copy-start | bytes 294916
  145.6 4.8 %copy-start.40 = (f32[24,1024]{1,0:T(8,128)S(1)}, f32[24,1024]{1,0:T(8,128)}, u32[]{:S(2)}) copy-start(f32[24,1024]{1,0:T(8,128)} %get-tuple-element.104) | copy-start | bytes 294916
  145.6 4.8 %copy-start.43 = (f32[24,1024]{1,0:T(8,128)S(1)}, f32[24,1024]{1,0:T(8,128)}, u32[]{:S(2)}) copy-start(f32[24,1024]{1,0:T(8,128)} %get-tuple-element.105) | copy-start | bytes 294916
  145.6 4.8 %copy-start.46 = (f32[24,1024]{1,0:T(8,128)S(1)}, f32[24,1024]{1,0:T(8,128)}, u32[]{:S(2)}) copy-start(f32[24,1024]{1,0:T(8,128)} %copy-done.44) | copy-start | bytes 294916
  145.6 4.8 %copy-start.49 = (f32[24,1024]{1,0:T(8,128)S(1)}, f32[24,1024]{1,0:T(8,128)}, u32[]{:S(2)}) copy-start(f32[24,1024]{1,0:T(8,128)} %copy-done.47) | copy-start | bytes 294916
  145.6 4.8 %copy-start.52 = (f32[24,1024]{1,0:T(8,128)S(1)}, f32[24,1024]{1,0:T(8,128)}, u32[]{:S(2)}) copy-start(f32[24,1024]{1,0:T(8,128)} %get-tuple-element.108) | copy-start | bytes 294916
  145.6 4.8 %copy-start.55 = (f32[24,1024]{1,0:T(8,128)S(1)}, f32[24,1024]{1,0:T(8,128)}, u32[]{:S(2)}) copy-start(f32[24,1024]{1,0:T(8,128)} %get-tuple-element.109) | copy-start | bytes 294916
  145.6 4.8 %copy-start.76 = (f32[24,1024]{1,0:T(8,128)S(1)}, f32[24,1024]{1,0:T(8,128)}, u32[]{:S(2)}) copy-start(f32[24,1024]{1,0:T(8,128)} %get-tuple-element.106) | copy-start | bytes 294916
  145.6 4.8 %copy-start.79 = (f32[24,1024]{1,0:T(8,128)S(1)}, f32[24,1024]{1,0:T(8,128)}, u32[]{:S(2)}) copy-start(f32[24,1024]{1,0:T(8,128)} %get-tuple-element.107) | copy-start | bytes 294916
  145.7 4.8 %copy-start.85 = (f32[24,1024]{1,0:T(8,128)S(1)}, f32[24,1024]{1,0:T(8,128)}, u32[]{:S(2)}) copy-start(f32[24,1024]{1,0:T(8,128)} %copy-done.83) | copy-start | bytes 294916
  145.7 4.8 %copy-start.88 = (f32[24,1024]{1,0:T(8,128)S(1)}, f32[24,1024]{1,0:T(8,128)}, u32[]{:S(2)}) copy-start(f32[24,1024]{1,0:T(8,128)} %copy-done.86) | copy-start | bytes 294916
  145.7 4.8 %copy-start.106 = (f32[24,1024]{1,0:T(8,128)S(1)}, f32[24,1024]{1,0:T(8,128)}, u32[]{:S(2)}) copy-start(f32[24,1024]{1,0:T(8,128)} %get-tuple-element.76) | copy-start | bytes 294916
  145.7 4.8 %copy-start.108 = (f32[24,1024]{1,0:T(8,128)S(1)}, f32[24,1024]{1,0:T(8,128)}, u32[]{:S(2)}) copy-start(f32[24,1024]{1,0:T(8,128)} %get-tuple-element.77) | copy-start | bytes 294916
  150.5 24.0 %copy-start.3 = (f32[2,12,24,1024]{3,2,1,0:T(8,128)}, f32[2,12,24,1024]{3,2,1,0:T(8,128)S(1)}, u32[]{:S(2)}) copy-start(f32[2,12,24,1024]{3,2,1,0:T(8,128)S(1)} %subtract_divide_fusion) | copy-start | bytes 7077892
  156.3 9.7 %collective-permute-start.4 = (f32[2,12,4,1024]{3,1,2,0:T(8,128)S(1)}, f32[2,12,4,1024]{3,1,2,0:T(8,128)S(1)}, u32[]{:S(2)}, u32[]{:S(2)}) collective-permute-start(f32[2,12,4,1024]{3,1,2,0:T(8,128)S(1)} %copy.160), channel_id=1, source_target_pairs={{1,0},{2,1},{3,2},{4,3},{5,4},{6,5},{7,6},{8,7},{9,8},{10,9},{11,1... | collective-permute-start | bytes 1179656 | tf_op jit(solution)/shard_map/ppermute | solution.py:39
  159.5 14.7 %collective-permute-start.5 = (f32[2,12,4,1024]{3,1,2,0:T(8,128)S(1)}, f32[2,12,4,1024]{3,1,2,0:T(8,128)S(1)}, u32[]{:S(2)}, u32[]{:S(2)}) collective-permute-start(f32[2,12,4,1024]{3,1,2,0:T(8,128)S(1)} %copy.162), channel_id=1, source_target_pairs={{0,1},{1,2},{2,3},{3,4},{4,5},{5,6},{6,7},{7,8},{8,9},{9,10},{10,1... | collective-permute-start | bytes 1179656 | tf_op jit(solution)/shard_map/ppermute | solution.py:36
  161.7 12.8 %copy-start.2 = (f32[2,12,24,1024]{3,2,1,0:T(8,128)S(1)}, f32[2,12,24,1024]{3,2,1,0:T(8,128)}, u32[]{:S(2)}) copy-start(f32[2,12,24,1024]{3,2,1,0:T(8,128)} %copy-done.1) | copy-start | bytes 7077892
  161.8 12.7 %copy-start.32 = (f32[12,24,1024]{2,1,0:T(8,128)S(1)}, f32[12,24,1024]{2,1,0:T(8,128)}, u32[]{:S(2)}) copy-start(f32[12,24,1024]{2,1,0:T(8,128)} %get-tuple-element.174) | copy-start | bytes 3538948
  161.8 12.7 %copy-start.36 = (f32[12,24,1024]{2,1,0:T(8,128)S(1)}, f32[12,24,1024]{2,1,0:T(8,128)}, u32[]{:S(2)}) copy-start(f32[12,24,1024]{2,1,0:T(8,128)} %get-tuple-element.175) | copy-start | bytes 3538948
  161.8 12.7 %copy-start.97 = (f32[24,1024]{1,0:T(8,128)S(1)}, f32[24,1024]{1,0:T(8,128)}, u32[]{:S(2)}) copy-start(f32[24,1024]{1,0:T(8,128)} %param.10) | copy-start | bytes 294916
  161.8 12.7 %copy-start.102 = (f32[24,1024]{1,0:T(8,128)S(1)}, f32[24,1024]{1,0:T(8,128)}, u32[]{:S(2)}) copy-start(f32[24,1024]{1,0:T(8,128)} %param.8) | copy-start | bytes 294916
  162.4 12.1 %copy-start.28 = (f32[12,24,1024]{2,1,0:T(8,128)S(1)}, f32[12,24,1024]{2,1,0:T(8,128)}, u32[]{:S(2)}) copy-start(f32[12,24,1024]{2,1,0:T(8,128)} %get-tuple-element.169) | copy-start | bytes 3538948
  187.6 13.3 %all-to-all-start.7 = ((f32[64,1,4]{2,1,0:T(1,128)}), f32[64,1,4]{2,1,0:T(1,128)S(1)}, u32[]{:S(2)}, u32[]{:S(2)}) async-start(f32[64,1,4]{2,1,0:T(1,128)} %broadcast_in_dim.96), calls=%async_computation.7 | async-start | bytes 65536 | tf_op jit(solution)/shard_map/all_to_all | solution.py:18
  214.7 18.7 %copy-start.4 = (f32[2,12,24,1024]{3,2,1,0:T(8,128)}, f32[2,12,24,1024]{3,2,1,0:T(8,128)S(1)}, u32[]{:S(2)}) copy-start(f32[2,12,24,1024]{3,2,1,0:T(8,128)S(1)} %multiply_add_fusion) | copy-start | bytes 7077892
  215.1 9.7 %collective-permute-start.6 = (f32[2,12,4,1024]{3,1,2,0:T(8,128)S(1)}, f32[2,12,4,1024]{3,1,2,0:T(8,128)S(1)}, u32[]{:S(2)}, u32[]{:S(2)}) collective-permute-start(f32[2,12,4,1024]{3,1,2,0:T(8,128)S(1)} %copy.166), channel_id=1, source_target_pairs={{1,0},{2,1},{3,2},{4,3},{5,4},{6,5},{7,6},{8,7},{9,8},{10,9},{11,1... | collective-permute-start | bytes 1179656 | tf_op jit(solution)/shard_map/ppermute | solution.py:39
  218.3 14.7 %collective-permute-start.7 = (f32[2,12,4,1024]{3,1,2,0:T(8,128)S(1)}, f32[2,12,4,1024]{3,1,2,0:T(8,128)S(1)}, u32[]{:S(2)}, u32[]{:S(2)}) collective-permute-start(f32[2,12,4,1024]{3,1,2,0:T(8,128)S(1)} %copy.168), channel_id=1, source_target_pairs={{0,1},{1,2},{2,3},{3,4},{4,5},{5,6},{6,7},{7,8},{8,9},{9,10},{10,1... | collective-permute-start | bytes 1179656 | tf_op jit(solution)/shard_map/ppermute | solution.py:36
  220.8 12.5 %copy-start.33 = (f32[12,24,1024]{2,1,0:T(8,128)S(1)}, f32[12,24,1024]{2,1,0:T(8,128)}, u32[]{:S(2)}) copy-start(f32[12,24,1024]{2,1,0:T(8,128)} %get-tuple-element.174) | copy-start | bytes 3538948
  220.8 12.5 %copy-start.37 = (f32[12,24,1024]{2,1,0:T(8,128)S(1)}, f32[12,24,1024]{2,1,0:T(8,128)}, u32[]{:S(2)}) copy-start(f32[12,24,1024]{2,1,0:T(8,128)} %get-tuple-element.175) | copy-start | bytes 3538948
  220.9 12.5 %copy-start.93 = (pred[24,1024]{1,0:T(8,128)(4,1)S(1)}, pred[24,1024]{1,0:T(8,128)(4,1)}, u32[]{:S(2)}) copy-start(pred[24,1024]{1,0:T(8,128)(4,1)} %copy-done.89) | copy-start | bytes 73732
  220.9 12.5 %copy-start.98 = (f32[24,1024]{1,0:T(8,128)S(1)}, f32[24,1024]{1,0:T(8,128)}, u32[]{:S(2)}) copy-start(f32[24,1024]{1,0:T(8,128)} %param.10) | copy-start | bytes 294916
  220.9 12.5 %copy-start.103 = (f32[24,1024]{1,0:T(8,128)S(1)}, f32[24,1024]{1,0:T(8,128)}, u32[]{:S(2)}) copy-start(f32[24,1024]{1,0:T(8,128)} %param.8) | copy-start | bytes 294916
  221.5 11.9 %copy-start.29 = (f32[12,24,1024]{2,1,0:T(8,128)S(1)}, f32[12,24,1024]{2,1,0:T(8,128)}, u32[]{:S(2)}) copy-start(f32[12,24,1024]{2,1,0:T(8,128)} %get-tuple-element.169) | copy-start | bytes 3538948
  (61 other events, 119.9 us)
where the time goes:
time: 241 us; the launch traced here: 239 us
  other arithmetic  67.3 us (28%)
  waiting for transfers between devices  63.8 us (26%)
  starting transfers between devices  41.2 us (17%)
  blocking collectives  27.7 us (11%)
  local copies, waits for them, and re-layouts  19.7 us (8%)
  between operations  19.7 us (8%)
    ppermute x4, waiting for transfers between devices, extended(): lax.ppermute(lax.slice_in_dim(block, block.shape[dim] - width, None, axis...  32.1 us
    all_to_all x5, blocking collectives, sent_to_all(): return lax.all_to_all(copies, axis, split_axis=0, concat_axis=0, tiled=True)  27.7 us
    all_to_all x3, starting transfers between devices, sent_to_all(): return lax.all_to_all(copies, axis, split_axis=0, concat_axis=0, tiled=True)  21.5 us
    reduce_sum x3, other arithmetic, body(): local_terms = [jnp.sum(centre_image * vector) for vector in aligned]  20.1 us
    all_to_all x3, waiting for transfers between devices, sent_to_all(): return lax.all_to_all(copies, axis, split_axis=0, concat_axis=0, tiled=True)  17.8 us
    ppermute x4, waiting for transfers between devices, extended(): lax.ppermute(lax.slice_in_dim(block, 0, width, axis=dim), axis, backward)  13.9 us
    ppermute x4, starting transfers between devices, extended(): lax.ppermute(lax.slice_in_dim(block, 0, width, axis=dim), axis, backward)  11.8 us
    ppermute x4, starting transfers between devices, extended(): lax.ppermute(lax.slice_in_dim(block, block.shape[dim] - width, None, axis...  7.94 us
  transfers between devices with their start and end apart: 11, of which 11 were waited for; matrix products, arithmetic and copies ran while one was open for 4% of the time, Pallas kernels for 0%

commit v1 on v0

v1 whole, which is shorter than its diff:
```python
import jax
import jax.numpy as jnp
from jax import lax
from jax.experimental import pallas as pl
from jax.experimental.pallas import tpu as pltpu
from jax.sharding import Mesh
from jax.sharding import PartitionSpec as P


FLOW = ("flow_0", "flow_1", "flow_2", "flow_3")
CORE = "flow_3"
epsilon = 1e-06
relaxation = 0.5
reach_weights = (1.0, 0.6, 0.35, 0.2)
horiz_total = 2.0 * sum(reach_weights) + 2.0

L = 12
ROWS = 24
REACH = 4
EDGE = 2 * REACH
INNER = ROWS - EDGE
F32 = jnp.float32
TILE = (8, 128)

VM = pl.BlockSpec(memory_space=pltpu.VMEM)
HB = pl.BlockSpec(memory_space=pltpu.HBM)


def vmem(*lead):
    return pltpu.VMEM((*lead, *TILE), F32)


def edge_order(index):
    return index if index < REACH else ROWS - 1 - (index - REACH)


def place_of(core, t):
    tile, sub = t // 8, t % 8
    return (
        jnp.where(core == 1, tile, 2 - tile),
        jnp.where(core == 1, sub, 7 - sub),
    )


def row(ref, plane, place):
    tile, sub = place
    return ref[plane, tile, pl.ds(sub, 8, stride=8), :]


def rows(ref, plane, places):
    return jnp.stack([row(ref, plane, place) for place in places])


def factor(places, raws, inv_real, inv_imag, link_out, nu_out, start):
    vraw, nuraw, fricraw, rotraw, iceraw, groundraw = raws
    span = pl.ds(start, len(places))
    active = rows(iceraw, 0, places) > 0
    nu = rows(nuraw, 0, places)
    drag = jnp.where(rows(groundraw, 0, places) > 0, rows(fricraw, 0, places), 0.0)
    imag = jnp.where(active, rows(rotraw, 0, places), 0.0)
    base = (relaxation + horiz_total) * nu
    nu_out[span] = jnp.where(active, nu, 0.0)
    below = None
    for k in range(L):
        real = base
        if k == 0:
            real = real + drag
        else:
            real = real + below
        if k < L - 1:
            above = rows(vraw, k, places)
            real = real + above
        real = jnp.where(active, real, 1.0)
        pivot_imag = imag
        if k > 0:
            link = jnp.where(active, below, 0.0)
            link_out[k - 1, span] = link
            square = link * link
            real = real - square * er
            pivot_imag = imag - square * ei
        inverse = 1.0 / (real * real + pivot_imag * pivot_imag)
        er = real * inverse
        ei = -(pivot_imag * inverse)
        inv_real[k, span] = er
        inv_imag[k, span] = ei
        if k < L - 1:
            below = above


def solve(source, inv_real, inv_imag, link, span, put, get):
    cf = cg = None
    for k in range(L):
        sf, sg = source(k), source(L + k)
        if k > 0:
            ln = link[k - 1, span]
            sf = sf + ln * cf
            sg = sg + ln * cg
        er, ei = inv_real[k, span], inv_imag[k, span]
        cf, cg = er * sf + ei * sg, er * sg - ei * sf
        put(k, cf)
        put(L + k, cg)
    xf, xg = cf, cg
    for k in range(L - 2, -1, -1):
        ln = link[k, span]
        pf, pg = ln * xf, ln * xg
        er, ei = inv_real[k, span], inv_imag[k, span]
        xf = get(k) + (er * pf + ei * pg)
        xg = get(L + k) + (er * pg - ei * pf)
        put(k, xf)
        put(L + k, xg)


def edge_put(sa, sb):
    def put(plane, value):
        sa[plane] = value[:REACH]
        sb[plane] = value[REACH:]

    def get(plane):
        return jnp.concatenate([sa[plane], sb[plane]], 0)

    return put, get


def lanes():
    return lax.broadcasted_iota(jnp.int32, TILE, 1)


def cross(s, masks):
    first, last, first_end, last_end = masks
    up = jnp.where(first, pltpu.roll(s, 7, 0), s)
    up = jnp.where(first_end, 0.0, up)
    down = jnp.where(last, pltpu.roll(s, 1, 0), s)
    down = jnp.where(last_end, 0.0, down)
    return pltpu.roll(up, 127, 1) + pltpu.roll(down, 1, 1)


def cross_masks():
    lane = lanes()
    sub = lax.broadcasted_iota(jnp.int32, TILE, 0)
    first, last = lane == 0, lane == 127
    return first, last, first & (sub == 7), last & (sub == 0)


def apply_stencil(sa, sb, si, nu_i, u_edges, u_inners, u_new, nsum, extra=None):
    masks = cross_masks()
    count = len(u_inners)
    pairs = count + 1
    zero = jnp.zeros(TILE, F32)

    def step(plane, sums):
        sums = list(sums)
        s = (
            [sa[plane, d] for d in range(REACH)]
            + [si[plane, d] for d in range(INNER)]
            + [sb[plane, REACH - 1 - d] for d in range(REACH)]
        )
        for t in range(ROWS):
            total = cross(s[t], masks)
            for m in range(1, REACH + 1):
                weight = reach_weights[m - 1]
                near = [s[q] for q in (t - m, t + m) if 0 <= q < ROWS]
                both = near[0] + near[1] if len(near) == 2 else near[0]
                total = total + (both if weight == 1.0 else weight * both)
            if REACH <= t < ROWS - REACH:
                i = t - REACH
                new = nu_i[i] * total
                u_new[plane, i] = new
                for a in range(count):
                    sums[a] = sums[a] + new * u_inners[a][plane, i]
                sums[count] = sums[count] + new * new
            else:
                nsum[plane, t if t < REACH else REACH + ROWS - 1 - t] = total
        for e in range(EDGE):
            now = u_edges[-1][plane, e]
            for a in range(count):
                other = now if a == count - 1 else u_edges[a][plane, e]
                sums[pairs + a] = sums[pairs + a] + now * other
        if extra is not None:
            for i in range(INNER):
                now = u_inners[0][plane, i]
                sums[pairs + count] = sums[pairs + count] + now * now
        return tuple(sums)

    size = pairs + count + (extra is not None)
    return lax.fori_loop(0, 2 * L, step, (zero,) * size)


def first_edge_kernel(f, v, nu, fric, rot, ice, ground, *rest):
    (inv_real, inv_imag, link, nu_e, sa, sb) = rest[:6]
    raws = rest[6:13]
    sems = rest[13]
    fraw, vraw = raws[0], raws[1]
    small = [
        pltpu.make_async_copy(src, dst, sems.at[i])
        for i, (src, dst) in enumerate(zip((nu, fric, rot, ice, ground), raws[2:]))
    ]
    v_edge = [pltpu.make_async_copy(v.at[:, i], vraw.at[:, i], sems.at[5 + i]) for i in (0, 2)]
    f_edge = [pltpu.make_async_copy(f.at[:, i], fraw.at[:, i], sems.at[8 + i]) for i in (0, 2)]
    middle = [
        pltpu.make_async_copy(v.at[:, 1], vraw.at[:, 1], sems.at[6]),
        pltpu.make_async_copy(f.at[:, 1], fraw.at[:, 1], sems.at[9]),
    ]
    for copy in small + v_edge + f_edge + middle:
        copy.start()
    core = lax.axis_index(CORE)
    places = [place_of(core, edge_order(e)) for e in range(EDGE)]
    for copy in small + v_edge:
        copy.wait()
    factor(places, raws[1:], inv_real, inv_imag, link, nu_e, 0)
    for copy in f_edge:
        copy.wait()
    put, get = edge_put(sa, sb)
    span = pl.ds(0, EDGE)
    solve(lambda plane: rows(fraw, plane, places), inv_real, inv_imag, link, span, put, get)
    for copy in middle:
        copy.wait()


def first_inner_kernel(fraw, vraw, nuraw, fricraw, rotraw, iceraw, groundraw, sa, sb, *rest):
    (inv_real, inv_imag, link, nu_i, si, f_e, f_i, u_new, nsum, sums_out) = rest
    raws = (vraw, nuraw, fricraw, rotraw, iceraw, groundraw)
    core = lax.axis_index(CORE)
    edge_places = [place_of(core, edge_order(e)) for e in range(EDGE)]
    places = [place_of(core, REACH + i) for i in range(INNER)]

    def spread(plane, carry):
        for e in range(EDGE):
            f_e[plane, e] = row(fraw, plane, edge_places[e])
        for i in range(INNER):
            f_i[plane, i] = row(fraw, plane, places[i])
        return carry

    lax.fori_loop(0, 2 * L, spread, 0)
    for start in (0, 8):
        factor(places[start : start + 8], raws, inv_real, inv_imag, link, nu_i, start)
    inner_solve(f_i, inv_real, inv_imag, link, si)
    sums = apply_stencil(sa, sb, si, nu_i, [f_e], [f_i], u_new, nsum, extra=True)
    for a, value in enumerate(sums):
        sums_out[a] = value


def inner_solve(u_i, inv_real, inv_imag, link, si):
    def batch(b, carry):
        span = pl.ds(b * 8, 8)

        def put(plane, value):
            si[plane, span] = value

        solve(
            lambda plane: u_i[plane, span],
            inv_real,
            inv_imag,
            link,
            span,
            put,
            lambda plane: si[plane, span],
        )
        return carry

    lax.fori_loop(0, INNER // 8, batch, 0)


def edge_source(halo, nsum, nu_e):
    def of_side(plane, side):
        parts = []
        for d in range(REACH):
            total = nsum[plane, side * REACH + d]
            for q in range(1, REACH + 1 - d):
                weight = reach_weights[d + q - 1]
                value = halo[side][plane, q - 1]
                total = total + (value if weight == 1.0 else weight * value)
            parts.append(nu_e[side * REACH + d] * total)
        return parts

    return lambda plane: jnp.stack(of_side(plane, 0) + of_side(plane, 1))


def edge_kernel(ha, hb, nsum, nu_e, inv_real, inv_imag, link, u_e, sa, sb):
    finish = edge_source((ha, hb), nsum, nu_e)

    def source(plane):
        value = finish(plane)
        u_e[plane] = value
        return value

    put, get = edge_put(sa, sb)
    solve(source, inv_real, inv_imag, link, pl.ds(0, EDGE), put, get)


def inner_kernel(order, *refs):
    sa, sb, inv_real, inv_imag, link, nu_i = refs[:6]
    u_edges = refs[6 : 7 + order]
    u_inners = refs[7 + order : 8 + 2 * order]
    si, u_new, nsum, sums_out = refs[8 + 2 * order :]
    inner_solve(u_inners[-1], inv_real, inv_imag, link, si)
    sums = apply_stencil(sa, sb, si, nu_i, u_edges, u_inners, u_new, nsum)
    for a, value in enumerate(sums):
        sums_out[a] = value


GRAM = [(a, b) for b in range(4) for a in range(b + 1)]


def last_edge_kernel(ha, hb, nsum, nu_e, u0, u1, u2, s0, s1, s2, u_e, payload):
    finish = edge_source((ha, hb), nsum, nu_e)
    zero = jnp.zeros(TILE, F32)

    def step(plane, sums):
        sums = list(sums)
        value = finish(plane)
        u_e[plane] = value
        for a, ref in enumerate((u0, u1, u2)):
            other = ref[plane]
            for e in range(EDGE):
                sums[a] = sums[a] + value[e] * other[e]
        for e in range(EDGE):
            sums[3] = sums[3] + value[e] * value[e]
        return tuple(sums)

    last = lax.fori_loop(0, 2 * L, step, (zero,) * 4)
    gram = {
        (0, 0): s0[2] + s0[3],
        (0, 1): s0[0] + s1[3],
        (1, 1): s0[1] + s1[4],
        (0, 2): s1[0] + s2[4],
        (1, 2): s1[1] + s2[5],
        (2, 2): s1[2] + s2[6],
        (0, 3): s2[0] + last[0],
        (1, 3): s2[1] + last[1],
        (2, 3): s2[2] + last[2],
        (3, 3): s2[3] + last[3],
    }
    lane = lanes()
    out = zero
    for i, pair in enumerate(GRAM):
        value = jnp.sum(jnp.sum(gram[pair], axis=0, keepdims=True), axis=1, keepdims=True)
        out = out + jnp.where(lane == i, value, 0.0)
    for r in range(payload.shape[0] // 8):
        payload[pl.ds(8 * r, 8), :] = out


def least_squares(columns, start):
    count_cols = len(columns)
    givens_rhs = [start] + [start * 0.0 for index in range(count_cols)]
    cosines, sines, upper_cols = ([], [], [])
    for column_index, column_in in enumerate(columns):
        column = list(column_in)
        for row_index in range(column_index):
            rotated_a = (
                cosines[row_index] * column[row_index] + sines[row_index] * column[row_index + 1]
            )
            rotated_b = (
                -sines[row_index] * column[row_index] + cosines[row_index] * column[row_index + 1]
            )
            column[row_index] = rotated_a
            column[row_index + 1] = rotated_b
        radius = jnp.sqrt(
            column[column_index] * column[column_index]
            + column[column_index + 1] * column[column_index + 1]
        )
        inverse = 1.0 / radius
        cosine = column[column_index] * inverse
        sine_value = column[column_index + 1] * inverse
        column[column_index] = inverse
        cosines.append(cosine)
        sines.append(sine_value)
        upper_cols.append(column)
        next_rhs = -sine_value * givens_rhs[column_index]
        givens_rhs[column_index] = cosine * givens_rhs[column_index]
        givens_rhs[column_index + 1] = next_rhs
    factors = [None] * count_cols
    for column_index in range(count_cols - 1, -1, -1):
        accum = givens_rhs[column_index]
        for later in range(column_index + 1, count_cols):
            accum = accum - upper_cols[later][column_index] * factors[later]
        factors[column_index] = accum * upper_cols[column_index][column_index]
    return factors


def dot(left, right):
    total = left[0] * right[0]
    for a, b in zip(left[1:], right[1:]):
        total = total + a * b
    return total


def coefficients(gram):
    size = 4
    upper = {}
    for a in range(size):
        square = gram[(a, a)]
        for p in range(a):
            square = square - upper[(p, a)] * upper[(p, a)]
        square = jnp.maximum(square, 0.0)
        length = jnp.sqrt(square)
        inverse = jnp.where(length > 0.0, 1.0 / jnp.where(length > 0.0, length, 1.0), 0.0)
        upper[(a, a)] = length
        for b in range(a + 1, size):
            value = gram[(a, b)]
            for p in range(a):
                value = value - upper[(p, a)] * upper[(p, b)]
            upper[(a, b)] = value * inverse
    beta = jnp.sqrt(gram[(0, 0)] + epsilon)
    inverse = 1.0 / beta
    basis = [[inverse]]
    ortho = [[upper[(0, 0)] * inverse]]
    columns = []
    for j in range(3):
        current = basis[j]
        w = [current[0]]
        for i in range(1, j + 1):
            w.append(current[i] - current[i - 1])
        w.append(-current[j])
        q = [dot([upper[(i, m)] for m in range(i, j + 2)], w[i:]) for i in range(j + 2)]
        column = []
        for i in range(j + 1):
            h = dot(q[: i + 1], ortho[i])
            for m in range(i + 1):
                q[m] = q[m] - h * ortho[i][m]
                w[m] = w[m] - h * basis[i][m]
            column.append(h)
        length = jnp.sqrt(dot(q, q) + epsilon)
        column.append(length)
        columns.append(column)
        if j < 2:
            inverse = 1.0 / length
            basis.append([value * inverse for value in w])
            ortho.append([value * inverse for value in q])
    y = least_squares(columns, beta)
    return [dot(y[i:], [basis[j][i] for j in range(i, 3)]) for i in range(3)]


def final_kernel(gathered, *refs):
    u_edges, u_inners = refs[0:4], refs[4:8]
    sas, sbs, sis = refs[8:11], refs[11:14], refs[14:17]
    out_s, out_r, buf_s, buf_r, sem_s, sem_r = refs[17:]
    total = gathered[pl.ds(0, 8), :]
    for r in range(1, gathered.shape[0] // 8):
        total = total + gathered[pl.ds(8 * r, 8), :]
    total = jnp.sum(total, axis=0, keepdims=True)
    total = jnp.broadcast_to(total, TILE)
    lane = lanes()
    gram = {}
    for i, pair in enumerate(GRAM):
        value = jnp.sum(jnp.where(lane == i, total, 0.0), axis=1, keepdims=True)
        gram[pair] = jnp.broadcast_to(value, TILE)
    c0, c1, c2 = coefficients(gram)
    e0, e1, e2 = 1.0 - c0, c0 - c1, c1 - c2
    core = lax.axis_index(CORE)
    places = [place_of(core, t) for t in range(ROWS)]

    def copies(plane):
        return (
            pltpu.make_async_copy(buf_s.at[plane], out_s.at[plane], sem_s),
            pltpu.make_async_copy(buf_r.at[plane], out_r.at[plane], sem_r),
        )

    def step(plane, carry):
        for t in range(ROWS):
            if t < REACH:
                s = [ref[plane, t] for ref in sas]
                u = [ref[plane, t] for ref in u_edges]
            elif t < ROWS - REACH:
                s = [ref[plane, t - REACH] for ref in sis]
                u = [ref[plane, t - REACH] for ref in u_inners]
            else:
                s = [ref[plane, ROWS - 1 - t] for ref in sbs]
                u = [ref[plane, REACH + ROWS - 1 - t] for ref in u_edges]
            tile, sub = places[t]
            buf_s[plane, tile, pl.ds(sub, 8, stride=8), :] = c0 * s[0] + c1 * s[1] + c2 * s[2]
            buf_r[plane, tile, pl.ds(sub, 8, stride=8), :] = (
                e0 * u[0] + e1 * u[1] + (e2 * u[2] + c2 * u[3])
            )
        for copy in copies(plane):
            copy.start()
        return carry

    lax.fori_loop(0, 2 * L, step, 0)
    pltpu.make_async_copy(buf_s, out_s, sem_s).wait()
    pltpu.make_async_copy(buf_r, out_r, sem_r).wait()


def tiled(x):
    x = x.reshape(-1, ROWS // 8, 8, 8, 128)
    return x.transpose(0, 1, 3, 2, 4).reshape(-1, ROWS // 8, 64, 128)


def untiled(x):
    x = x.reshape(2 * L, ROWS // 8, 8, 8, 128).transpose(0, 1, 3, 2, 4)
    return x.reshape(2, L, ROWS, 1024)


def call(kernel, name, out_shape, args, in_specs=None, out_specs=None, scratch=(), limit=None):
    return pl.pallas_call(
        kernel,
        out_shape=out_shape,
        in_specs=in_specs or [VM] * len(args),
        out_specs=out_specs or [VM] * len(out_shape),
        scratch_shapes=scratch,
        compiler_params=pltpu.CompilerParams(vmem_limit_bytes=limit or (4 << 20)),
        name=name,
    )(*args)


def exchange(sa, sb):
    count = 128
    across = [(i, i + 1) for i in range(1, count - 1, 2)]
    across = across + [(b, a) for a, b in across]
    within = [(i, i ^ 1) for i in range(count)]
    hb = lax.ppermute(sb, FLOW, across)
    ha = lax.ppermute(sa, FLOW, within)
    return ha, hb


def body(forcing, viscosity, friction, rotation, vertical, ice_mask, grounded):
    raw = [tiled(x) for x in (forcing, vertical, viscosity, friction, rotation, ice_mask, grounded)]
    raw = [pltpu.with_memory_space_constraint(x, pltpu.HBM) for x in raw]
    planes = 2 * L

    def rawtype(x):
        return pltpu.VMEM(x.shape, x.dtype)

    out = call(
        first_edge_kernel,
        "edge0",
        [vmem(L, EDGE), vmem(L, EDGE), vmem(L - 1, EDGE), vmem(EDGE)]
        + [vmem(planes, REACH)] * 2
        + [rawtype(x) for x in raw],
        raw,
        in_specs=[HB] * 7,
        scratch=[pltpu.SemaphoreType.DMA((11,))],
    )
    ier, iei, ie_link, nu_e, sa, sb = out[:6]
    sas, sbs, sis = [sa], [sb], []
    inner_vec = vmem(planes, INNER)
    edge_vec = vmem(planes, EDGE)
    halo = exchange(sa, sb)
    ir, ii, i_link, nu_i, si, f_e, f_i, u_i, nsum, sums = call(
        first_inner_kernel,
        "inner0",
        [vmem(L, INNER), vmem(L, INNER), vmem(L - 1, INNER), vmem(INNER)]
        + [inner_vec, edge_vec, inner_vec, inner_vec, edge_vec, vmem(4)],
        list(out[6:]) + [sa, sb],
    )
    sis.append(si)
    u_edges, u_inners, all_sums = [f_e], [f_i, u_i], [sums]
    for order in (1, 2):
        u_e, sa, sb = call(
            edge_kernel,
            f"edge{order}",
            [edge_vec] + [vmem(planes, REACH)] * 2,
            [*halo, nsum, nu_e, ier, iei, ie_link],
        )
        u_edges.append(u_e)
        sas.append(sa)
        sbs.append(sb)
        halo = exchange(sa, sb)

        def kernel(*refs, order=order):
            inner_kernel(order, *refs)

        si, u_i, nsum, sums = call(
            kernel,
            f"inner{order}",
            [inner_vec, inner_vec, edge_vec, vmem(2 * order + 3)],
            [sa, sb, ir, ii, i_link, nu_i, *u_edges, *u_inners],
        )
        sis.append(si)
        u_inners.append(u_i)
        all_sums.append(sums)
    u_e, payload = call(
        last_edge_kernel,
        "edge3",
        [edge_vec, jax.ShapeDtypeStruct((128, 128), F32)],
        [*halo, nsum, nu_e, *u_edges, *all_sums],
    )
    u_edges.append(u_e)
    gathered = lax.all_to_all(payload, FLOW, split_axis=0, concat_axis=0, tiled=True)
    shape = (planes, ROWS // 8, 64, 128)
    outs = call(
        final_kernel,
        "combine",
        [jax.ShapeDtypeStruct(shape, F32)] * 2,
        [gathered, *u_edges, *u_inners, *sas, *sbs, *sis],
        out_specs=[HB] * 2,
        scratch=[pltpu.VMEM(shape, F32)] * 2 + [pltpu.SemaphoreType.DMA] * 2,
        limit=8 << 20,
    )
    return untiled(outs[0]), untiled(outs[1])


def solution(mesh):
    finer = Mesh(mesh.devices.reshape(4, 4, 4, 2), FLOW)
    return jax.shard_map(
        body,
        mesh=finer,
        in_specs=(
            P(None, None, FLOW, None),
            P(FLOW, None),
            P(FLOW, None),
            P(FLOW, None),
            P(None, FLOW, None),
            P(FLOW, None),
            P(FLOW, None),
        ),
        out_specs=(P(None, None, FLOW, None), P(None, None, FLOW, None)),
        check_vma=False,
    )
```

time: 241 us -> 68.1 us (0.28)
  the two profiles are of different devices: /device:TPU:8 before, /device:TPU:1 now
where the time goes in v1:
time: 68.1 us; the launch traced here: 68 us
  blocking collectives  31.9 us (47%)
  Pallas kernels  18.6 us (27%)
  starting transfers between devices  12.1 us (18%)
  waiting for transfers between devices  4.67 us (7%)
  between operations  0.74 us (1%)
    all_to_all x1, blocking collectives, body(): lax.all_to_all(payload, FLOW, split_axis=0, concat_axis=0, tiled=True)  31.9 us
    pallas_call x8, Pallas kernels, call(): pl.pallas_call(kernel, out_shape=out_shape, in_specs=in_specs or [VM] * l...  18.6 us
    ppermute x3, starting transfers between devices, exchange(): hb = lax.ppermute(sb, FLOW, across)  10.4 us
    ppermute x3, waiting for transfers between devices, exchange(): hb = lax.ppermute(sb, FLOW, across)  4.66 us
    ppermute x3, starting transfers between devices, exchange(): ha = lax.ppermute(sa, FLOW, within)  1.63 us
  transfers between devices with their start and end apart: 6, of which 3 were waited for; matrix products, arithmetic and copies ran while one was open for 0% of the time, Pallas kernels for 18%

profile of v1, /device:TPU:1, one launch (start us, length us, event | category | flops | bytes accessed | tf_op | source)
XLA Modules:
  0.0 68.0 jit_solution(5406243992338618381)
XLA Ops:
  0.6 2.3 %edge0.1 = (f32[12,8,8,128]{3,2,1,0:T(8,128)S(1)}, f32[12,8,8,128]{3,2,1,0:T(8,128)S(1)}, f32[11,8,8,128]{3,2,1,0:T(8,128)S(1)}, f32[8,8,128]{2,1,0:T(8,128)S(1)...) custom-call(f32[24,3,64,128]{3,2,1,0:T(8,128)} %bitcast.51, ...), custom_call_target="tpu_custom_call" | custom-call | tf_op jit(solution)/shard_map/edge0/pallas_call | solution.py:494
  3.0 1.5 %collective-permute-start = (f32[24,4,8,128]{3,2,1,0:T(8,128)S(1)}, f32[24,4,8,128]{3,2,1,0:T(8,128)S(1)}, u32[]{:S(2)}, u32[]{:S(2)}) collective-permute-start(f32[24,4,8,128]{3,2,1,0:T(8,128)S(1)} %get-tuple-element.43.sa.refs_8_), channel_id=1, source_target_pairs={{0,1},{1,0},{2,3},{3,2},{4,5},{5,4},{6,7},{7,6},{8,9},{9,8},{10,11... | collective-permute-start | bytes 1179656 | tf_op jit(solution)/shard_map/ppermute | solution.py:511
  4.4 3.1 %collective-permute-start.1 = (f32[24,4,8,128]{3,2,1,0:T(8,128)S(1)}, f32[24,4,8,128]{3,2,1,0:T(8,128)S(1)}, u32[]{:S(2)}, u32[]{:S(2)}) collective-permute-start(f32[24,4,8,128]{3,2,1,0:T(8,128)S(1)} %get-tuple-element.44.sb.refs_11_), channel_id=1, source_target_pairs={{1,2},{3,4},{5,6},{7,8},{9,10},{11,12},{13,14},{15,16},{17,18},{19... | collective-permute-start | bytes 1179656 | tf_op jit(solution)/shard_map/ppermute | solution.py:510
  7.6 4.9 %inner0.1 = (f32[12,16,8,128]{3,2,1,0:T(8,128)S(1)}, f32[12,16,8,128]{3,2,1,0:T(8,128)S(1)}, f32[11,16,8,128]{3,2,1,0:T(8,128)S(1)}, f32[16,8,128]{2,1,0:T(8,128...) custom-call(f32[24,3,64,128]{3,2,1,0:T(8,128)S(1)} %get-tuple-elemen, ...), custom_call_target="tpu_custom_call" | custom-call | tf_op jit(solution)/shard_map/inner0/pallas_call | solution.py:494
  12.5 0.0 collective-permute-done.ha
  12.5 1.0 %collective-permute-done.1.hb = f32[24,4,8,128]{3,2,1,0:T(8,128)S(1)} collective-permute-done((f32[24,4,8,128]{3,2,1,0:T(8,128)S(1)}, f32[24,4,8,128]{3,2,1,0:T(8,128)S(1)}, u32[]{:S(2)}, u32[]{:S(2)}) %collective-permute-start.1) | collective-permute-done | bytes 393248 | tf_op jit(solution)/shard_map/ppermute | solution.py:510
  13.5 0.4 edge1.1
  13.9 0.1 collective-permute-start.2
  14.0 3.6 %collective-permute-start.3 = (f32[24,4,8,128]{3,2,1,0:T(8,128)S(1)}, f32[24,4,8,128]{3,2,1,0:T(8,128)S(1)}, u32[]{:S(2)}, u32[]{:S(2)}) collective-permute-start(f32[24,4,8,128]{3,2,1,0:T(8,128)S(1)} %get-tuple-element.58.refs_1_.refs_12_), channel_id=1, source_target_pairs={{1,2},{3,4},{5,6},{7,8},{9,10},{11,12},{13,14},{15,16},{17,18},{19... | collective-permute-start | bytes 1179656 | tf_op jit(solution)/shard_map/ppermute | solution.py:510
  17.6 3.6 %inner1.1 = (f32[24,16,8,128]{3,2,1,0:T(8,128)S(1)}, f32[24,16,8,128]{3,2,1,0:T(8,128)S(1)}, f32[24,8,8,128]{3,2,1,0:T(8,128)S(1)}, f32[5,8,128]{2,1,0:T(8,128)S(1)}) custom-call(f32[24,4,8,128]{3,2,1,0:T(8,128)S(1)} %get-tuple-element.57.refs_0_.refs_9_, f32[24,4,8,128]{3,2,1,0:T(8,128)S(1)} %get-tuple-element.58.refs_1_.refs_12_, ...), custom_call_target="tpu_custom_call" | custom-call | tf_op jit(solution)/shard_map/inner1/pallas_call | solution.py:494
  21.2 0.0 collective-permute-done.2.ha
  21.2 1.9 %collective-permute-done.3.hb = f32[24,4,8,128]{3,2,1,0:T(8,128)S(1)} collective-permute-done((f32[24,4,8,128]{3,2,1,0:T(8,128)S(1)}, f32[24,4,8,128]{3,2,1,0:T(8,128)S(1)}, u32[]{:S(2)}, u32[]{:S(2)}) %collective-permute-start.3) | collective-permute-done | bytes 393248 | tf_op jit(solution)/shard_map/ppermute | solution.py:510
  23.1 0.4 edge2.1
  23.5 0.1 collective-permute-start.4
  23.6 3.7 %collective-permute-start.5 = (f32[24,4,8,128]{3,2,1,0:T(8,128)S(1)}, f32[24,4,8,128]{3,2,1,0:T(8,128)S(1)}, u32[]{:S(2)}, u32[]{:S(2)}) collective-permute-start(f32[24,4,8,128]{3,2,1,0:T(8,128)S(1)} %get-tuple-element.69.refs_1_.refs_13_), channel_id=1, source_target_pairs={{1,2},{3,4},{5,6},{7,8},{9,10},{11,12},{13,14},{15,16},{17,18},{19... | collective-permute-start | bytes 1179656 | tf_op jit(solution)/shard_map/ppermute | solution.py:510
  27.3 3.7 %inner2.1 = (f32[24,16,8,128]{3,2,1,0:T(8,128)S(1)}, f32[24,16,8,128]{3,2,1,0:T(8,128)S(1)}, f32[24,8,8,128]{3,2,1,0:T(8,128)S(1)}, f32[7,8,128]{2,1,0:T(8,128)S(1)}) custom-call(f32[24,4,8,128]{3,2,1,0:T(8,128)S(1)} %get-tuple-element.68.refs_0_.refs_10_, f32[24,4,8,128]{3,2,1,0:T(8,128)S(1)} %get-tuple-element.69.refs_1_.refs_13_, ...), custom_call_target="tpu_custom_call" | custom-call | tf_op jit(solution)/shard_map/inner2/pallas_call | solution.py:494
  31.1 0.0 collective-permute-done.4.ha
  31.1 1.7 %collective-permute-done.5.hb = f32[24,4,8,128]{3,2,1,0:T(8,128)S(1)} collective-permute-done((f32[24,4,8,128]{3,2,1,0:T(8,128)S(1)}, f32[24,4,8,128]{3,2,1,0:T(8,128)S(1)}, u32[]{:S(2)}, u32[]{:S(2)}) %collective-permute-start.5) | collective-permute-done | bytes 393248 | tf_op jit(solution)/shard_map/ppermute | solution.py:510
  32.8 0.6 edge3.1
  33.4 31.9 %all_to_all.11 = f32[128,1,128]{2,1,0:T(1,128)S(1)} all-to-all(f32[128,1,128]{2,1,0:T(1,128)S(1)} %bitcast.50), channel_id=1, replica_groups=mesh['flow_0'=4,'flow_1'=4,'flow_2'=4,'flow_3'=2] {'flow_0','flow_1','fl..., dimensions={0} | all-to-all | bytes 131072 | tf_op jit(solution)/shard_map/all_to_all | solution.py:578
  65.3 2.7 %combine.1 = (f32[24,3,64,128]{3,2,1,0:T(8,128)}, f32[24,3,64,128]{3,2,1,0:T(8,128)}) custom-call(f32[128,128]{1,0:T(8,128)S(1)} %bitcast.49, f32[24,8,8,128]{3,2,1,0:T(8,128)S(1)} %get-tuple-element.63.refs_6_.u0.refs_0_, f32[24,8,8,128]{3,2,1,0:T(8,128)S(1)} %get-tuple-element.64.refs_7_.u1.refs_1_, ...), custom_call_target="tpu_custom_call" | custom-call | tf_op jit(solution)/shard_map/combine/pallas_call | solution.py:494
Async XLA Ops:
  3.0 9.5 %collective-permute-start = (f32[24,4,8,128]{3,2,1,0:T(8,128)S(1)}, f32[24,4,8,128]{3,2,1,0:T(8,128)S(1)}, u32[]{:S(2)}, u32[]{:S(2)}) collective-permute-start(f32[24,4,8,128]{3,2,1,0:T(8,128)S(1)} %get-tuple-element.43.sa.refs_8_), channel_id=1, source_target_pairs={{0,1},{1,0},{2,3},{3,2},{4,5},{5,4},{6,7},{7,6},{8,9},{9,8},{10,11... | collective-permute-start | bytes 1179656 | tf_op jit(solution)/shard_map/ppermute | solution.py:511
  4.4 9.1 %collective-permute-start.1 = (f32[24,4,8,128]{3,2,1,0:T(8,128)S(1)}, f32[24,4,8,128]{3,2,1,0:T(8,128)S(1)}, u32[]{:S(2)}, u32[]{:S(2)}) collective-permute-start(f32[24,4,8,128]{3,2,1,0:T(8,128)S(1)} %get-tuple-element.44.sb.refs_11_), channel_id=1, source_target_pairs={{1,2},{3,4},{5,6},{7,8},{9,10},{11,12},{13,14},{15,16},{17,18},{19... | collective-permute-start | bytes 1179656 | tf_op jit(solution)/shard_map/ppermute | solution.py:510
  13.9 7.3 %collective-permute-start.2 = (f32[24,4,8,128]{3,2,1,0:T(8,128)S(1)}, f32[24,4,8,128]{3,2,1,0:T(8,128)S(1)}, u32[]{:S(2)}, u32[]{:S(2)}) collective-permute-start(f32[24,4,8,128]{3,2,1,0:T(8,128)S(1)} %get-tuple-element.57.refs_0_.refs_9_), channel_id=1, source_target_pairs={{0,1},{1,0},{2,3},{3,2},{4,5},{5,4},{6,7},{7,6},{8,9},{9,8},{10,11... | collective-permute-start | bytes 1179656 | tf_op jit(solution)/shard_map/ppermute | solution.py:511
  14.0 9.1 %collective-permute-start.3 = (f32[24,4,8,128]{3,2,1,0:T(8,128)S(1)}, f32[24,4,8,128]{3,2,1,0:T(8,128)S(1)}, u32[]{:S(2)}, u32[]{:S(2)}) collective-permute-start(f32[24,4,8,128]{3,2,1,0:T(8,128)S(1)} %get-tuple-element.58.refs_1_.refs_12_), channel_id=1, source_target_pairs={{1,2},{3,4},{5,6},{7,8},{9,10},{11,12},{13,14},{15,16},{17,18},{19... | collective-permute-start | bytes 1179656 | tf_op jit(solution)/shard_map/ppermute | solution.py:510
  23.5 7.5 %collective-permute-start.4 = (f32[24,4,8,128]{3,2,1,0:T(8,128)S(1)}, f32[24,4,8,128]{3,2,1,0:T(8,128)S(1)}, u32[]{:S(2)}, u32[]{:S(2)}) collective-permute-start(f32[24,4,8,128]{3,2,1,0:T(8,128)S(1)} %get-tuple-element.68.refs_0_.refs_10_), channel_id=1, source_target_pairs={{0,1},{1,0},{2,3},{3,2},{4,5},{5,4},{6,7},{7,6},{8,9},{9,8},{10,11... | collective-permute-start | bytes 1179656 | tf_op jit(solution)/shard_map/ppermute | solution.py:511
  23.6 9.1 %collective-permute-start.5 = (f32[24,4,8,128]{3,2,1,0:T(8,128)S(1)}, f32[24,4,8,128]{3,2,1,0:T(8,128)S(1)}, u32[]{:S(2)}, u32[]{:S(2)}) collective-permute-start(f32[24,4,8,128]{3,2,1,0:T(8,128)S(1)} %get-tuple-element.69.refs_1_.refs_13_), channel_id=1, source_target_pairs={{1,2},{3,4},{5,6},{7,8},{9,10},{11,12},{13,14},{15,16},{17,18},{19... | collective-permute-start | bytes 1179656 | tf_op jit(solution)/shard_map/ppermute | solution.py:510

commit v2 on v0

v2 whole, which is shorter than its diff:
```python
import jax
import jax.numpy as jnp
from jax import lax
from jax.experimental import pallas as pl
from jax.experimental.pallas import tpu as pltpu
from jax.sharding import Mesh
from jax.sharding import PartitionSpec as P


FLOW = ("flow_0", "flow_1", "flow_2", "flow_3")
CORE = "flow_3"
epsilon = 1e-06
relaxation = 0.5
reach_weights = (1.0, 0.6, 0.35, 0.2)
horiz_total = 2.0 * sum(reach_weights) + 2.0

L = 12
PLANES = 2 * L
ROWS = 24
REACH = 4
HALF = 12
F32 = jnp.float32
TILE = (8, 128)
GRAM = [(a, b) for b in range(4) for a in range(b + 1)]

VM = pl.BlockSpec(memory_space=pltpu.VMEM)
HB = pl.BlockSpec(memory_space=pltpu.HBM)


def vmem(*lead):
    return pltpu.VMEM((*lead, *TILE), F32)


def span(start, stop):
    return list(range(start, stop))


def place_of(core, t):
    tile, sub = t // 8, t % 8
    return (
        jnp.where(core == 1, tile, 2 - tile),
        jnp.where(core == 1, sub, 7 - sub),
    )


def raw_row(ref, plane, place):
    tile, sub = place
    return ref[plane, tile, pl.ds(sub, 8, stride=8), :]


class Field:
    def __init__(self, *parts):
        self.parts = parts

    def find(self, t):
        for ref, first, index in self.parts:
            if t in index:
                return ref, first, index[t]
        raise KeyError(t)

    def row(self, plane, t):
        ref, first, i = self.find(t)
        return ref[first + plane, i]

    def get(self, plane, ts):
        return jnp.stack([self.row(plane, t) for t in ts])

    def put(self, plane, ts, value):
        for i, t in enumerate(ts):
            ref, first, j = self.find(t)
            ref[first + plane, j] = value[i]


def part(ref, start, stop, first=0):
    return (ref, first, {t: t - start for t in range(start, stop)})


def mirrored(ref, start, stop, first=0):
    return (ref, first, {ROWS - 1 - d: d - start for d in range(start, stop)})


def factor(ts, read, inv_real, inv_imag, link, nu_out):
    vert, active, nu, drag, rot = read
    imag = jnp.where(active, rot, 0.0)
    base = (relaxation + horiz_total) * nu
    if nu_out is not None:
        nu_out.put(0, ts, jnp.where(active, nu, 0.0))
    below = er = ei = None
    for k in range(L):
        real = base + (drag if k == 0 else below)
        if k < L - 1:
            above = vert(k)
            real = real + above
        real = jnp.where(active, real, 1.0)
        pivot_imag = imag
        if k > 0:
            ln = jnp.where(active, below, 0.0)
            link.put(k - 1, ts, ln)
            square = ln * ln
            real = real - square * er
            pivot_imag = imag - square * ei
        inverse = 1.0 / (real * real + pivot_imag * pivot_imag)
        er = real * inverse
        ei = -(pivot_imag * inverse)
        inv_real.put(k, ts, er)
        inv_imag.put(k, ts, ei)
        if k < L - 1:
            below = above


def solve(ts, source, inv_real, inv_imag, link, result, also=None):
    cf = cg = None
    for k in range(L):
        sf, sg = source(k, ts), source(L + k, ts)
        if k > 0:
            ln = link.get(k - 1, ts)
            sf = sf + ln * cf
            sg = sg + ln * cg
        er, ei = inv_real.get(k, ts), inv_imag.get(k, ts)
        cf, cg = er * sf + ei * sg, er * sg - ei * sf
        result.put(k, ts, cf)
        result.put(L + k, ts, cg)
    xf, xg = cf, cg
    for k in range(L - 1, -1, -1):
        if k < L - 1:
            ln = link.get(k, ts)
            pf, pg = ln * xf, ln * xg
            er, ei = inv_real.get(k, ts), inv_imag.get(k, ts)
            xf = result.get(k, ts) + (er * pf + ei * pg)
            xg = result.get(L + k, ts) + (er * pg - ei * pf)
            result.put(k, ts, xf)
            result.put(L + k, ts, xg)
        if also is not None:
            copy, rows = also
            for i, t in enumerate(ts):
                if t in rows:
                    copy.put(k, [t], xf[i : i + 1])
                    copy.put(L + k, [t], xg[i : i + 1])


def lanes():
    return lax.broadcasted_iota(jnp.int32, TILE, 1)


def cross_masks():
    lane = lanes()
    sub = lax.broadcasted_iota(jnp.int32, TILE, 0)
    first, last = lane == 0, lane == 127
    return first, last, first & (sub == 7), last & (sub == 0)


def cross(s, masks):
    first, last, first_end, last_end = masks
    up = jnp.where(first, pltpu.roll(s, 7, 0), s)
    up = jnp.where(first_end, 0.0, up)
    down = jnp.where(last, pltpu.roll(s, 1, 0), s)
    down = jnp.where(last_end, 0.0, down)
    return pltpu.roll(up, 127, 1) + pltpu.roll(down, 1, 1)


def stencil(ts, known, s, masks):
    for t in ts:
        total = cross(s[t], masks)
        for m in range(1, REACH + 1):
            near = [s[q] for q in (t - m, t + m) if q in known]
            if near:
                both = near[0] + near[1] if len(near) == 2 else near[0]
                weight = reach_weights[m - 1]
                total = total + (both if weight == 1.0 else weight * both)
        yield t, total


def halo_sum(total, distance, halo):
    for q in range(1, REACH + 1 - distance):
        weight = reach_weights[distance + q - 1]
        value = halo(q - 1)
        total = total + (value if weight == 1.0 else weight * value)
    return total


def loop_sums(pairs, step):
    pairs = list(pairs)

    def run(plane, carry):
        sums = dict(zip(pairs, carry))

        def add(pair, value):
            sums[pair] = sums[pair] + value

        step(plane, add)
        return tuple(sums[pair] for pair in pairs)

    zero = jnp.zeros(TILE, F32)
    return dict(zip(pairs, lax.fori_loop(0, PLANES, run, (zero,) * len(pairs))))


def with_all(add, b, value, plane, t, us):
    for a in range(b):
        add((a, b), value * us[a].row(plane, t))
    add((b, b), value * value)


def pairs_of(*bs):
    return [(a, b) for a, b in GRAM if b in bs]


def raw_reader(r, core, ts):
    places = [place_of(core, t) for t in ts]

    def rows(ref, plane):
        return jnp.stack([raw_row(ref, plane, place) for place in places])

    active = rows(r.iceraw, 0) > 0
    drag = jnp.where(rows(r.groundraw, 0) > 0, rows(r.fricraw, 0), 0.0)
    return (
        lambda k: rows(r.vraw, k),
        active,
        rows(r.nuraw, 0),
        drag,
        rows(r.rotraw, 0),
    )


def raw_source(fraw, core):
    return lambda plane, ts: jnp.stack([raw_row(fraw, plane, place_of(core, t)) for t in ts])


def load_kernel(r):
    core = lax.axis_index(CORE)
    edge = jnp.where(core == 1, 2, 0)
    small = [
        pltpu.make_async_copy(getattr(r, n), getattr(r, n + "raw"), r.sems.at[i])
        for i, n in enumerate(("nu", "fric", "rot", "ice", "ground"))
    ]
    v_copy = [
        pltpu.make_async_copy(r.v.at[:, tile], r.vraw.at[:, tile], r.sems.at[5 + i])
        for i, tile in enumerate((edge, 1, 2 - edge))
    ]
    f_copy = [
        pltpu.make_async_copy(r.f.at[:, tile], r.fraw.at[:, tile], r.sems.at[8 + i])
        for i, tile in enumerate((edge, 1, 2 - edge))
    ]
    for copy in small + v_copy[:2] + f_copy[:2] + [v_copy[2], f_copy[2]]:
        copy.start()
    for copy in small + v_copy[:2]:
        copy.wait()
    er, ei, link, nu = (Field(part(x, HALF, ROWS)) for x in (r.er, r.ei, r.link, r.nuh))
    packed = Field(mirrored(r.p1, 0, REACH))
    for start in (12, 18):
        ts = span(start, start + 6)
        read = raw_reader(r, core, ts)
        factor(ts, read, er, ei, link, nu)
        vert, active, nu_row, drag, rot = read
        for i, t in enumerate(ts):
            if t >= ROWS - REACH:
                for k in range(L - 1):
                    packed.put(PLANES + k, [t], vert(k)[i : i + 1])
                packed.put(PLANES + L - 1, [t], jnp.where(active, nu_row, 0.0)[i : i + 1])
                packed.put(PLANES + L, [t], drag[i : i + 1])
                packed.put(PLANES + L + 1, [t], rot[i : i + 1])
    for copy in f_copy[:2]:
        copy.wait()
    source = raw_source(r.fraw, core)
    s0 = Field(part(r.s0, HALF, ROWS))
    for start in (12, 18):
        ts = span(start, start + 6)
        solve(ts, source, er, ei, link, s0, (packed, span(ROWS - REACH, ROWS)))
    v_copy[2].wait()
    f_copy[2].wait()


def ahead_kernel(r):
    masks = cross_masks()
    s0 = Field(part(r.s0, HALF, ROWS))
    nu = Field(part(r.nuh, HALF, ROWS))
    sums = Field(mirrored(r.p2, 0, REACH))
    known = span(HALF, ROWS)
    u1 = Field(part(r.u1, 16, 20))

    def step(plane, carry):
        s = {t: s0.row(plane, t) for t in known}
        for t, total in stencil(span(16, 24), known, s, masks):
            if t < 20:
                u1.put(plane, [t], (nu.row(0, t) * total)[None])
            else:
                sums.put(plane, [t], total[None])
        return carry

    lax.fori_loop(0, PLANES, step, 0)
    er, ei, link = (Field(part(x, HALF, ROWS)) for x in (r.er, r.ei, r.link))
    packed = Field(mirrored(r.p2, REACH, 2 * REACH, PLANES))
    solve(span(16, 20), u1.get, er, ei, link, Field(part(r.s1, 16, 20)), (packed, span(16, 20)))


def rest_kernel(r):
    core = lax.axis_index(CORE)
    er, ei, link, nu = (Field(part(x, 0, HALF)) for x in (r.er, r.ei, r.link, r.nuh))
    for start in (0, 6):
        ts = span(start, start + 6)
        factor(ts, raw_reader(r, core, ts), er, ei, link, nu)
    places = [place_of(core, t) for t in range(ROWS)]

    def spread(plane, carry):
        for t in range(ROWS):
            r.u0[plane, t] = raw_row(r.fraw, plane, places[t])
        return carry

    lax.fori_loop(0, PLANES, spread, 0)
    u0 = Field(part(r.u0, 0, ROWS))
    s0 = Field(part(r.s0, 0, HALF))
    for start in (0, 6):
        solve(span(start, start + 6), u0.get, er, ei, link, s0, (Field(part(r.sa, 0, REACH)), span(0, REACH)))


def both_halves(r, name):
    return Field(part(getattr(r, name + "_a"), 0, HALF), part(getattr(r, name + "_b"), HALF, ROWS))


def inner1_kernel(r):
    masks = cross_masks()
    s0, nu = both_halves(r, "s0"), both_halves(r, "nuh")
    known = span(0, 20)

    def step(plane, carry):
        s = {t: s0.row(plane, t) for t in known}
        for t, total in stencil(span(0, 16), known, s, masks):
            if t < REACH:
                r.nsum[plane, t] = total
            else:
                r.u1[plane, t - REACH] = nu.row(0, t) * total
        return carry

    lax.fori_loop(0, PLANES, step, 0)


def edge_a_kernel(r):
    nu = Field(part(r.nuh_a, 0, HALF))
    er, ei, link = (both_halves(r, n) for n in ("er", "ei", "link"))
    edge = Field(part(r.u_edge, 0, REACH))
    inner = Field(part(r.u_in, REACH, 16))

    def source(plane, ts):
        rows = []
        for t in ts:
            if t < REACH:
                value = halo_sum(r.nsum[plane, t], t, lambda q: r.ha[plane, q])
                value = nu.row(0, t) * value
                edge.put(plane, [t], value[None])
            else:
                value = inner.row(plane, t)
            rows.append(value)
        return jnp.stack(rows)

    result = Field(part(r.s, 0, 16))
    sa = Field(part(r.sa, 0, REACH))
    for start in (0, 8):
        solve(span(start, start + 8), source, er, ei, link, result, (sa, span(0, REACH)))


def write_sums(ref, sums):
    zero = jnp.zeros(TILE, F32)
    for i, pair in enumerate(GRAM):
        ref[i] = sums.get(pair, zero)


def inner2_kernel(r):
    masks = cross_masks()
    s1 = Field(part(r.s1_a, 0, 16), part(r.s1_m, 16, 20))
    nu = both_halves(r, "nuh")
    u0 = Field(part(r.u0, 0, ROWS))
    u1 = Field(part(r.u1_e, 0, REACH), part(r.u1_i, REACH, 16), part(r.u1_m, 16, 20))
    known = span(0, 20)

    def step(plane, add):
        s = {t: s1.row(plane, t) for t in known}
        for t, total in stencil(span(0, 16), known, s, masks):
            if t < REACH:
                r.nsum[plane, t] = total
            else:
                value = nu.row(0, t) * total
                r.u2[plane, t - REACH] = value
                with_all(add, 2, value, plane, t, (u0, u1))
        for t in span(0, ROWS):
            value = u0.row(plane, t)
            add((0, 0), value * value)
            if t < 20:
                with_all(add, 1, u1.row(plane, t), plane, t, (u0,))

    write_sums(r.sums, loop_sums(pairs_of(0, 1, 2), step))


def inner3_kernel(r):
    masks = cross_masks()
    s2 = Field(part(r.s2, 0, 16))
    nu = Field(part(r.nuh_a, 0, HALF))
    u0 = Field(part(r.u0, 0, ROWS))
    u1 = Field(part(r.u1_e, 0, REACH), part(r.u1_i, REACH, 16))
    u2 = Field(part(r.u2_e, 0, REACH), part(r.u2_i, REACH, 16))
    known = span(0, 16)

    def step(plane, add):
        s = {t: s2.row(plane, t) for t in known}
        for t, total in stencil(span(0, HALF), known, s, masks):
            if t < REACH:
                r.nsum[plane, t] = total
                with_all(add, 2, u2.row(plane, t), plane, t, (u0, u1))
            else:
                value = nu.row(0, t) * total
                r.u3[plane, t - REACH] = value
                with_all(add, 3, value, plane, t, (u0, u1, u2))

    write_sums(r.sums, loop_sums(pairs_of(2, 3), step))


def beyond_kernel(r):
    nu_a = Field(part(r.nuh_a, 0, HALF))
    nu_b = Field(part(r.nuh_b, HALF, ROWS))
    u0 = Field(part(r.u0, 0, ROWS))
    u1 = Field(part(r.u1_e, 0, REACH))
    u2 = Field(part(r.u2_e, 0, REACH))
    ts = span(ROWS, ROWS + REACH)
    nu = r.p1[PLANES + L - 1]
    read = (
        lambda k: r.p1[PLANES + k],
        nu > 0.0,
        nu,
        r.p1[PLANES + L],
        r.p1[PLANES + L + 1],
    )
    er, ei, link = (Field(part(x, ROWS, ROWS + REACH)) for x in (r.er, r.ei, r.link))
    factor(ts, read, er, ei, link, None)

    def step(plane, add):
        for t in range(REACH):
            value = halo_sum(r.nsum[plane, t], t, lambda q: r.ha[plane, q])
            value = nu_a.row(0, t) * value
            r.u3[plane, t] = value
            with_all(add, 3, value, plane, t, (u0, u1, u2))
        for d in range(REACH):
            t = ROWS - 1 - d
            value = nu_b.row(0, t) * halo_sum(r.p2s[plane, d], d, lambda q: r.p1[plane, q])
            r.u1[plane, t - 20] = value
            with_all(add, 1, value, plane, t, (u0,))

    write_sums(r.sums, loop_sums(pairs_of(1, 3), step))


def band_kernel(r):
    masks = cross_masks()
    nu_b = Field(part(r.nuh_b, HALF, ROWS))
    nu = Field(part(r.nuh_b, HALF, ROWS), part(r.p1, ROWS, ROWS + REACH, PLANES + L - 1))
    er, ei, link = (
        Field(part(getattr(r, n + "_b"), HALF, ROWS), part(getattr(r, n + "_h"), ROWS, ROWS + REACH))
        for n in ("er", "ei", "link")
    )
    s0 = Field(part(r.s0_b, HALF, ROWS))
    u1 = Field(part(r.u1_i, REACH, 16), part(r.u1_m, 16, 20), part(r.u1_b, 20, ROWS))

    def source(plane, ts):
        rows = []
        for t in ts:
            if t < ROWS:
                rows.append(u1.row(plane, t))
            else:
                j = t - ROWS
                value = halo_sum(r.p2[plane, j], j, lambda q: s0.row(plane, ROWS - 1 - q))
                rows.append(nu.row(0, t) * value)
        return jnp.stack(rows)

    s1_b = part(r.s1, 20, 28)
    solve(span(20, 28), source, er, ei, link, Field(s1_b))
    s1 = Field(
        part(r.s1_a, 0, 16), part(r.s1_m, 16, 20), s1_b, part(r.p2, 28, 32, PLANES)
    )
    u0 = Field(part(r.u0, 0, ROWS))
    u2_b = part(r.u2, 16, 28)
    u2 = Field(part(r.u2_i, REACH, 16), u2_b)
    known = span(12, 32)

    def step(plane, add):
        s = {t: s1.row(plane, t) for t in known}
        for t, total in stencil(span(16, 28), known, s, masks):
            value = nu.row(0, t) * total
            u2.put(plane, [t], value[None])
            if t < ROWS:
                with_all(add, 2, value, plane, t, (u0, u1))

    sums = loop_sums(pairs_of(2), step)
    s2_b = part(r.s2, 16, 28)
    for start in (16, 22):
        solve(span(start, start + 6), u2.get, er, ei, link, Field(s2_b))
    s2 = Field(part(r.s2_a, 0, 16), s2_b)
    known3 = span(8, 28)

    def last(plane, add):
        s = {t: s2.row(plane, t) for t in known3}
        for t, total in stencil(span(12, 24), known3, s, masks):
            value = nu_b.row(0, t) * total
            r.u3[plane, t - 12] = value
            with_all(add, 3, value, plane, t, (u0, u1, u2))

    sums.update(loop_sums(pairs_of(3), last))
    lane = lanes()
    out = jnp.zeros(TILE, F32)
    for i, pair in enumerate(GRAM):
        value = r.sums2[i] + r.sums3[i] + r.sums4[i]
        if pair in sums:
            value = value + sums[pair]
        value = jnp.sum(jnp.sum(value, axis=0, keepdims=True), axis=1, keepdims=True)
        out = out + jnp.where(lane == i, value, 0.0)
    for i in range(r.payload.shape[0] // 8):
        r.payload[pl.ds(8 * i, 8), :] = out


def least_squares(columns, start):
    count_cols = len(columns)
    givens_rhs = [start] + [start * 0.0 for index in range(count_cols)]
    cosines, sines, upper_cols = ([], [], [])
    for column_index, column_in in enumerate(columns):
        column = list(column_in)
        for row_index in range(column_index):
            rotated_a = (
                cosines[row_index] * column[row_index] + sines[row_index] * column[row_index + 1]
            )
            rotated_b = (
                -sines[row_index] * column[row_index] + cosines[row_index] * column[row_index + 1]
            )
            column[row_index] = rotated_a
            column[row_index + 1] = rotated_b
        radius = jnp.sqrt(
            column[column_index] * column[column_index]
            + column[column_index + 1] * column[column_index + 1]
        )
        inverse = 1.0 / radius
        cosine = column[column_index] * inverse
        sine_value = column[column_index + 1] * inverse
        column[column_index] = inverse
        cosines.append(cosine)
        sines.append(sine_value)
        upper_cols.append(column)
        next_rhs = -sine_value * givens_rhs[column_index]
        givens_rhs[column_index] = cosine * givens_rhs[column_index]
        givens_rhs[column_index + 1] = next_rhs
    factors = [None] * count_cols
    for column_index in range(count_cols - 1, -1, -1):
        accum = givens_rhs[column_index]
        for later in range(column_index + 1, count_cols):
            accum = accum - upper_cols[later][column_index] * factors[later]
        factors[column_index] = accum * upper_cols[column_index][column_index]
    return factors


def dot(left, right):
    total = left[0] * right[0]
    for a, b in zip(left[1:], right[1:]):
        total = total + a * b
    return total


def coefficients(gram):
    size = 4
    upper = {}
    for a in range(size):
        square = gram[(a, a)]
        for p in range(a):
            square = square - upper[(p, a)] * upper[(p, a)]
        square = jnp.maximum(square, 0.0)
        length = jnp.sqrt(square)
        inverse = jnp.where(length > 0.0, 1.0 / jnp.where(length > 0.0, length, 1.0), 0.0)
        upper[(a, a)] = length
        for b in range(a + 1, size):
            value = gram[(a, b)]
            for p in range(a):
                value = value - upper[(p, a)] * upper[(p, b)]
            upper[(a, b)] = value * inverse
    beta = jnp.sqrt(gram[(0, 0)] + epsilon)
    inverse = 1.0 / beta
    basis = [[inverse]]
    ortho = [[upper[(0, 0)] * inverse]]
    columns = []
    for j in range(3):
        current = basis[j]
        w = [current[0]]
        for i in range(1, j + 1):
            w.append(current[i] - current[i - 1])
        w.append(-current[j])
        q = [dot([upper[(i, m)] for m in range(i, j + 2)], w[i:]) for i in range(j + 2)]
        column = []
        for i in range(j + 1):
            h = dot(q[: i + 1], ortho[i])
            for m in range(i + 1):
                q[m] = q[m] - h * ortho[i][m]
                w[m] = w[m] - h * basis[i][m]
            column.append(h)
        length = jnp.sqrt(dot(q, q) + epsilon)
        column.append(length)
        columns.append(column)
        if j < 2:
            inverse = 1.0 / length
            basis.append([value * inverse for value in w])
            ortho.append([value * inverse for value in q])
    y = least_squares(columns, beta)
    return [dot(y[i:], [basis[j][i] for j in range(i, 3)]) for i in range(3)]


def final_kernel(r):
    total = r.gathered[pl.ds(0, 8), :]
    for i in range(1, r.gathered.shape[0] // 8):
        total = total + r.gathered[pl.ds(8 * i, 8), :]
    total = jnp.sum(total, axis=0, keepdims=True)
    total = jnp.broadcast_to(total, TILE)
    lane = lanes()
    gram = {}
    for i, pair in enumerate(GRAM):
        value = jnp.sum(jnp.where(lane == i, total, 0.0), axis=1, keepdims=True)
        gram[pair] = jnp.broadcast_to(value, TILE)
    c0, c1, c2 = coefficients(gram)
    e0, e1, e2 = 1.0 - c0, c0 - c1, c1 - c2
    core = lax.axis_index(CORE)
    places = [place_of(core, t) for t in range(ROWS)]
    s0 = both_halves(r, "s0")
    s1 = Field(part(r.s1_a, 0, 16), part(r.s1_m, 16, 20), part(r.s1_b, 20, 28))
    s2 = Field(part(r.s2_a, 0, 16), part(r.s2_b, 16, 28))
    u0 = Field(part(r.u0, 0, ROWS))
    u1 = Field(
        part(r.u1_e, 0, 4), part(r.u1_i, 4, 16), part(r.u1_m, 16, 20), part(r.u1_b, 20, 24)
    )
    u2 = Field(part(r.u2_e, 0, 4), part(r.u2_i, 4, 16), part(r.u2_b, 16, 28))
    u3 = Field(part(r.u3_e, 0, 4), part(r.u3_i, 4, 12), part(r.u3_b, 12, 24))

    def step(plane, carry):
        for t in range(ROWS):
            s = [x.row(plane, t) for x in (s0, s1, s2)]
            u = [x.row(plane, t) for x in (u0, u1, u2, u3)]
            tile, sub = places[t]
            r.buf_s[plane, tile, pl.ds(sub, 8, stride=8), :] = c0 * s[0] + c1 * s[1] + c2 * s[2]
            r.buf_r[plane, tile, pl.ds(sub, 8, stride=8), :] = (
                e0 * u[0] + e1 * u[1] + (e2 * u[2] + c2 * u[3])
            )
        pltpu.make_async_copy(r.buf_s.at[plane], r.out_s.at[plane], r.sem_s).start()
        pltpu.make_async_copy(r.buf_r.at[plane], r.out_r.at[plane], r.sem_r).start()
        return carry

    lax.fori_loop(0, PLANES, step, 0)
    pltpu.make_async_copy(r.buf_s, r.out_s, r.sem_s).wait()
    pltpu.make_async_copy(r.buf_r, r.out_r, r.sem_r).wait()


def tiled(x):
    x = x.reshape(-1, ROWS // 8, 8, 8, 128)
    return x.transpose(0, 1, 3, 2, 4).reshape(-1, ROWS // 8, 64, 128)


def untiled(x):
    x = x.reshape(PLANES, ROWS // 8, 8, 8, 128).transpose(0, 1, 3, 2, 4)
    return x.reshape(2, L, ROWS, 1024)


class Refs:
    def __init__(self, names, refs):
        self.__dict__.update(zip(names, refs))


def call(kernel, name, ins, outs, scratch={}, in_specs=None, out_specs=None, limit=4 << 20):
    names = [*ins, *outs, *scratch]

    def run(*refs):
        kernel(Refs(names, refs))

    results = pl.pallas_call(
        run,
        out_shape=list(outs.values()),
        in_specs=[in_specs or VM] * len(ins),
        out_specs=[out_specs or VM] * len(outs),
        scratch_shapes=list(scratch.values()),
        compiler_params=pltpu.CompilerParams(vmem_limit_bytes=limit),
        name=name,
    )(*ins.values())
    return dict(zip(outs, results))


def within(x):
    return lax.ppermute(x, FLOW, [(i, i ^ 1) for i in range(128)])


def across(x):
    pairs = [(i, i + 1) for i in range(1, 127, 2)]
    return lax.ppermute(x, FLOW, pairs + [(b, a) for a, b in pairs])


def body(forcing, viscosity, friction, rotation, vertical, ice_mask, grounded):
    names = ("f", "v", "nu", "fric", "rot", "ice", "ground")
    arrays = (forcing, vertical, viscosity, friction, rotation, ice_mask, grounded)
    ins = {
        n: pltpu.with_memory_space_constraint(tiled(x), pltpu.HBM) for n, x in zip(names, arrays)
    }
    raws = {n + "raw": pltpu.VMEM(x.shape, x.dtype) for n, x in ins.items()}

    def factors(rows):
        return {"er": vmem(L, rows), "ei": vmem(L, rows), "link": vmem(L - 1, rows)}

    def pick(src, tag, *keys):
        return {k + tag: src[k] for k in keys}

    edge = vmem(PLANES, REACH)
    k0 = call(
        load_kernel,
        "load",
        ins,
        {
            **factors(HALF),
            "nuh": vmem(1, HALF),
            "s0": vmem(PLANES, HALF),
            "p1": vmem(PLANES + L + 2, REACH),
            **raws,
        },
        {"sems": pltpu.SemaphoreType.DMA((11,))},
        in_specs=HB,
    )
    p1 = across(k0["p1"])
    ahead = call(
        ahead_kernel,
        "ahead",
        pick(k0, "", "s0", "nuh", "er", "ei", "link"),
        {"u1": edge, "s1": edge, "p2": vmem(2 * PLANES, REACH)},
    )
    p2 = across(ahead["p2"])
    k1 = call(
        rest_kernel,
        "rest",
        {**pick(k0, "", *raws), "order": ahead["p2"]},
        {
            **factors(HALF),
            "nuh": vmem(1, HALF),
            "s0": vmem(PLANES, HALF),
            "u0": vmem(PLANES, ROWS),
            "sa": edge,
        },
    )
    halves = {}
    for key in ("er", "ei", "link", "nuh", "s0"):
        halves[key + "_a"], halves[key + "_b"] = k1[key], k0[key]
    u0 = {"u0": k1["u0"]}

    def some(*keys):
        return {k: halves[k] for k in keys}

    operator = some("er_a", "er_b", "ei_a", "ei_b", "link_a", "link_b", "nuh_a")
    solved = {"u_edge": edge, "s": vmem(PLANES, 16), "sa": edge}
    ha = within(k1["sa"])
    n1 = call(
        inner1_kernel,
        "inner1",
        some("s0_a", "s0_b", "nuh_a", "nuh_b"),
        {"nsum": edge, "u1": vmem(PLANES, HALF)},
    )
    e1 = call(
        edge_a_kernel,
        "edge1",
        {"ha": ha, "nsum": n1["nsum"], "u_in": n1["u1"], **operator},
        solved,
    )
    ha = within(e1["sa"])
    first = {"u1_e": e1["u_edge"], "u1_i": n1["u1"]}
    middle = {"u1_m": ahead["u1"]}
    s1 = {"s1_a": e1["s"], "s1_m": ahead["s1"]}
    n2 = call(
        inner2_kernel,
        "inner2",
        {**s1, **some("nuh_a", "nuh_b"), **u0, **first, **middle},
        {"nsum": edge, "u2": vmem(PLANES, HALF), "sums": vmem(10)},
    )
    e2 = call(
        edge_a_kernel,
        "edge2",
        {"ha": ha, "nsum": n2["nsum"], "u_in": n2["u2"], **operator},
        solved,
    )
    ha = within(e2["sa"])
    second = {"u2_e": e2["u_edge"], "u2_i": n2["u2"]}
    n3 = call(
        inner3_kernel,
        "inner3",
        {"s2": e2["s"], **some("nuh_a"), **u0, **first, **second},
        {"nsum": edge, "u3": vmem(PLANES, 8), "sums": vmem(10)},
    )
    b1 = call(
        beyond_kernel,
        "beyond",
        {
            "ha": ha,
            "nsum": n3["nsum"],
            "p1": p1,
            "p2s": ahead["p2"],
            **some("nuh_a", "nuh_b"),
            **u0,
            "u1_e": first["u1_e"],
            "u2_e": second["u2_e"],
        },
        {**factors(REACH), "u1": edge, "u3": edge, "sums": vmem(10)},
    )
    b2 = call(
        band_kernel,
        "band",
        {
            "p1": p1,
            "p2": p2,
            **some("er_b", "ei_b", "link_b", "nuh_b", "s0_b"),
            **pick(b1, "_h", "er", "ei", "link"),
            **u0,
            "u1_i": n1["u1"],
            **middle,
            "u1_b": b1["u1"],
            **s1,
            "u2_i": n2["u2"],
            "s2_a": e2["s"],
            "sums2": n2["sums"],
            "sums3": n3["sums"],
            "sums4": b1["sums"],
        },
        {
            "s1": vmem(PLANES, 8),
            "u2": vmem(PLANES, HALF),
            "s2": vmem(PLANES, HALF),
            "u3": vmem(PLANES, HALF),
            "payload": jax.ShapeDtypeStruct((128, 128), F32),
        },
    )
    gathered = lax.all_to_all(b2["payload"], FLOW, split_axis=0, concat_axis=0, tiled=True)
    shape = (PLANES, ROWS // 8, 64, 128)
    outs = call(
        final_kernel,
        "combine",
        {
            "gathered": gathered,
            **some("s0_a", "s0_b"),
            **s1,
            "s1_b": b2["s1"],
            "s2_a": e2["s"],
            "s2_b": b2["s2"],
            **u0,
            **first,
            **middle,
            "u1_b": b1["u1"],
            **second,
            "u2_b": b2["u2"],
            "u3_e": b1["u3"],
            "u3_i": n3["u3"],
            "u3_b": b2["u3"],
        },
        {"out_s": jax.ShapeDtypeStruct(shape, F32), "out_r": jax.ShapeDtypeStruct(shape, F32)},
        {
            "buf_s": pltpu.VMEM(shape, F32),
            "buf_r": pltpu.VMEM(shape, F32),
            "sem_s": pltpu.SemaphoreType.DMA,
            "sem_r": pltpu.SemaphoreType.DMA,
        },
        out_specs=HB,
        limit=8 << 20,
    )
    return untiled(outs["out_s"]), untiled(outs["out_r"])


def solution(mesh):
    finer = Mesh(mesh.devices.reshape(4, 4, 4, 2), FLOW)
    return jax.shard_map(
        body,
        mesh=finer,
        in_specs=(
            P(None, None, FLOW, None),
            P(FLOW, None),
            P(FLOW, None),
            P(FLOW, None),
            P(None, FLOW, None),
            P(FLOW, None),
            P(FLOW, None),
        ),
        out_specs=(P(None, None, FLOW, None), P(None, None, FLOW, None)),
        check_vma=False,
    )
```

time: 241 us -> 64.6 us (0.27)
  the two profiles are of different devices: /device:TPU:8 before, /device:TPU:1 now
where the time goes in v2:
time: 64.6 us; the launch traced here: 64.4 us
  Pallas kernels  24.3 us (38%)
  blocking collectives  23.5 us (36%)
  waiting for transfers between devices  8.66 us (13%)
  starting transfers between devices  7.2 us (11%)
  between operations  0.76 us (1%)
    pallas_call x11, Pallas kernels, call(): pl.pallas_call(run, out_shape=list(outs.values()), in_specs=[in_specs or...  24.3 us
    all_to_all x1, blocking collectives, body(): lax.all_to_all(b2['payload'], FLOW, split_axis=0, concat_axis=0, tiled=True)  23.5 us
    ppermute x2, waiting for transfers between devices, across(): return lax.ppermute(x, FLOW, pairs + [(b, a) for a, b in pairs])  8.65 us
    ppermute x2, starting transfers between devices, across(): return lax.ppermute(x, FLOW, pairs + [(b, a) for a, b in pairs])  5.56 us
    ppermute x3, starting transfers between devices, within(): return lax.ppermute(x, FLOW, [(i, i ^ 1) for i in range(128)])  1.64 us
  transfers between devices with their start and end apart: 5, of which 1 were waited for; matrix products, arithmetic and copies ran while one was open for 0% of the time, Pallas kernels for 14%

profile of v2, /device:TPU:1, one launch (start us, length us, event | category | flops | bytes accessed | tf_op | source)
XLA Modules:
  0.0 64.4 jit_solution(9818137128981748893)
XLA Ops:
  0.6 2.5 %load.1 = (f32[12,12,8,128]{3,2,1,0:T(8,128)S(1)}, f32[12,12,8,128]{3,2,1,0:T(8,128)S(1)}, f32[11,12,8,128]{3,2,1,0:T(8,128)S(1)}, f32[1,12,8,128]{3,2,1,0:T(8,1...) custom-call(f32[24,3,64,128]{3,2,1,0:T(8,128)} %bitcast.51, ...), custom_call_target="tpu_custom_call" | custom-call | tf_op jit(solution)/shard_map/load/pallas_call | solution.py:670
  3.2 2.3 %ahead.1 = (f32[24,4,8,128]{3,2,1,0:T(8,128)S(1)}, f32[24,4,8,128]{3,2,1,0:T(8,128)S(1)}, f32[48,4,8,128]{3,2,1,0:T(8,128)S(1)}) custom-call(f32[24,12,8,128]{3,2,1,0:T(8,128)S(1)} %get-tuple-element.53.refs_0_.refs_1_.refs_6_.refs_2_, f32[1,12,8,128]{3,2,1,0:T(8,128)S(1)} %get-tuple-element.54.refs_1_.refs_3_.refs_5_, ...), custom_call_target="tpu_custom_call" | custom-call | tf_op jit(solution)/shard_map/ahead/pallas_call | solution.py:670
  5.5 1.6 %rest.1 = (f32[12,12,8,128]{3,2,1,0:T(8,128)S(1)}, f32[12,12,8,128]{3,2,1,0:T(8,128)S(1)}, f32[11,12,8,128]{3,2,1,0:T(8,128)S(1)}, f32[1,12,8,128]{3,2,1,0:T(8,1...) custom-call(f32[24,3,64,128]{3,2,1,0:T(8,128)S(1)} %get-tuple-element.59.refs, ...), custom_call_target="tpu_custom_call" | custom-call | tf_op jit(solution)/shard_map/rest/pallas_call | solution.py:670
  7.1 1.5 %collective-permute-start.2 = (f32[24,4,8,128]{3,2,1,0:T(8,128)S(1)}, f32[24,4,8,128]{3,2,1,0:T(8,128)S(1)}, u32[]{:S(2)}, u32[]{:S(2)}) collective-permute-start(f32[24,4,8,128]{3,2,1,0:T(8,128)S(1)} %get-tuple-element.66), channel_id=1, source_target_pairs={{0,1},{1,0},{2,3},{3,2},{4,5},{5,4},{6,7},{7,6},{8,9},{9,8},{10,11... | collective-permute-start | bytes 1179656 | tf_op jit(solution)/shard_map/ppermute | solution.py:683
  8.5 2.6 %inner1.1 = (f32[24,4,8,128]{3,2,1,0:T(8,128)S(1)}, f32[24,12,8,128]{3,2,1,0:T(8,128)S(1)}) custom-call(f32[24,12,8,128]{3,2,1,0:T(8,128)S(1)} %get-tuple-element.67.refs_0_.refs_1_, f32[24,12,8,128]{3,2,1,0:T(8,128)S(1)} %get-tuple-element.53.refs_0_.refs_1_.refs_6_.refs_2_, f32[1,12,8,128]{3,2,1,0:T(8,128)S(1)} %get-tuple-element.68.refs_2_.refs_9_.refs_1_.refs_4_, ...), custom_call_target="tpu_custom_call" | custom-call | tf_op jit(solution)/shard_map/inner1/pallas_call | solution.py:670
  11.1 0.0 collective-permute-done.2.refs_0_
  11.1 0.6 edge1.1
  11.8 0.1 collective-permute-start.3
  11.9 3.6 %collective-permute-start.1 = (f32[48,4,8,128]{3,2,1,0:T(8,128)S(1)}, f32[48,4,8,128]{3,2,1,0:T(8,128)S(1)}, u32[]{:S(2)}, u32[]{:S(2)}) collective-permute-start(f32[48,4,8,128]{3,2,1,0:T(8,128)S(1)} %get-tuple-element.58.refs_7_.refs_3_), channel_id=1, source_target_pairs={{1,2},{3,4},{5,6},{7,8},{9,10},{11,12},{13,14},{15,16},{17,18},{19... | collective-permute-start | bytes 2359304 | tf_op jit(solution)/shard_map/ppermute | solution.py:688
  15.5 2.0 %collective-permute-start = (f32[38,4,8,128]{3,2,1,0:T(8,128)S(1)}, f32[38,4,8,128]{3,2,1,0:T(8,128)S(1)}, u32[]{:S(2)}, u32[]{:S(2)}) collective-permute-start(f32[38,4,8,128]{3,2,1,0:T(8,128)S(1)} %get-tuple-element.52), channel_id=1, source_target_pairs={{1,2},{3,4},{5,6},{7,8},{9,10},{11,12},{13,14},{15,16},{17,18},{19... | collective-permute-start | bytes 1867784 | tf_op jit(solution)/shard_map/ppermute | solution.py:688
  17.4 2.6 %inner2.1 = (f32[24,4,8,128]{3,2,1,0:T(8,128)S(1)}, f32[24,12,8,128]{3,2,1,0:T(8,128)S(1)}, f32[10,8,128]{2,1,0:T(8,128)S(1)}) custom-call(f32[24,16,8,128]{3,2,1,0:T(8,128)S(1)} %get-tuple-element.75.refs_0_.refs_14_.refs_3_, f32[24,4,8,128]{3,2,1,0:T(8,128)S(1)} %get-tuple-element.76.refs_1_.refs_15_.refs_4_, ...), custom_call_target="tpu_custom_call" | custom-call | tf_op jit(solution)/shard_map/inner2/pallas_call | solution.py:670
  20.0 0.0 collective-permute-done.3.refs_0_
  20.0 0.6 edge2.1
  20.7 0.1 collective-permute-start.4
  20.8 2.4 %inner3.1 = (f32[24,4,8,128]{3,2,1,0:T(8,128)S(1)}, f32[24,8,8,128]{3,2,1,0:T(8,128)S(1)}, f32[10,8,128]{2,1,0:T(8,128)S(1)}) custom-call(f32[24,16,8,128]{3,2,1,0:T(8,128)S(1)} %get-tuple-element.83.refs_0_.refs_17_.refs_6_, f32[1,12,8,128]{3,2,1,0:T(8,128)S(1)} %get-tuple-element.68.refs_2_.refs_9_.refs_1_.refs_4_, ...), custom_call_target="tpu_custom_call" | custom-call | tf_op jit(solution)/shard_map/inner3/pallas_call | solution.py:670
  23.2 8.7 %collective-permute-done.refs_2_.refs_0_ = f32[38,4,8,128]{3,2,1,0:T(8,128)S(1)} collective-permute-done((f32[38,4,8,128]{3,2,1,0:T(8,128)S(1)}, f32[38,4,8,128]{3,2,1,0:T(8,128)S(1)}, u32[]{:S(2)}, u32[]{:S(2)}) %collective-permute-start) | collective-permute-done | bytes 622624 | tf_op jit(solution)/shard_map/ppermute | solution.py:688
  31.8 0.0 collective-permute-done.4.refs_0_
  31.8 0.7 %beyond.1 = (f32[12,4,8,128]{3,2,1,0:T(8,128)S(1)}, f32[12,4,8,128]{3,2,1,0:T(8,128)S(1)}, f32[11,4,8,128]{3,2,1,0:T(8,128)S(1)}, f32[24,4,8,128]{3,2,1,0:T(8,12...) custom-call(f32[24,4,8,128]{3,2,1,0:T(8,128)S(1)} %collective-permute-done.4.refs_0_, ...), custom_call_target="tpu_custom_call" | custom-call | tf_op jit(solution)/shard_map/beyond/pallas_call | solution.py:670
  32.5 0.0 collective-permute-done.1.refs_1_
  32.5 5.8 %band.1 = (f32[24,8,8,128]{3,2,1,0:T(8,128)S(1)}, f32[24,12,8,128]{3,2,1,0:T(8,128)S(1)}, f32[24,12,8,128]{3,2,1,0:T(8,128)S(1)}, f32[24,12,8,128]{3,2,1,0:T(8,128)S(1)}, f32[128,128]{1,0:T(8,128)S(1)}) custom-call(f32[38,4,8,128]{3,2,1,0:T(8,128)S(1)} %collective-permute-done.refs_2_.refs_0_, f32[48,4,8,128]{3,2,1,0:T(8,128)S(1)} %collective-permute-done.1.refs_1_, ...), custom_call_target="tpu_custom_call" | custom-call | tf_op jit(solution)/shard_map/band/pallas_call | solution.py:670
  38.3 23.5 %all_to_all.11 = f32[128,1,128]{2,1,0:T(1,128)S(1)} all-to-all(f32[128,1,128]{2,1,0:T(1,128)S(1)} %bitcast.50), channel_id=1, replica_groups=mesh['flow_0'=4,'flow_1'=4,'flow_2'=4,'flow_3'=2] {'flow_0','flow_1','fl..., dimensions={0} | all-to-all | bytes 131072 | tf_op jit(solution)/shard_map/all_to_all | solution.py:829
  61.8 2.6 %combine.1 = (f32[24,3,64,128]{3,2,1,0:T(8,128)}, f32[24,3,64,128]{3,2,1,0:T(8,128)}) custom-call(f32[128,128]{1,0:T(8,128)S(1)} %bitcast.49, f32[24,12,8,128]{3,2,1,0:T(8,128)S(1)} %get-tuple-element.67.refs_0_.refs_1_, f32[24,12,8,128]{3,2,1,0:T(8,128)S(1)} %get-tuple-element.53.refs_0_.refs_1_.refs_6_.refs_2_, ...), custom_call_target="tpu_custom_call" | custom-call | tf_op jit(solution)/shard_map/combine/pallas_call | solution.py:670
Async XLA Ops:
  7.1 4.0 %collective-permute-start.2 = (f32[24,4,8,128]{3,2,1,0:T(8,128)S(1)}, f32[24,4,8,128]{3,2,1,0:T(8,128)S(1)}, u32[]{:S(2)}, u32[]{:S(2)}) collective-permute-start(f32[24,4,8,128]{3,2,1,0:T(8,128)S(1)} %get-tuple-element.66), channel_id=1, source_target_pairs={{0,1},{1,0},{2,3},{3,2},{4,5},{5,4},{6,7},{7,6},{8,9},{9,8},{10,11... | collective-permute-start | bytes 1179656 | tf_op jit(solution)/shard_map/ppermute | solution.py:683
  11.8 8.3 %collective-permute-start.3 = (f32[24,4,8,128]{3,2,1,0:T(8,128)S(1)}, f32[24,4,8,128]{3,2,1,0:T(8,128)S(1)}, u32[]{:S(2)}, u32[]{:S(2)}) collective-permute-start(f32[24,4,8,128]{3,2,1,0:T(8,128)S(1)} %get-tuple-element.74), channel_id=1, source_target_pairs={{0,1},{1,0},{2,3},{3,2},{4,5},{5,4},{6,7},{7,6},{8,9},{9,8},{10,11... | collective-permute-start | bytes 1179656 | tf_op jit(solution)/shard_map/ppermute | solution.py:683
  11.9 20.6 %collective-permute-start.1 = (f32[48,4,8,128]{3,2,1,0:T(8,128)S(1)}, f32[48,4,8,128]{3,2,1,0:T(8,128)S(1)}, u32[]{:S(2)}, u32[]{:S(2)}) collective-permute-start(f32[48,4,8,128]{3,2,1,0:T(8,128)S(1)} %get-tuple-element.58.refs_7_.refs_3_), channel_id=1, source_target_pairs={{1,2},{3,4},{5,6},{7,8},{9,10},{11,12},{13,14},{15,16},{17,18},{19... | collective-permute-start | bytes 2359304 | tf_op jit(solution)/shard_map/ppermute | solution.py:688
  15.5 16.4 %collective-permute-start = (f32[38,4,8,128]{3,2,1,0:T(8,128)S(1)}, f32[38,4,8,128]{3,2,1,0:T(8,128)S(1)}, u32[]{:S(2)}, u32[]{:S(2)}) collective-permute-start(f32[38,4,8,128]{3,2,1,0:T(8,128)S(1)} %get-tuple-element.52), channel_id=1, source_target_pairs={{1,2},{3,4},{5,6},{7,8},{9,10},{11,12},{13,14},{15,16},{17,18},{19... | collective-permute-start | bytes 1867784 | tf_op jit(solution)/shard_map/ppermute | solution.py:688
  20.7 11.2 %collective-permute-start.4 = (f32[24,4,8,128]{3,2,1,0:T(8,128)S(1)}, f32[24,4,8,128]{3,2,1,0:T(8,128)S(1)}, u32[]{:S(2)}, u32[]{:S(2)}) collective-permute-start(f32[24,4,8,128]{3,2,1,0:T(8,128)S(1)} %get-tuple-element.82), channel_id=1, source_target_pairs={{0,1},{1,0},{2,3},{3,2},{4,5},{5,4},{6,7},{7,6},{8,9},{9,8},{10,11... | collective-permute-start | bytes 1179656 | tf_op jit(solution)/shard_map/ppermute | solution.py:683

commit v3 on v2

--- a/solution.py
+++ b/solution.py
@@ -514,7 +514,7 @@
 
 def least_squares(columns, start):
     count_cols = len(columns)
-    givens_rhs = [start] + [start * 0.0 for index in range(count_cols)]
+    givens_rhs = [start] + [start * 0.0 for _ in range(count_cols)]
     cosines, sines, upper_cols = ([], [], [])
     for column_index, column_in in enumerate(columns):
         column = list(column_in)
@@ -661,7 +661,7 @@
         self.__dict__.update(zip(names, refs))
 
 
-def call(kernel, name, ins, outs, scratch={}, in_specs=None, out_specs=None, limit=4 << 20):
+def call(kernel, ins, outs, scratch={}, in_specs=None, out_specs=None, limit=4 << 20):
     names = [*ins, *outs, *scratch]
 
     def run(*refs):
@@ -674,7 +674,6 @@
         out_specs=[out_specs or VM] * len(outs),
         scratch_shapes=list(scratch.values()),
         compiler_params=pltpu.CompilerParams(vmem_limit_bytes=limit),
-        name=name,
     )(*ins.values())
     return dict(zip(outs, results))
 
@@ -705,7 +704,6 @@
     edge = vmem(PLANES, REACH)
     k0 = call(
         load_kernel,
-        "load",
         ins,
         {
             **factors(HALF),
@@ -720,14 +718,12 @@
     p1 = across(k0["p1"])
     ahead = call(
         ahead_kernel,
-        "ahead",
         pick(k0, "", "s0", "nuh", "er", "ei", "link"),
         {"u1": edge, "s1": edge, "p2": vmem(2 * PLANES, REACH)},
     )
     p2 = across(ahead["p2"])
     k1 = call(
         rest_kernel,
-        "rest",
         {**pick(k0, "", *raws), "order": ahead["p2"]},
         {
             **factors(HALF),
@@ -750,43 +746,29 @@
     ha = within(k1["sa"])
     n1 = call(
         inner1_kernel,
-        "inner1",
         some("s0_a", "s0_b", "nuh_a", "nuh_b"),
         {"nsum": edge, "u1": vmem(PLANES, HALF)},
     )
-    e1 = call(
-        edge_a_kernel,
-        "edge1",
-        {"ha": ha, "nsum": n1["nsum"], "u_in": n1["u1"], **operator},
-        solved,
-    )
+    e1 = call(edge_a_kernel, {"ha": ha, "nsum": n1["nsum"], "u_in": n1["u1"], **operator}, solved)
     ha = within(e1["sa"])
     first = {"u1_e": e1["u_edge"], "u1_i": n1["u1"]}
     middle = {"u1_m": ahead["u1"]}
     s1 = {"s1_a": e1["s"], "s1_m": ahead["s1"]}
     n2 = call(
         inner2_kernel,
-        "inner2",
         {**s1, **some("nuh_a", "nuh_b"), **u0, **first, **middle},
         {"nsum": edge, "u2": vmem(PLANES, HALF), "sums": vmem(10)},
     )
-    e2 = call(
-        edge_a_kernel,
-        "edge2",
-        {"ha": ha, "nsum": n2["nsum"], "u_in": n2["u2"], **operator},
-        solved,
-    )
+    e2 = call(edge_a_kernel, {"ha": ha, "nsum": n2["nsum"], "u_in": n2["u2"], **operator}, solved)
     ha = within(e2["sa"])
     second = {"u2_e": e2["u_edge"], "u2_i": n2["u2"]}
     n3 = call(
         inner3_kernel,
-        "inner3",
         {"s2": e2["s"], **some("nuh_a"), **u0, **first, **second},
         {"nsum": edge, "u3": vmem(PLANES, 8), "sums": vmem(10)},
     )
     b1 = call(
         beyond_kernel,
-        "beyond",
         {
             "ha": ha,
             "nsum": n3["nsum"],
@@ -801,7 +783,6 @@
     )
     b2 = call(
         band_kernel,
-        "band",
         {
             "p1": p1,
             "p2": p2,
@@ -830,7 +811,6 @@
     shape = (PLANES, ROWS // 8, 64, 128)
     outs = call(
         final_kernel,
-        "combine",
         {
             "gathered": gathered,
             **some("s0_a", "s0_b"),
@@ -863,6 +843,7 @@
 
 def solution(mesh):
     finer = Mesh(mesh.devices.reshape(4, 4, 4, 2), FLOW)
+
     return jax.shard_map(
         body,
         mesh=finer,

time: 64.6 us -> 64.6 us (level)
  no operation moved by 1% of the time
where the time goes in v3:
time: 64.6 us; the launch traced here: 64.4 us
  Pallas kernels  24.3 us (38%)
  blocking collectives  23.5 us (36%)
  waiting for transfers between devices  8.66 us (13%)
  starting transfers between devices  7.2 us (11%)
  between operations  0.76 us (1%)
    pallas_call x11, Pallas kernels, call(): pl.pallas_call(run, out_shape=list(outs.values()), in_specs=[in_specs or...  24.3 us
    all_to_all x1, blocking collectives, body(): lax.all_to_all(b2['payload'], FLOW, split_axis=0, concat_axis=0, tiled=True)  23.5 us
    ppermute x2, waiting for transfers between devices, across(): return lax.ppermute(x, FLOW, pairs + [(b, a) for a, b in pairs])  8.65 us
    ppermute x2, starting transfers between devices, across(): return lax.ppermute(x, FLOW, pairs + [(b, a) for a, b in pairs])  5.56 us
    ppermute x3, starting transfers between devices, within(): return lax.ppermute(x, FLOW, [(i, i ^ 1) for i in range(128)])  1.64 us
  transfers between devices with their start and end apart: 5, of which 1 were waited for; matrix products, arithmetic and copies ran while one was open for 0% of the time, Pallas kernels for 14%

profile of v3, /device:TPU:1, one launch (start us, length us, event | category | flops | bytes accessed | tf_op | source)
XLA Modules:
  0.0 64.4 jit_solution(9818137128981748893)
XLA Ops:
  0.6 2.5 %shard_map.86 = (f32[12,12,8,128]{3,2,1,0:T(8,128)S(1)}, f32[12,12,8,128]{3,2,1,0:T(8,128)S(1)}, f32[11,12,8,128]{3,2,1,0:T(8,128)S(1)}, f32[1,12,8,128]{3,2,1,0...) custom-call(f32[24,3,64,128]{3,2,1,0:T(8,128)} %bitcast.51, ...), custom_call_target="tpu_custom_call" | custom-call | tf_op jit(solution)/shard_map/pallas_call | solution.py:670
  3.2 2.3 %shard_map.87 = (f32[24,4,8,128]{3,2,1,0:T(8,128)S(1)}, f32[24,4,8,128]{3,2,1,0:T(8,128)S(1)}, f32[48,4,8,128]{3,2,1,0:T(8,128)S(1)}) custom-call(f32[24,12,8,128]{3,2,1,0:T(8,128)S(1)} %get-tuple-element.53.refs_0_.refs_1_.refs_6_.refs_2_, f32[1,12,8,128]{3,2,1,0:T(8,128)S(1)} %get-tuple-element.54.refs_1_.refs_3_.refs_5_, ...), custom_call_target="tpu_custom_call" | custom-call | tf_op jit(solution)/shard_map/pallas_call | solution.py:670
  5.5 1.6 %shard_map.88 = (f32[12,12,8,128]{3,2,1,0:T(8,128)S(1)}, f32[12,12,8,128]{3,2,1,0:T(8,128)S(1)}, f32[11,12,8,128]{3,2,1,0:T(8,128)S(1)}, f32[1,12,8,128]{3,2,1,0...) custom-call(f32[24,3,64,128]{3,2,1,0:T(8,128)S(1)} %get-tuple-element.5, ...), custom_call_target="tpu_custom_call" | custom-call | tf_op jit(solution)/shard_map/pallas_call | solution.py:670
  7.1 1.5 %collective-permute-start.2 = (f32[24,4,8,128]{3,2,1,0:T(8,128)S(1)}, f32[24,4,8,128]{3,2,1,0:T(8,128)S(1)}, u32[]{:S(2)}, u32[]{:S(2)}) collective-permute-start(f32[24,4,8,128]{3,2,1,0:T(8,128)S(1)} %get-tuple-element.66), channel_id=1, source_target_pairs={{0,1},{1,0},{2,3},{3,2},{4,5},{5,4},{6,7},{7,6},{8,9},{9,8},{10,11... | collective-permute-start | bytes 1179656 | tf_op jit(solution)/shard_map/ppermute | solution.py:682
  8.5 2.6 %shard_map.89 = (f32[24,4,8,128]{3,2,1,0:T(8,128)S(1)}, f32[24,12,8,128]{3,2,1,0:T(8,128)S(1)}) custom-call(f32[24,12,8,128]{3,2,1,0:T(8,128)S(1)} %get-tuple-element.67.refs_0_.refs_1_, f32[24,12,8,128]{3,2,1,0:T(8,128)S(1)} %get-tuple-element.53.refs_0_.refs_1_.refs_6_.refs_2_, f32[1,12,8,128]{3,2,1,0:T(8,128)S(1)} %get-tuple-element.68.refs_2_.refs_9_.refs_1_.refs_4_, ...), custom_call_target="tpu_custom_call" | custom-call | tf_op jit(solution)/shard_map/pallas_call | solution.py:670
  11.1 0.0 collective-permute-done.2.refs_0_
  11.1 0.6 shard_map.90
  11.8 0.1 collective-permute-start.3
  11.9 3.6 %collective-permute-start.1 = (f32[48,4,8,128]{3,2,1,0:T(8,128)S(1)}, f32[48,4,8,128]{3,2,1,0:T(8,128)S(1)}, u32[]{:S(2)}, u32[]{:S(2)}) collective-permute-start(f32[48,4,8,128]{3,2,1,0:T(8,128)S(1)} %get-tuple-element.58.refs_7_.refs_3_), channel_id=1, source_target_pairs={{1,2},{3,4},{5,6},{7,8},{9,10},{11,12},{13,14},{15,16},{17,18},{19... | collective-permute-start | bytes 2359304 | tf_op jit(solution)/shard_map/ppermute | solution.py:687
  15.5 2.0 %collective-permute-start = (f32[38,4,8,128]{3,2,1,0:T(8,128)S(1)}, f32[38,4,8,128]{3,2,1,0:T(8,128)S(1)}, u32[]{:S(2)}, u32[]{:S(2)}) collective-permute-start(f32[38,4,8,128]{3,2,1,0:T(8,128)S(1)} %get-tuple-element.52), channel_id=1, source_target_pairs={{1,2},{3,4},{5,6},{7,8},{9,10},{11,12},{13,14},{15,16},{17,18},{19... | collective-permute-start | bytes 1867784 | tf_op jit(solution)/shard_map/ppermute | solution.py:687
  17.4 2.6 %shard_map.91 = (f32[24,4,8,128]{3,2,1,0:T(8,128)S(1)}, f32[24,12,8,128]{3,2,1,0:T(8,128)S(1)}, f32[10,8,128]{2,1,0:T(8,128)S(1)}) custom-call(f32[24,16,8,128]{3,2,1,0:T(8,128)S(1)} %get-tuple-element.75.refs_0_.refs_14_.refs_3_, f32[24,4,8,128]{3,2,1,0:T(8,128)S(1)} %get-tuple-element.76.refs_1_.refs_15_.refs_4_, ...), custom_call_target="tpu_custom_call" | custom-call | tf_op jit(solution)/shard_map/pallas_call | solution.py:670
  20.0 0.0 collective-permute-done.3.refs_0_
  20.0 0.6 shard_map.92
  20.7 0.1 collective-permute-start.4
  20.8 2.4 %shard_map.93 = (f32[24,4,8,128]{3,2,1,0:T(8,128)S(1)}, f32[24,8,8,128]{3,2,1,0:T(8,128)S(1)}, f32[10,8,128]{2,1,0:T(8,128)S(1)}) custom-call(f32[24,16,8,128]{3,2,1,0:T(8,128)S(1)} %get-tuple-element.83.refs_0_.refs_17_.refs_6_, f32[1,12,8,128]{3,2,1,0:T(8,128)S(1)} %get-tuple-element.68.refs_2_.refs_9_.refs_1_.refs_4_, ...), custom_call_target="tpu_custom_call" | custom-call | tf_op jit(solution)/shard_map/pallas_call | solution.py:670
  23.2 8.7 %collective-permute-done.refs_2_.refs_0_ = f32[38,4,8,128]{3,2,1,0:T(8,128)S(1)} collective-permute-done((f32[38,4,8,128]{3,2,1,0:T(8,128)S(1)}, f32[38,4,8,128]{3,2,1,0:T(8,128)S(1)}, u32[]{:S(2)}, u32[]{:S(2)}) %collective-permute-start) | collective-permute-done | bytes 622624 | tf_op jit(solution)/shard_map/ppermute | solution.py:687
  31.8 0.0 collective-permute-done.4.refs_0_
  31.8 0.7 %shard_map.94 = (f32[12,4,8,128]{3,2,1,0:T(8,128)S(1)}, f32[12,4,8,128]{3,2,1,0:T(8,128)S(1)}, f32[11,4,8,128]{3,2,1,0:T(8,128)S(1)}, f32[24,4,8,128]{3,2,1,0:T(...) custom-call(f32[24,4,8,128]{3,2,1,0:T(8,128)S(1)} %collective-permute-done.4.refs_0_, ...), custom_call_target="tpu_custom_call" | custom-call | tf_op jit(solution)/shard_map/pallas_call | solution.py:670
  32.5 0.0 collective-permute-done.1.refs_1_
  32.5 5.8 %shard_map.95 = (f32[24,8,8,128]{3,2,1,0:T(8,128)S(1)}, f32[24,12,8,128]{3,2,1,0:T(8,128)S(1)}, f32[24,12,8,128]{3,2,1,0:T(8,128)S(1)}, f32[24,12,8,128]{3,2,1,0:T(8,128)S(1)}, f32[128,128]{1,0:T(8,128)S(1)}) custom-call(f32[38,4,8,128]{3,2,1,0:T(8,128)S(1)} %collective-permute-done.refs_2_.refs_0_, f32[48,4,8,128]{3,2,1,0:T(8,128)S(1)} %collective-permute-done.1.refs_1_, ...), custom_call_target="tpu_custom_call" | custom-call | tf_op jit(solution)/shard_map/pallas_call | solution.py:670
  38.3 23.5 %all_to_all.11 = f32[128,1,128]{2,1,0:T(1,128)S(1)} all-to-all(f32[128,1,128]{2,1,0:T(1,128)S(1)} %bitcast.50), channel_id=1, replica_groups=mesh['flow_0'=4,'flow_1'=4,'flow_2'=4,'flow_3'=2] {'flow_0','flow_1','fl..., dimensions={0} | all-to-all | bytes 131072 | tf_op jit(solution)/shard_map/all_to_all | solution.py:810
  61.8 2.6 %shard_map.96 = (f32[24,3,64,128]{3,2,1,0:T(8,128)}, f32[24,3,64,128]{3,2,1,0:T(8,128)}) custom-call(f32[128,128]{1,0:T(8,128)S(1)} %bitcast.49, f32[24,12,8,128]{3,2,1,0:T(8,128)S(1)} %get-tuple-element.67.refs_0_.refs_1_, f32[24,12,8,128]{3,2,1,0:T(8,128)S(1)} %get-tuple-element.53.refs_0_.refs_1_.refs_6_.refs_2_, ...), custom_call_target="tpu_custom_call" | custom-call | tf_op jit(solution)/shard_map/pallas_call | solution.py:670
Async XLA Ops:
  7.1 4.0 %collective-permute-start.2 = (f32[24,4,8,128]{3,2,1,0:T(8,128)S(1)}, f32[24,4,8,128]{3,2,1,0:T(8,128)S(1)}, u32[]{:S(2)}, u32[]{:S(2)}) collective-permute-start(f32[24,4,8,128]{3,2,1,0:T(8,128)S(1)} %get-tuple-element.66), channel_id=1, source_target_pairs={{0,1},{1,0},{2,3},{3,2},{4,5},{5,4},{6,7},{7,6},{8,9},{9,8},{10,11... | collective-permute-start | bytes 1179656 | tf_op jit(solution)/shard_map/ppermute | solution.py:682
  11.8 8.3 %collective-permute-start.3 = (f32[24,4,8,128]{3,2,1,0:T(8,128)S(1)}, f32[24,4,8,128]{3,2,1,0:T(8,128)S(1)}, u32[]{:S(2)}, u32[]{:S(2)}) collective-permute-start(f32[24,4,8,128]{3,2,1,0:T(8,128)S(1)} %get-tuple-element.74), channel_id=1, source_target_pairs={{0,1},{1,0},{2,3},{3,2},{4,5},{5,4},{6,7},{7,6},{8,9},{9,8},{10,11... | collective-permute-start | bytes 1179656 | tf_op jit(solution)/shard_map/ppermute | solution.py:682
  11.9 20.6 %collective-permute-start.1 = (f32[48,4,8,128]{3,2,1,0:T(8,128)S(1)}, f32[48,4,8,128]{3,2,1,0:T(8,128)S(1)}, u32[]{:S(2)}, u32[]{:S(2)}) collective-permute-start(f32[48,4,8,128]{3,2,1,0:T(8,128)S(1)} %get-tuple-element.58.refs_7_.refs_3_), channel_id=1, source_target_pairs={{1,2},{3,4},{5,6},{7,8},{9,10},{11,12},{13,14},{15,16},{17,18},{19... | collective-permute-start | bytes 2359304 | tf_op jit(solution)/shard_map/ppermute | solution.py:687
  15.5 16.4 %collective-permute-start = (f32[38,4,8,128]{3,2,1,0:T(8,128)S(1)}, f32[38,4,8,128]{3,2,1,0:T(8,128)S(1)}, u32[]{:S(2)}, u32[]{:S(2)}) collective-permute-start(f32[38,4,8,128]{3,2,1,0:T(8,128)S(1)} %get-tuple-element.52), channel_id=1, source_target_pairs={{1,2},{3,4},{5,6},{7,8},{9,10},{11,12},{13,14},{15,16},{17,18},{19... | collective-permute-start | bytes 1867784 | tf_op jit(solution)/shard_map/ppermute | solution.py:687
  20.7 11.2 %collective-permute-start.4 = (f32[24,4,8,128]{3,2,1,0:T(8,128)S(1)}, f32[24,4,8,128]{3,2,1,0:T(8,128)S(1)}, u32[]{:S(2)}, u32[]{:S(2)}) collective-permute-start(f32[24,4,8,128]{3,2,1,0:T(8,128)S(1)} %get-tuple-element.82), channel_id=1, source_target_pairs={{0,1},{1,0},{2,3},{3,2},{4,5},{5,4},{6,7},{7,6},{8,9},{9,8},{10,11... | collective-permute-start | bytes 1179656 | tf_op jit(solution)/shard_map/ppermute | solution.py:682

commit v4 on v3

--- a/solution.py
+++ b/solution.py
@@ -19,6 +19,8 @@
 ROWS = 24
 REACH = 4
 HALF = 12
+GROUP = 4
+COEFS = 2 * PLANES
 F32 = jnp.float32
 TILE = (8, 128)
 GRAM = [(a, b) for b in range(4) for a in range(b + 1)]
@@ -178,20 +180,30 @@
     return total
 
 
-def loop_sums(pairs, step):
+def over_planes(step, together=GROUP):
+    def run(group, carry):
+        for i in range(together):
+            step(group * together + i)
+        return carry
+
+    lax.fori_loop(0, PLANES // together, run, 0)
+
+
+def loop_sums(pairs, step, together=GROUP):
     pairs = list(pairs)
 
-    def run(plane, carry):
+    def run(group, carry):
         sums = dict(zip(pairs, carry))
 
         def add(pair, value):
             sums[pair] = sums[pair] + value
 
-        step(plane, add)
+        for i in range(together):
+            step(group * together + i, add)
         return tuple(sums[pair] for pair in pairs)
 
     zero = jnp.zeros(TILE, F32)
-    return dict(zip(pairs, lax.fori_loop(0, PLANES, run, (zero,) * len(pairs))))
+    return dict(zip(pairs, lax.fori_loop(0, PLANES // together, run, (zero,) * len(pairs))))
 
 
 def with_all(add, b, value, plane, t, us):
@@ -245,7 +257,7 @@
     for copy in small + v_copy[:2]:
         copy.wait()
     er, ei, link, nu = (Field(part(x, HALF, ROWS)) for x in (r.er, r.ei, r.link, r.nuh))
-    packed = Field(mirrored(r.p1, 0, REACH))
+    packed = Field(mirrored(r.p1, 0, REACH), mirrored(r.p1, REACH, 2 * REACH, PLANES))
     for start in (12, 18):
         ts = span(start, start + 6)
         read = raw_reader(r, core, ts)
@@ -254,17 +266,17 @@
         for i, t in enumerate(ts):
             if t >= ROWS - REACH:
                 for k in range(L - 1):
-                    packed.put(PLANES + k, [t], vert(k)[i : i + 1])
-                packed.put(PLANES + L - 1, [t], jnp.where(active, nu_row, 0.0)[i : i + 1])
-                packed.put(PLANES + L, [t], drag[i : i + 1])
-                packed.put(PLANES + L + 1, [t], rot[i : i + 1])
+                    packed.put(COEFS + k, [t], vert(k)[i : i + 1])
+                packed.put(COEFS + L - 1, [t], jnp.where(active, nu_row, 0.0)[i : i + 1])
+                packed.put(COEFS + L, [t], drag[i : i + 1])
+                packed.put(COEFS + L + 1, [t], rot[i : i + 1])
     for copy in f_copy[:2]:
         copy.wait()
     source = raw_source(r.fraw, core)
     s0 = Field(part(r.s0, HALF, ROWS))
     for start in (12, 18):
         ts = span(start, start + 6)
-        solve(ts, source, er, ei, link, s0, (packed, span(ROWS - REACH, ROWS)))
+        solve(ts, source, er, ei, link, s0, (packed, span(ROWS - 2 * REACH, ROWS)))
     v_copy[2].wait()
     f_copy[2].wait()
 
@@ -273,22 +285,17 @@
     masks = cross_masks()
     s0 = Field(part(r.s0, HALF, ROWS))
     nu = Field(part(r.nuh, HALF, ROWS))
-    sums = Field(mirrored(r.p2, 0, REACH))
     known = span(HALF, ROWS)
     u1 = Field(part(r.u1, 16, 20))
 
-    def step(plane, carry):
+    def step(plane):
         s = {t: s0.row(plane, t) for t in known}
-        for t, total in stencil(span(16, 24), known, s, masks):
-            if t < 20:
-                u1.put(plane, [t], (nu.row(0, t) * total)[None])
-            else:
-                sums.put(plane, [t], total[None])
-        return carry
-
-    lax.fori_loop(0, PLANES, step, 0)
+        for t, total in stencil(span(16, 20), known, s, masks):
+            u1.put(plane, [t], (nu.row(0, t) * total)[None])
+
+    over_planes(step, 8)
     er, ei, link = (Field(part(x, HALF, ROWS)) for x in (r.er, r.ei, r.link))
-    packed = Field(mirrored(r.p2, REACH, 2 * REACH, PLANES))
+    packed = Field(mirrored(r.p2, REACH, 2 * REACH))
     solve(span(16, 20), u1.get, er, ei, link, Field(part(r.s1, 16, 20)), (packed, span(16, 20)))
 
 
@@ -300,12 +307,11 @@
         factor(ts, raw_reader(r, core, ts), er, ei, link, nu)
     places = [place_of(core, t) for t in range(ROWS)]
 
-    def spread(plane, carry):
+    def spread(plane):
         for t in range(ROWS):
             r.u0[plane, t] = raw_row(r.fraw, plane, places[t])
-        return carry
-
-    lax.fori_loop(0, PLANES, spread, 0)
+
+    over_planes(spread, 2)
     u0 = Field(part(r.u0, 0, ROWS))
     s0 = Field(part(r.s0, 0, HALF))
     for start in (0, 6):
@@ -321,16 +327,15 @@
     s0, nu = both_halves(r, "s0"), both_halves(r, "nuh")
     known = span(0, 20)
 
-    def step(plane, carry):
+    def step(plane):
         s = {t: s0.row(plane, t) for t in known}
         for t, total in stencil(span(0, 16), known, s, masks):
             if t < REACH:
                 r.nsum[plane, t] = total
             else:
                 r.u1[plane, t - REACH] = nu.row(0, t) * total
-        return carry
-
-    lax.fori_loop(0, PLANES, step, 0)
+
+    over_planes(step)
 
 
 def edge_a_kernel(r):
@@ -412,66 +417,56 @@
     write_sums(r.sums, loop_sums(pairs_of(2, 3), step))
 
 
-def beyond_kernel(r):
-    nu_a = Field(part(r.nuh_a, 0, HALF))
-    nu_b = Field(part(r.nuh_b, HALF, ROWS))
+def last_a_kernel(r):
+    nu = Field(part(r.nuh_a, 0, HALF))
     u0 = Field(part(r.u0, 0, ROWS))
     u1 = Field(part(r.u1_e, 0, REACH))
     u2 = Field(part(r.u2_e, 0, REACH))
-    ts = span(ROWS, ROWS + REACH)
-    nu = r.p1[PLANES + L - 1]
-    read = (
-        lambda k: r.p1[PLANES + k],
-        nu > 0.0,
-        nu,
-        r.p1[PLANES + L],
-        r.p1[PLANES + L + 1],
-    )
-    er, ei, link = (Field(part(x, ROWS, ROWS + REACH)) for x in (r.er, r.ei, r.link))
-    factor(ts, read, er, ei, link, None)
 
     def step(plane, add):
         for t in range(REACH):
             value = halo_sum(r.nsum[plane, t], t, lambda q: r.ha[plane, q])
-            value = nu_a.row(0, t) * value
+            value = nu.row(0, t) * value
             r.u3[plane, t] = value
             with_all(add, 3, value, plane, t, (u0, u1, u2))
-        for d in range(REACH):
-            t = ROWS - 1 - d
-            value = nu_b.row(0, t) * halo_sum(r.p2s[plane, d], d, lambda q: r.p1[plane, q])
-            r.u1[plane, t - 20] = value
-            with_all(add, 1, value, plane, t, (u0,))
-
-    write_sums(r.sums, loop_sums(pairs_of(1, 3), step))
+
+    write_sums(r.sums, loop_sums(pairs_of(3), step))
 
 
 def band_kernel(r):
     masks = cross_masks()
+    beyond = span(ROWS, ROWS + REACH)
     nu_b = Field(part(r.nuh_b, HALF, ROWS))
-    nu = Field(part(r.nuh_b, HALF, ROWS), part(r.p1, ROWS, ROWS + REACH, PLANES + L - 1))
-    er, ei, link = (
-        Field(part(getattr(r, n + "_b"), HALF, ROWS), part(getattr(r, n + "_h"), ROWS, ROWS + REACH))
-        for n in ("er", "ei", "link")
-    )
-    s0 = Field(part(r.s0_b, HALF, ROWS))
-    u1 = Field(part(r.u1_i, REACH, 16), part(r.u1_m, 16, 20), part(r.u1_b, 20, ROWS))
-
-    def source(plane, ts):
-        rows = []
-        for t in ts:
-            if t < ROWS:
-                rows.append(u1.row(plane, t))
-            else:
-                j = t - ROWS
-                value = halo_sum(r.p2[plane, j], j, lambda q: s0.row(plane, ROWS - 1 - q))
-                rows.append(nu.row(0, t) * value)
-        return jnp.stack(rows)
-
+    nu = Field(part(r.nuh_b, HALF, ROWS), part(r.p1, ROWS, ROWS + REACH, COEFS + L - 1))
+    er_h, ei_h, link_h = (part(x, ROWS, ROWS + REACH) for x in (r.er_h, r.ei_h, r.link_h))
+    nu_h = r.p1[COEFS + L - 1]
+    read = (
+        lambda k: r.p1[COEFS + k],
+        nu_h > 0.0,
+        nu_h,
+        r.p1[COEFS + L],
+        r.p1[COEFS + L + 1],
+    )
+    factor(beyond, read, Field(er_h), Field(ei_h), Field(link_h), None)
+    er = Field(part(r.er_b, HALF, ROWS), er_h)
+    ei = Field(part(r.ei_b, HALF, ROWS), ei_h)
+    link = Field(part(r.link_b, HALF, ROWS), link_h)
+    s0 = Field(
+        part(r.s0_b, HALF, ROWS), part(r.p1, 24, 28), part(r.p1, 28, 32, PLANES)
+    )
+    u1_b = part(r.u1_b, 20, 28)
+    known1 = span(16, 32)
+
+    def first(plane):
+        s = {t: s0.row(plane, t) for t in known1}
+        for t, total in stencil(span(20, 28), known1, s, masks):
+            r.u1_b[plane, t - 20] = nu.row(0, t) * total
+
+    over_planes(first)
     s1_b = part(r.s1, 20, 28)
-    solve(span(20, 28), source, er, ei, link, Field(s1_b))
-    s1 = Field(
-        part(r.s1_a, 0, 16), part(r.s1_m, 16, 20), s1_b, part(r.p2, 28, 32, PLANES)
-    )
+    solve(span(20, 28), Field(u1_b).get, er, ei, link, Field(s1_b))
+    s1 = Field(part(r.s1_a, 0, 16), part(r.s1_m, 16, 20), s1_b, part(r.p2, 28, 32))
+    u1 = Field(part(r.u1_i, REACH, 16), part(r.u1_m, 16, 20), u1_b)
     u0 = Field(part(r.u0, 0, ROWS))
     u2_b = part(r.u2, 16, 28)
     u2 = Field(part(r.u2_i, REACH, 16), u2_b)
@@ -484,8 +479,10 @@
             u2.put(plane, [t], value[None])
             if t < ROWS:
                 with_all(add, 2, value, plane, t, (u0, u1))
-
-    sums = loop_sums(pairs_of(2), step)
+        for t in span(20, ROWS):
+            with_all(add, 1, u1.row(plane, t), plane, t, (u0,))
+
+    sums = loop_sums(pairs_of(1, 2), step)
     s2_b = part(r.s2, 16, 28)
     for start in (16, 22):
         solve(span(start, start + 6), u2.get, er, ei, link, Field(s2_b))
@@ -623,12 +620,12 @@
     s2 = Field(part(r.s2_a, 0, 16), part(r.s2_b, 16, 28))
     u0 = Field(part(r.u0, 0, ROWS))
     u1 = Field(
-        part(r.u1_e, 0, 4), part(r.u1_i, 4, 16), part(r.u1_m, 16, 20), part(r.u1_b, 20, 24)
+        part(r.u1_e, 0, 4), part(r.u1_i, 4, 16), part(r.u1_m, 16, 20), part(r.u1_b, 20, 28)
     )
     u2 = Field(part(r.u2_e, 0, 4), part(r.u2_i, 4, 16), part(r.u2_b, 16, 28))
     u3 = Field(part(r.u3_e, 0, 4), part(r.u3_i, 4, 12), part(r.u3_b, 12, 24))
 
-    def step(plane, carry):
+    def step(plane):
         for t in range(ROWS):
             s = [x.row(plane, t) for x in (s0, s1, s2)]
             u = [x.row(plane, t) for x in (u0, u1, u2, u3)]
@@ -639,9 +636,8 @@
             )
         pltpu.make_async_copy(r.buf_s.at[plane], r.out_s.at[plane], r.sem_s).start()
         pltpu.make_async_copy(r.buf_r.at[plane], r.out_r.at[plane], r.sem_r).start()
-        return carry
-
-    lax.fori_loop(0, PLANES, step, 0)
+
+    over_planes(step, 2)
     pltpu.make_async_copy(r.buf_s, r.out_s, r.sem_s).wait()
     pltpu.make_async_copy(r.buf_r, r.out_r, r.sem_r).wait()
 
@@ -709,7 +705,7 @@
             **factors(HALF),
             "nuh": vmem(1, HALF),
             "s0": vmem(PLANES, HALF),
-            "p1": vmem(PLANES + L + 2, REACH),
+            "p1": vmem(COEFS + L + 2, REACH),
             **raws,
         },
         {"sems": pltpu.SemaphoreType.DMA((11,))},
@@ -719,7 +715,7 @@
     ahead = call(
         ahead_kernel,
         pick(k0, "", "s0", "nuh", "er", "ei", "link"),
-        {"u1": edge, "s1": edge, "p2": vmem(2 * PLANES, REACH)},
+        {"u1": edge, "s1": edge, "p2": edge},
     )
     p2 = across(ahead["p2"])
     k1 = call(
@@ -767,19 +763,17 @@
         {"s2": e2["s"], **some("nuh_a"), **u0, **first, **second},
         {"nsum": edge, "u3": vmem(PLANES, 8), "sums": vmem(10)},
     )
-    b1 = call(
-        beyond_kernel,
+    a3 = call(
+        last_a_kernel,
         {
             "ha": ha,
             "nsum": n3["nsum"],
-            "p1": p1,
-            "p2s": ahead["p2"],
-            **some("nuh_a", "nuh_b"),
+            **some("nuh_a"),
             **u0,
             "u1_e": first["u1_e"],
             "u2_e": second["u2_e"],
         },
-        {**factors(REACH), "u1": edge, "u3": edge, "sums": vmem(10)},
+        {"u3": edge, "sums": vmem(10)},
     )
     b2 = call(
         band_kernel,
@@ -787,25 +781,25 @@
             "p1": p1,
             "p2": p2,
             **some("er_b", "ei_b", "link_b", "nuh_b", "s0_b"),
-            **pick(b1, "_h", "er", "ei", "link"),
             **u0,
             "u1_i": n1["u1"],
             **middle,
-            "u1_b": b1["u1"],
             **s1,
             "u2_i": n2["u2"],
             "s2_a": e2["s"],
             "sums2": n2["sums"],
             "sums3": n3["sums"],
-            "sums4": b1["sums"],
+            "sums4": a3["sums"],
         },
         {
+            "u1_b": vmem(PLANES, 8),
             "s1": vmem(PLANES, 8),
             "u2": vmem(PLANES, HALF),
             "s2": vmem(PLANES, HALF),
             "u3": vmem(PLANES, HALF),
             "payload": jax.ShapeDtypeStruct((128, 128), F32),
         },
+        {"er_h": vmem(L, REACH), "ei_h": vmem(L, REACH), "link_h": vmem(L - 1, REACH)},
     )
     gathered = lax.all_to_all(b2["payload"], FLOW, split_axis=0, concat_axis=0, tiled=True)
     shape = (PLANES, ROWS // 8, 64, 128)
@@ -821,10 +815,10 @@
             **u0,
             **first,
             **middle,
-            "u1_b": b1["u1"],
+            "u1_b": b2["u1_b"],
             **second,
             "u2_b": b2["u2"],
-            "u3_e": b1["u3"],
+            "u3_e": a3["u3"],
             "u3_i": n3["u3"],
             "u3_b": b2["u3"],
         },

time: 64.6 us -> 57.3 us (0.89)
  Pallas kernels: 24.3 us -> 17.2 us
  waiting for transfers between devices: 8.66 us -> 7.37 us
  starting transfers between devices: 7.2 us -> 8.27 us
    pallas_call x11, Pallas kernels: 24.3 us -> 17.2 us  [call(): pl.pallas_call(run, out_shape=list(outs.values()), in_specs=[in_specs or...]
    ppermute x2, waiting for transfers between devices: 8.65 us -> 7.36 us  [across(): return lax.ppermute(x, FLOW, pairs + [(b, a) for a, b in pairs])]
  transfers between devices with their start and end apart: 5 -> 5, of which waited for: 1 -> 1; matrix products, arithmetic and copies ran while one was open for 0% -> 0% of each run, Pallas kernels for 14% -> 10%
where the time goes in v4:
time: 57.3 us; the launch traced here: 57.1 us
  blocking collectives  23.5 us (41%)
  Pallas kernels  17.2 us (30%)
  starting transfers between devices  8.27 us (14%)
  waiting for transfers between devices  7.37 us (13%)
  between operations  0.75 us (1%)
    all_to_all x1, blocking collectives, body(): lax.all_to_all(b2['payload'], FLOW, split_axis=0, concat_axis=0, tiled=True)  23.5 us
    pallas_call x11, Pallas kernels, call(): pl.pallas_call(run, out_shape=list(outs.values()), in_specs=[in_specs or...  17.2 us
    ppermute x2, waiting for transfers between devices, across(): return lax.ppermute(x, FLOW, pairs + [(b, a) for a, b in pairs])  7.36 us
    ppermute x2, starting transfers between devices, across(): return lax.ppermute(x, FLOW, pairs + [(b, a) for a, b in pairs])  6.15 us
    ppermute x3, starting transfers between devices, within(): return lax.ppermute(x, FLOW, [(i, i ^ 1) for i in range(128)])  2.12 us
  transfers between devices with their start and end apart: 5, of which 1 were waited for; matrix products, arithmetic and copies ran while one was open for 0% of the time, Pallas kernels for 10%

profile of v4, /device:TPU:1, one launch (start us, length us, event | category | flops | bytes accessed | tf_op | source)
XLA Modules:
  0.0 57.1 jit_solution(18427821751224338418)
XLA Ops:
  0.6 2.6 %shard_map.86 = (f32[12,12,8,128]{3,2,1,0:T(8,128)S(1)}, f32[12,12,8,128]{3,2,1,0:T(8,128)S(1)}, f32[11,12,8,128]{3,2,1,0:T(8,128)S(1)}, f32[1,12,8,128]{3,2,1,0...) custom-call(f32[24,3,64,128]{3,2,1,0:T(8,128)} %bitcast.51, ...), custom_call_target="tpu_custom_call" | custom-call | tf_op jit(solution)/shard_map/pallas_call | solution.py:666
  3.2 0.6 shard_map.87
  3.8 1.5 %shard_map.88 = (f32[12,12,8,128]{3,2,1,0:T(8,128)S(1)}, f32[12,12,8,128]{3,2,1,0:T(8,128)S(1)}, f32[11,12,8,128]{3,2,1,0:T(8,128)S(1)}, f32[1,12,8,128]{3,2,1,0...) custom-call(f32[24,3,64,128]{3,2,1,0:T(8,128)S(1)} %get-tuple-element.5, ...), custom_call_target="tpu_custom_call" | custom-call | tf_op jit(solution)/shard_map/pallas_call | solution.py:666
  5.3 1.5 %collective-permute-start.2 = (f32[24,4,8,128]{3,2,1,0:T(8,128)S(1)}, f32[24,4,8,128]{3,2,1,0:T(8,128)S(1)}, u32[]{:S(2)}, u32[]{:S(2)}) collective-permute-start(f32[24,4,8,128]{3,2,1,0:T(8,128)S(1)} %get-tuple-element.68), channel_id=1, source_target_pairs={{0,1},{1,0},{2,3},{3,2},{4,5},{5,4},{6,7},{7,6},{8,9},{9,8},{10,11... | collective-permute-start | bytes 1179656 | tf_op jit(solution)/shard_map/ppermute | solution.py:678
  6.7 3.1 %collective-permute-start = (f32[62,4,8,128]{3,2,1,0:T(8,128)S(1)}, f32[62,4,8,128]{3,2,1,0:T(8,128)S(1)}, u32[]{:S(2)}, u32[]{:S(2)}) collective-permute-start(f32[62,4,8,128]{3,2,1,0:T(8,128)S(1)} %get-tuple-element.49), channel_id=1, source_target_pairs={{1,2},{3,4},{5,6},{7,8},{9,10},{11,12},{13,14},{15,16},{17,18},{19... | collective-permute-start | bytes 3047432 | tf_op jit(solution)/shard_map/ppermute | solution.py:683
  9.9 1.3 %shard_map.89 = (f32[24,4,8,128]{3,2,1,0:T(8,128)S(1)}, f32[24,12,8,128]{3,2,1,0:T(8,128)S(1)}) custom-call(f32[24,12,8,128]{3,2,1,0:T(8,128)S(1)} %get-tuple-element.64.refs_0_.refs_1_, f32[24,12,8,128]{3,2,1,0:T(8,128)S(1)} %get-tuple-element.50.refs_0_.refs_1_.refs_6_.refs_2_, f32[1,12,8,128]{3,2,1,0:T(8,128)S(1)} %get-tuple-element.65.refs_2_.refs_9_.refs_1_, ...), custom_call_target="tpu_custom_call" | custom-call | tf_op jit(solution)/shard_map/pallas_call | solution.py:666
  11.2 0.0 collective-permute-done.2.refs_0_
  11.2 0.6 %shard_map.90 = (f32[24,4,8,128]{3,2,1,0:T(8,128)S(1)}, f32[24,16,8,128]{3,2,1,0:T(8,128)S(1)}, f32[24,4,8,128]{3,2,1,0:T(8,128)S(1)}) custom-call(f32[24,4,8,128]{3,2,1,0:T(8,128)S(1)} %collective-permute-done.2.refs_0_, f32[24,4,8,128]{3,2,1,0:T(8,128)S(1)} %get-tuple-element.69.refs_1_, ...), custom_call_target="tpu_custom_call" | custom-call | tf_op jit(solution)/shard_map/pallas_call | solution.py:666
  11.8 0.1 collective-permute-start.3
  11.9 1.7 %shard_map.91 = (f32[24,4,8,128]{3,2,1,0:T(8,128)S(1)}, f32[24,12,8,128]{3,2,1,0:T(8,128)S(1)}, f32[10,8,128]{2,1,0:T(8,128)S(1)}) custom-call(f32[24,16,8,128]{3,2,1,0:T(8,128)S(1)} %get-tuple-element.73.refs_0_.refs_10_.refs_3_, f32[24,4,8,128]{3,2,1,0:T(8,128)S(1)} %get-tuple-element.74.refs_1_.refs_11_.refs_4_, ...), custom_call_target="tpu_custom_call" | custom-call | tf_op jit(solution)/shard_map/pallas_call | solution.py:666
  13.7 0.0 collective-permute-done.3.refs_0_
  13.7 0.6 %shard_map.92 = (f32[24,4,8,128]{3,2,1,0:T(8,128)S(1)}, f32[24,16,8,128]{3,2,1,0:T(8,128)S(1)}, f32[24,4,8,128]{3,2,1,0:T(8,128)S(1)}) custom-call(f32[24,4,8,128]{3,2,1,0:T(8,128)S(1)} %collective-permute-done.3.refs_0_, f32[24,4,8,128]{3,2,1,0:T(8,128)S(1)} %get-tuple-element.78.refs_1_, ...), custom_call_target="tpu_custom_call" | custom-call | tf_op jit(solution)/shard_map/pallas_call | solution.py:666
  14.3 0.6 %collective-permute-start.4 = (f32[24,4,8,128]{3,2,1,0:T(8,128)S(1)}, f32[24,4,8,128]{3,2,1,0:T(8,128)S(1)}, u32[]{:S(2)}, u32[]{:S(2)}) collective-permute-start(f32[24,4,8,128]{3,2,1,0:T(8,128)S(1)} %get-tuple-element.83), channel_id=1, source_target_pairs={{0,1},{1,0},{2,3},{3,2},{4,5},{5,4},{6,7},{7,6},{8,9},{9,8},{10,11... | collective-permute-start | bytes 1179656 | tf_op jit(solution)/shard_map/ppermute | solution.py:678
  14.9 3.0 %collective-permute-start.1 = (f32[24,4,8,128]{3,2,1,0:T(8,128)S(1)}, f32[24,4,8,128]{3,2,1,0:T(8,128)S(1)}, u32[]{:S(2)}, u32[]{:S(2)}) collective-permute-start(f32[24,4,8,128]{3,2,1,0:T(8,128)S(1)} %get-tuple-element.55.refs_7_), channel_id=1, source_target_pairs={{1,2},{3,4},{5,6},{7,8},{9,10},{11,12},{13,14},{15,16},{17,18},{19... | collective-permute-start | bytes 1179656 | tf_op jit(solution)/shard_map/ppermute | solution.py:683
  17.9 1.2 %shard_map.93 = (f32[24,4,8,128]{3,2,1,0:T(8,128)S(1)}, f32[24,8,8,128]{3,2,1,0:T(8,128)S(1)}, f32[10,8,128]{2,1,0:T(8,128)S(1)}) custom-call(f32[24,16,8,128]{3,2,1,0:T(8,128)S(1)} %get-tuple-element.79.refs_0_.refs_13_.refs_6_, f32[1,12,8,128]{3,2,1,0:T(8,128)S(1)} %get-tuple-element.65.refs_2_.refs_9_.refs_1_, ...), custom_call_target="tpu_custom_call" | custom-call | tf_op jit(solution)/shard_map/pallas_call | solution.py:666
  19.1 0.0 collective-permute-done.4.refs_0_
  19.1 0.2 shard_map.94
  19.4 7.4 %collective-permute-done.1.refs_1_ = f32[24,4,8,128]{3,2,1,0:T(8,128)S(1)} collective-permute-done((f32[24,4,8,128]{3,2,1,0:T(8,128)S(1)}, f32[24,4,8,128]{3,2,1,0:T(8,128)S(1)}, u32[]{:S(2)}, u32[]{:S(2)}) %collective-permute-start.1) | collective-permute-done | bytes 393248 | tf_op jit(solution)/shard_map/ppermute | solution.py:683
  26.7 0.0 collective-permute-done.refs_0_
  26.7 4.3 %shard_map.95 = (f32[24,8,8,128]{3,2,1,0:T(8,128)S(1)}, f32[24,8,8,128]{3,2,1,0:T(8,128)S(1)}, f32[24,12,8,128]{3,2,1,0:T(8,128)S(1)}, f32[24,12,8,128]{3,2,1,0:...) custom-call(f32[62,4,8,128]{3,2,1,0:T(8,128)S(1)} %collective-permute-done.refs_0_, ...), custom_call_target="tpu_custom_call" | custom-call | tf_op jit(solution)/shard_map/pallas_call | solution.py:666
  31.0 23.5 %all_to_all.11 = f32[128,1,128]{2,1,0:T(1,128)S(1)} all-to-all(f32[128,1,128]{2,1,0:T(1,128)S(1)} %bitcast.50), channel_id=1, replica_groups=mesh['flow_0'=4,'flow_1'=4,'flow_2'=4,'flow_3'=2] {'flow_0','flow_1','fl..., dimensions={0} | all-to-all | bytes 131072 | tf_op jit(solution)/shard_map/all_to_all | solution.py:804
  54.5 2.6 %shard_map.96 = (f32[24,3,64,128]{3,2,1,0:T(8,128)}, f32[24,3,64,128]{3,2,1,0:T(8,128)}) custom-call(f32[128,128]{1,0:T(8,128)S(1)} %bitcast.49, f32[24,12,8,128]{3,2,1,0:T(8,128)S(1)} %get-tuple-element.64.refs_0_.refs_1_, f32[24,12,8,128]{3,2,1,0:T(8,128)S(1)} %get-tuple-element.50.refs_0_.refs_1_.refs_6_.refs_2_, ...), custom_call_target="tpu_custom_call" | custom-call | tf_op jit(solution)/shard_map/pallas_call | solution.py:666
Async XLA Ops:
  5.3 5.9 %collective-permute-start.2 = (f32[24,4,8,128]{3,2,1,0:T(8,128)S(1)}, f32[24,4,8,128]{3,2,1,0:T(8,128)S(1)}, u32[]{:S(2)}, u32[]{:S(2)}) collective-permute-start(f32[24,4,8,128]{3,2,1,0:T(8,128)S(1)} %get-tuple-element.68), channel_id=1, source_target_pairs={{0,1},{1,0},{2,3},{3,2},{4,5},{5,4},{6,7},{7,6},{8,9},{9,8},{10,11... | collective-permute-start | bytes 1179656 | tf_op jit(solution)/shard_map/ppermute | solution.py:678
  6.7 20.0 %collective-permute-start = (f32[62,4,8,128]{3,2,1,0:T(8,128)S(1)}, f32[62,4,8,128]{3,2,1,0:T(8,128)S(1)}, u32[]{:S(2)}, u32[]{:S(2)}) collective-permute-start(f32[62,4,8,128]{3,2,1,0:T(8,128)S(1)} %get-tuple-element.49), channel_id=1, source_target_pairs={{1,2},{3,4},{5,6},{7,8},{9,10},{11,12},{13,14},{15,16},{17,18},{19... | collective-permute-start | bytes 3047432 | tf_op jit(solution)/shard_map/ppermute | solution.py:683
  11.8 1.8 %collective-permute-start.3 = (f32[24,4,8,128]{3,2,1,0:T(8,128)S(1)}, f32[24,4,8,128]{3,2,1,0:T(8,128)S(1)}, u32[]{:S(2)}, u32[]{:S(2)}) collective-permute-start(f32[24,4,8,128]{3,2,1,0:T(8,128)S(1)} %get-tuple-element.77), channel_id=1, source_target_pairs={{0,1},{1,0},{2,3},{3,2},{4,5},{5,4},{6,7},{7,6},{8,9},{9,8},{10,11... | collective-permute-start | bytes 1179656 | tf_op jit(solution)/shard_map/ppermute | solution.py:678
  14.3 4.8 %collective-permute-start.4 = (f32[24,4,8,128]{3,2,1,0:T(8,128)S(1)}, f32[24,4,8,128]{3,2,1,0:T(8,128)S(1)}, u32[]{:S(2)}, u32[]{:S(2)}) collective-permute-start(f32[24,4,8,128]{3,2,1,0:T(8,128)S(1)} %get-tuple-element.83), channel_id=1, source_target_pairs={{0,1},{1,0},{2,3},{3,2},{4,5},{5,4},{6,7},{7,6},{8,9},{9,8},{10,11... | collective-permute-start | bytes 1179656 | tf_op jit(solution)/shard_map/ppermute | solution.py:678
  14.9 11.8 %collective-permute-start.1 = (f32[24,4,8,128]{3,2,1,0:T(8,128)S(1)}, f32[24,4,8,128]{3,2,1,0:T(8,128)S(1)}, u32[]{:S(2)}, u32[]{:S(2)}) collective-permute-start(f32[24,4,8,128]{3,2,1,0:T(8,128)S(1)} %get-tuple-element.55.refs_7_), channel_id=1, source_target_pairs={{1,2},{3,4},{5,6},{7,8},{9,10},{11,12},{13,14},{15,16},{17,18},{19... | collective-permute-start | bytes 1179656 | tf_op jit(solution)/shard_map/ppermute | solution.py:683

commit v5 on v4

--- a/solution.py
+++ b/solution.py
@@ -10,6 +10,7 @@
 FLOW = ("flow_0", "flow_1", "flow_2", "flow_3")
 CORE = "flow_3"
 epsilon = 1e-06
+TINY = 1e-37
 relaxation = 0.5
 reach_weights = (1.0, 0.6, 0.35, 0.2)
 horiz_total = 2.0 * sum(reach_weights) + 2.0
@@ -19,6 +20,7 @@
 ROWS = 24
 REACH = 4
 HALF = 12
+BAND = 16
 GROUP = 4
 COEFS = 2 * PLANES
 F32 = jnp.float32
@@ -240,63 +242,60 @@
 def load_kernel(r):
     core = lax.axis_index(CORE)
     edge = jnp.where(core == 1, 2, 0)
-    small = [
-        pltpu.make_async_copy(getattr(r, n), getattr(r, n + "raw"), r.sems.at[i])
-        for i, n in enumerate(("nu", "fric", "rot", "ice", "ground"))
-    ]
-    v_copy = [
-        pltpu.make_async_copy(r.v.at[:, tile], r.vraw.at[:, tile], r.sems.at[5 + i])
-        for i, tile in enumerate((edge, 1, 2 - edge))
-    ]
-    f_copy = [
-        pltpu.make_async_copy(r.f.at[:, tile], r.fraw.at[:, tile], r.sems.at[8 + i])
-        for i, tile in enumerate((edge, 1, 2 - edge))
-    ]
-    for copy in small + v_copy[:2] + f_copy[:2] + [v_copy[2], f_copy[2]]:
-        copy.start()
-    for copy in small + v_copy[:2]:
-        copy.wait()
-    er, ei, link, nu = (Field(part(x, HALF, ROWS)) for x in (r.er, r.ei, r.link, r.nuh))
+    names = ("nu", "fric", "rot", "ice", "ground", "v", "f")
+    copies = {}
+    for i, tile in enumerate((edge, 1, 2 - edge)):
+        for j, n in enumerate(names):
+            copies[n, i] = pltpu.make_async_copy(
+                getattr(r, n).at[:, tile], getattr(r, n + "raw").at[:, tile], r.sems.at[i, j]
+            )
+            copies[n, i].start()
+    for n in names[:-1]:
+        copies[n, 0].wait()
+    er, ei, link, nu = (Field(part(x, BAND, ROWS)) for x in (r.er, r.ei, r.link, r.nuh))
     packed = Field(mirrored(r.p1, 0, REACH), mirrored(r.p1, REACH, 2 * REACH, PLANES))
-    for start in (12, 18):
-        ts = span(start, start + 6)
-        read = raw_reader(r, core, ts)
-        factor(ts, read, er, ei, link, nu)
-        vert, active, nu_row, drag, rot = read
-        for i, t in enumerate(ts):
-            if t >= ROWS - REACH:
-                for k in range(L - 1):
-                    packed.put(COEFS + k, [t], vert(k)[i : i + 1])
-                packed.put(COEFS + L - 1, [t], jnp.where(active, nu_row, 0.0)[i : i + 1])
-                packed.put(COEFS + L, [t], drag[i : i + 1])
-                packed.put(COEFS + L + 1, [t], rot[i : i + 1])
-    for copy in f_copy[:2]:
-        copy.wait()
-    source = raw_source(r.fraw, core)
-    s0 = Field(part(r.s0, HALF, ROWS))
-    for start in (12, 18):
-        ts = span(start, start + 6)
-        solve(ts, source, er, ei, link, s0, (packed, span(ROWS - 2 * REACH, ROWS)))
-    v_copy[2].wait()
-    f_copy[2].wait()
+    ts = span(BAND, ROWS)
+    read = raw_reader(r, core, ts)
+    factor(ts, read, er, ei, link, nu)
+    vert, active, nu_row, drag, rot = read
+    for i, t in enumerate(ts):
+        if t >= ROWS - REACH:
+            for k in range(L - 1):
+                packed.put(COEFS + k, [t], vert(k)[i : i + 1])
+            packed.put(COEFS + L - 1, [t], jnp.where(active, nu_row, 0.0)[i : i + 1])
+            packed.put(COEFS + L, [t], drag[i : i + 1])
+            packed.put(COEFS + L + 1, [t], rot[i : i + 1])
+    copies["f", 0].wait()
+    solve(ts, raw_source(r.fraw, core), er, ei, link, Field(part(r.s0, BAND, ROWS)), (packed, ts))
+    for i in (1, 2):
+        for n in names:
+            copies[n, i].wait()
 
 
 def ahead_kernel(r):
+    core = lax.axis_index(CORE)
     masks = cross_masks()
-    s0 = Field(part(r.s0, HALF, ROWS))
-    nu = Field(part(r.nuh, HALF, ROWS))
+    middle = span(HALF, BAND)
+    er_m, ei_m, link_m, nu_m = (part(x, HALF, BAND) for x in (r.er, r.ei, r.link, r.nuh))
+    s0_m = part(r.s0, HALF, BAND)
+    solver = (Field(er_m), Field(ei_m), Field(link_m))
+    factor(middle, raw_reader(r, core, middle), *solver, Field(nu_m))
+    solve(middle, raw_source(r.fraw, core), *solver, Field(s0_m))
+    s0 = Field(s0_m, part(r.s0_b, BAND, ROWS))
+    nu = Field(part(r.nuh_b, BAND, ROWS))
     known = span(HALF, ROWS)
+    ts = span(16, 20)
     u1 = Field(part(r.u1, 16, 20))
 
     def step(plane):
         s = {t: s0.row(plane, t) for t in known}
-        for t, total in stencil(span(16, 20), known, s, masks):
+        for t, total in stencil(ts, known, s, masks):
             u1.put(plane, [t], (nu.row(0, t) * total)[None])
 
     over_planes(step, 8)
-    er, ei, link = (Field(part(x, HALF, ROWS)) for x in (r.er, r.ei, r.link))
+    solver = tuple(Field(part(x, BAND, ROWS)) for x in (r.er_b, r.ei_b, r.link_b))
     packed = Field(mirrored(r.p2, REACH, 2 * REACH))
-    solve(span(16, 20), u1.get, er, ei, link, Field(part(r.s1, 16, 20)), (packed, span(16, 20)))
+    solve(ts, u1.get, *solver, Field(part(r.s1, 16, 20)), (packed, ts))
 
 
 def rest_kernel(r):
@@ -319,7 +318,8 @@
 
 
 def both_halves(r, name):
-    return Field(part(getattr(r, name + "_a"), 0, HALF), part(getattr(r, name + "_b"), HALF, ROWS))
+    starts = (("_a", 0, HALF), ("_m", HALF, BAND), ("_b", BAND, ROWS))
+    return Field(*(part(getattr(r, name + tag), a, b) for tag, a, b in starts if hasattr(r, name + tag)))
 
 
 def inner1_kernel(r):
@@ -436,8 +436,8 @@
 def band_kernel(r):
     masks = cross_masks()
     beyond = span(ROWS, ROWS + REACH)
-    nu_b = Field(part(r.nuh_b, HALF, ROWS))
-    nu = Field(part(r.nuh_b, HALF, ROWS), part(r.p1, ROWS, ROWS + REACH, COEFS + L - 1))
+    nu_own = both_halves(r, "nuh")
+    nu = Field(part(r.nuh_b, BAND, ROWS), part(r.p1, ROWS, ROWS + REACH, COEFS + L - 1))
     er_h, ei_h, link_h = (part(x, ROWS, ROWS + REACH) for x in (r.er_h, r.ei_h, r.link_h))
     nu_h = r.p1[COEFS + L - 1]
     read = (
@@ -448,11 +448,11 @@
         r.p1[COEFS + L + 1],
     )
     factor(beyond, read, Field(er_h), Field(ei_h), Field(link_h), None)
-    er = Field(part(r.er_b, HALF, ROWS), er_h)
-    ei = Field(part(r.ei_b, HALF, ROWS), ei_h)
-    link = Field(part(r.link_b, HALF, ROWS), link_h)
+    er = Field(part(r.er_b, BAND, ROWS), er_h)
+    ei = Field(part(r.ei_b, BAND, ROWS), ei_h)
+    link = Field(part(r.link_b, BAND, ROWS), link_h)
     s0 = Field(
-        part(r.s0_b, HALF, ROWS), part(r.p1, 24, 28), part(r.p1, 28, 32, PLANES)
+        part(r.s0_b, BAND, ROWS), part(r.p1, 24, 28), part(r.p1, 28, 32, PLANES)
     )
     u1_b = part(r.u1_b, 20, 28)
     known1 = span(16, 32)
@@ -465,42 +465,79 @@
     over_planes(first)
     s1_b = part(r.s1, 20, 28)
     solve(span(20, 28), Field(u1_b).get, er, ei, link, Field(s1_b))
-    s1 = Field(part(r.s1_a, 0, 16), part(r.s1_m, 16, 20), s1_b, part(r.p2, 28, 32))
+    s1 = Field(part(r.s1_a, 0, 16), part(r.s1_m, 16, 20), s1_b)
     u1 = Field(part(r.u1_i, REACH, 16), part(r.u1_m, 16, 20), u1_b)
     u0 = Field(part(r.u0, 0, ROWS))
-    u2_b = part(r.u2, 16, 28)
-    u2 = Field(part(r.u2_i, REACH, 16), u2_b)
-    known = span(12, 32)
-
-    def step(plane, add):
-        s = {t: s1.row(plane, t) for t in known}
-        for t, total in stencil(span(16, 28), known, s, masks):
-            value = nu.row(0, t) * total
-            u2.put(plane, [t], value[None])
+    u2_b = part(r.u2, 16, 24)
+    known2 = span(12, 28)
+
+    def second(plane, add):
+        s = {t: s1.row(plane, t) for t in known2}
+        for t, total in stencil(span(16, 28), known2, s, masks):
             if t < ROWS:
+                value = nu.row(0, t) * total
+                r.u2[plane, t - 16] = value
                 with_all(add, 2, value, plane, t, (u0, u1))
+            else:
+                r.nsum2[plane, t - ROWS] = total
         for t in span(20, ROWS):
             with_all(add, 1, u1.row(plane, t), plane, t, (u0,))
 
-    sums = loop_sums(pairs_of(1, 2), step)
-    s2_b = part(r.s2, 16, 28)
-    for start in (16, 22):
-        solve(span(start, start + 6), u2.get, er, ei, link, Field(s2_b))
+    sums = loop_sums(pairs_of(1, 2), second)
+    s2_b = part(r.s2, 16, 24)
+    solve(span(16, 24), Field(u2_b).get, er, ei, link, Field(s2_b))
     s2 = Field(part(r.s2_a, 0, 16), s2_b)
-    known3 = span(8, 28)
-
-    def last(plane, add):
+    u2 = Field(part(r.u2_i, REACH, 16), u2_b)
+    known3 = span(8, 24)
+
+    def third(plane, add):
         s = {t: s2.row(plane, t) for t in known3}
         for t, total in stencil(span(12, 24), known3, s, masks):
-            value = nu_b.row(0, t) * total
-            r.u3[plane, t - 12] = value
+            if t < 20:
+                value = nu_own.row(0, t) * total
+                r.u3[plane, t - 12] = value
+                with_all(add, 3, value, plane, t, (u0, u1, u2))
+            else:
+                r.nsum3[plane, t - 20] = total
+
+    sums.update(loop_sums(pairs_of(3), third))
+    zero = jnp.zeros(TILE, F32)
+    for i, pair in enumerate(GRAM):
+        r.sums[i] = r.sums2[i] + r.sums3[i] + r.sums4[i] + sums.get(pair, zero)
+
+
+def last_b_kernel(r):
+    beyond = span(ROWS, ROWS + REACH)
+    solver = tuple(Field(part(x, ROWS, ROWS + REACH)) for x in (r.er_h, r.ei_h, r.link_h))
+    nu_b = Field(part(r.nuh_b, BAND, ROWS))
+
+    def source(plane, ts):
+        rows = []
+        for j in range(REACH):
+            value = r.nsum2[plane, j]
+            for q in range(j + 1):
+                value = value + reach_weights[REACH - 1 - j + q] * r.p2[plane, q]
+            rows.append(r.p1[COEFS + L - 1, j] * value)
+        return jnp.stack(rows)
+
+    solve(beyond, source, *solver, Field(part(r.s2_h, ROWS, ROWS + REACH)))
+    u0 = Field(part(r.u0, 0, ROWS))
+    u1 = Field(part(r.u1_b, 20, 28))
+    u2 = Field(part(r.u2_b, 16, 24))
+
+    def step(plane, add):
+        for t in span(20, ROWS):
+            d = ROWS - 1 - t
+            value = halo_sum(r.nsum3[plane, t - 20], d, lambda q: r.s2_h[plane, q])
+            value = nu_b.row(0, t) * value
+            r.u3[plane, t - 20] = value
             with_all(add, 3, value, plane, t, (u0, u1, u2))
 
-    sums.update(loop_sums(pairs_of(3), last))
+    sums = loop_sums(pairs_of(3), step, 6)
     lane = lanes()
     out = jnp.zeros(TILE, F32)
     for i, pair in enumerate(GRAM):
-        value = r.sums2[i] + r.sums3[i] + r.sums4[i]
+        value = r.sums[i]
         if pair in sums:
             value = value + sums[pair]
         value = jnp.sum(jnp.sum(value, axis=0, keepdims=True), axis=1, keepdims=True)
@@ -524,11 +561,10 @@
             )
             column[row_index] = rotated_a
             column[row_index + 1] = rotated_b
-        radius = jnp.sqrt(
+        inverse = lax.rsqrt(
             column[column_index] * column[column_index]
             + column[column_index + 1] * column[column_index + 1]
         )
-        inverse = 1.0 / radius
         cosine = column[column_index] * inverse
         sine_value = column[column_index + 1] * inverse
         column[column_index] = inverse
@@ -561,17 +597,16 @@
         square = gram[(a, a)]
         for p in range(a):
             square = square - upper[(p, a)] * upper[(p, a)]
-        square = jnp.maximum(square, 0.0)
-        length = jnp.sqrt(square)
-        inverse = jnp.where(length > 0.0, 1.0 / jnp.where(length > 0.0, length, 1.0), 0.0)
-        upper[(a, a)] = length
+        inverse = jnp.where(square > 0.0, lax.rsqrt(jnp.maximum(square, TINY)), 0.0)
+        upper[(a, a)] = square * inverse
         for b in range(a + 1, size):
             value = gram[(a, b)]
             for p in range(a):
                 value = value - upper[(p, a)] * upper[(p, b)]
             upper[(a, b)] = value * inverse
-    beta = jnp.sqrt(gram[(0, 0)] + epsilon)
-    inverse = 1.0 / beta
+    square = gram[(0, 0)] + epsilon
+    inverse = lax.rsqrt(square)
+    beta = square * inverse
     basis = [[inverse]]
     ortho = [[upper[(0, 0)] * inverse]]
     columns = []
@@ -589,11 +624,11 @@
                 q[m] = q[m] - h * ortho[i][m]
                 w[m] = w[m] - h * basis[i][m]
             column.append(h)
-        length = jnp.sqrt(dot(q, q) + epsilon)
-        column.append(length)
+        square = dot(q, q) + epsilon
+        inverse = lax.rsqrt(square)
+        column.append(square * inverse)
         columns.append(column)
         if j < 2:
-            inverse = 1.0 / length
             basis.append([value * inverse for value in w])
             ortho.append([value * inverse for value in q])
     y = least_squares(columns, beta)
@@ -617,13 +652,15 @@
     places = [place_of(core, t) for t in range(ROWS)]
     s0 = both_halves(r, "s0")
     s1 = Field(part(r.s1_a, 0, 16), part(r.s1_m, 16, 20), part(r.s1_b, 20, 28))
-    s2 = Field(part(r.s2_a, 0, 16), part(r.s2_b, 16, 28))
+    s2 = Field(part(r.s2_a, 0, 16), part(r.s2_b, 16, 24))
     u0 = Field(part(r.u0, 0, ROWS))
     u1 = Field(
         part(r.u1_e, 0, 4), part(r.u1_i, 4, 16), part(r.u1_m, 16, 20), part(r.u1_b, 20, 28)
     )
-    u2 = Field(part(r.u2_e, 0, 4), part(r.u2_i, 4, 16), part(r.u2_b, 16, 28))
-    u3 = Field(part(r.u3_e, 0, 4), part(r.u3_i, 4, 12), part(r.u3_b, 12, 24))
+    u2 = Field(part(r.u2_e, 0, 4), part(r.u2_i, 4, 16), part(r.u2_b, 16, 24))
+    u3 = Field(
+        part(r.u3_e, 0, 4), part(r.u3_i, 4, 12), part(r.u3_b, 12, 20), part(r.u3_h, 20, 24)
+    )
 
     def step(plane):
         for t in range(ROWS):
@@ -698,29 +735,38 @@
         return {k + tag: src[k] for k in keys}
 
     edge = vmem(PLANES, REACH)
+    rows_b, rows_m = ROWS - BAND, BAND - HALF
     k0 = call(
         load_kernel,
         ins,
         {
-            **factors(HALF),
-            "nuh": vmem(1, HALF),
-            "s0": vmem(PLANES, HALF),
+            **factors(rows_b),
+            "nuh": vmem(1, rows_b),
+            "s0": vmem(PLANES, rows_b),
             "p1": vmem(COEFS + L + 2, REACH),
             **raws,
         },
-        {"sems": pltpu.SemaphoreType.DMA((11,))},
+        {"sems": pltpu.SemaphoreType.DMA((3, 7))},
         in_specs=HB,
     )
     p1 = across(k0["p1"])
+    raw = pick(k0, "", *raws)
     ahead = call(
         ahead_kernel,
-        pick(k0, "", "s0", "nuh", "er", "ei", "link"),
-        {"u1": edge, "s1": edge, "p2": edge},
+        {**pick(k0, "_b", "s0", "nuh", "er", "ei", "link"), **raw},
+        {
+            **factors(rows_m),
+            "nuh": vmem(1, rows_m),
+            "s0": vmem(PLANES, rows_m),
+            "u1": edge,
+            "s1": edge,
+            "p2": edge,
+        },
     )
     p2 = across(ahead["p2"])
     k1 = call(
         rest_kernel,
-        {**pick(k0, "", *raws), "order": ahead["p2"]},
+        {**raw, "order": ahead["p2"]},
         {
             **factors(HALF),
             "nuh": vmem(1, HALF),
@@ -731,18 +777,18 @@
     )
     halves = {}
     for key in ("er", "ei", "link", "nuh", "s0"):
-        halves[key + "_a"], halves[key + "_b"] = k1[key], k0[key]
+        halves[key + "_a"], halves[key + "_m"], halves[key + "_b"] = k1[key], ahead[key], k0[key]
     u0 = {"u0": k1["u0"]}
 
     def some(*keys):
         return {k: halves[k] for k in keys}
 
-    operator = some("er_a", "er_b", "ei_a", "ei_b", "link_a", "link_b", "nuh_a")
+    operator = some("er_a", "er_m", "ei_a", "ei_m", "link_a", "link_m", "nuh_a")
     solved = {"u_edge": edge, "s": vmem(PLANES, 16), "sa": edge}
     ha = within(k1["sa"])
     n1 = call(
         inner1_kernel,
-        some("s0_a", "s0_b", "nuh_a", "nuh_b"),
+        some("s0_a", "s0_m", "s0_b", "nuh_a", "nuh_m"),
         {"nsum": edge, "u1": vmem(PLANES, HALF)},
     )
     e1 = call(edge_a_kernel, {"ha": ha, "nsum": n1["nsum"], "u_in": n1["u1"], **operator}, solved)
@@ -752,7 +798,7 @@
     s1 = {"s1_a": e1["s"], "s1_m": ahead["s1"]}
     n2 = call(
         inner2_kernel,
-        {**s1, **some("nuh_a", "nuh_b"), **u0, **first, **middle},
+        {**s1, **some("nuh_a", "nuh_m"), **u0, **first, **middle},
         {"nsum": edge, "u2": vmem(PLANES, HALF), "sums": vmem(10)},
     )
     e2 = call(edge_a_kernel, {"ha": ha, "nsum": n2["nsum"], "u_in": n2["u2"], **operator}, solved)
@@ -775,12 +821,11 @@
         },
         {"u3": edge, "sums": vmem(10)},
     )
-    b2 = call(
+    b1 = call(
         band_kernel,
         {
             "p1": p1,
-            "p2": p2,
-            **some("er_b", "ei_b", "link_b", "nuh_b", "s0_b"),
+            **some("er_b", "ei_b", "link_b", "nuh_m", "nuh_b", "s0_b"),
             **u0,
             "u1_i": n1["u1"],
             **middle,
@@ -792,14 +837,29 @@
             "sums4": a3["sums"],
         },
         {
+            **{k + "_h": x for k, x in factors(REACH).items()},
             "u1_b": vmem(PLANES, 8),
             "s1": vmem(PLANES, 8),
-            "u2": vmem(PLANES, HALF),
-            "s2": vmem(PLANES, HALF),
-            "u3": vmem(PLANES, HALF),
-            "payload": jax.ShapeDtypeStruct((128, 128), F32),
+            "u2": vmem(PLANES, 8),
+            "nsum2": edge,
+            "s2": vmem(PLANES, 8),
+            "u3": vmem(PLANES, 8),
+            "nsum3": edge,
+            "sums": vmem(10),
         },
-        {"er_h": vmem(L, REACH), "ei_h": vmem(L, REACH), "link_h": vmem(L - 1, REACH)},
+    )
+    b2 = call(
+        last_b_kernel,
+        {
+            "p1": p1,
+            "p2": p2,
+            **some("nuh_b"),
+            **u0,
+            **pick(b1, "", "er_h", "ei_h", "link_h", "nsum2", "nsum3", "u1_b", "sums"),
+            "u2_b": b1["u2"],
+        },
+        {"u3": edge, "payload": jax.ShapeDtypeStruct((128, 128), F32)},
+        {"s2_h": edge},
     )
     gathered = lax.all_to_all(b2["payload"], FLOW, split_axis=0, concat_axis=0, tiled=True)
     shape = (PLANES, ROWS // 8, 64, 128)
@@ -807,20 +867,21 @@
         final_kernel,
         {
             "gathered": gathered,
-            **some("s0_a", "s0_b"),
+            **some("s0_a", "s0_m", "s0_b"),
             **s1,
-            "s1_b": b2["s1"],
+            "s1_b": b1["s1"],
             "s2_a": e2["s"],
-            "s2_b": b2["s2"],
+            "s2_b": b1["s2"],
             **u0,
             **first,
             **middle,
-            "u1_b": b2["u1_b"],
+            "u1_b": b1["u1_b"],
             **second,
-            "u2_b": b2["u2"],
+            "u2_b": b1["u2"],
             "u3_e": a3["u3"],
             "u3_i": n3["u3"],
-            "u3_b": b2["u3"],
+            "u3_b": b1["u3"],
+            "u3_h": b2["u3"],
         },
         {"out_s": jax.ShapeDtypeStruct(shape, F32), "out_r": jax.ShapeDtypeStruct(shape, F32)},
         {

time: 57.3 us -> 53.8 us (0.939)
  waiting for transfers between devices: 7.37 us -> 3.35 us
    ppermute x2, waiting for transfers between devices: 7.36 us -> 3.34 us  [across(): return lax.ppermute(x, FLOW, pairs + [(b, a) for a, b in pairs])]
    pallas_call x11 -> x12, Pallas kernels: 17.2 us -> 17.7 us  [call(): pl.pallas_call(run, out_shape=list(outs.values()), in_specs=[in_specs or...]
  transfers between devices with their start and end apart: 5 -> 5, of which waited for: 1 -> 2; matrix products, arithmetic and copies ran while one was open for 0% -> 0% of each run, Pallas kernels for 10% -> 18%
where the time goes in v5:
time: 53.8 us; the launch traced here: 53.6 us
  blocking collectives  23.5 us (44%)
  Pallas kernels  17.7 us (33%)
  starting transfers between devices  8.27 us (15%)
  waiting for transfers between devices  3.35 us (6%)
  between operations  0.75 us (1%)
    all_to_all x1, blocking collectives, body(): lax.all_to_all(b2['payload'], FLOW, split_axis=0, concat_axis=0, tiled=True)  23.5 us
    pallas_call x12, Pallas kernels, call(): pl.pallas_call(run, out_shape=list(outs.values()), in_specs=[in_specs or...  17.7 us
    ppermute x2, starting transfers between devices, across(): return lax.ppermute(x, FLOW, pairs + [(b, a) for a, b in pairs])  6.15 us
    ppermute x2, waiting for transfers between devices, across(): return lax.ppermute(x, FLOW, pairs + [(b, a) for a, b in pairs])  3.34 us
    ppermute x3, starting transfers between devices, within(): return lax.ppermute(x, FLOW, [(i, i ^ 1) for i in range(128)])  2.12 us
  transfers between devices with their start and end apart: 5, of which 2 were waited for; matrix products, arithmetic and copies ran while one was open for 0% of the time, Pallas kernels for 18%

profile of v5, /device:TPU:1, one launch (start us, length us, event | category | flops | bytes accessed | tf_op | source)
XLA Modules:
  0.0 53.6 jit_solution(4867976448001472146)
XLA Ops:
  0.6 2.3 %shard_map.86 = (f32[12,8,8,128]{3,2,1,0:T(8,128)S(1)}, f32[12,8,8,128]{3,2,1,0:T(8,128)S(1)}, f32[11,8,8,128]{3,2,1,0:T(8,128)S(1)}, f32[1,8,8,128]{3,2,1,0:T(8...) custom-call(f32[24,3,64,128]{3,2,1,0:T(8,128)} %bitcast.51, ...), custom_call_target="tpu_custom_call" | custom-call | tf_op jit(solution)/shard_map/pallas_call | solution.py:703
  3.0 0.9 %shard_map.87 = (f32[12,4,8,128]{3,2,1,0:T(8,128)S(1)}, f32[12,4,8,128]{3,2,1,0:T(8,128)S(1)}, f32[11,4,8,128]{3,2,1,0:T(8,128)S(1)}, f32[1,4,8,128]{3,2,1,0:T(8...) custom-call(f32[24,8,8,128]{3,2,1,0:T(8,128)S(1)} %get-tuple-element, ...), custom_call_target="tpu_custom_call" | custom-call | tf_op jit(solution)/shard_map/pallas_call | solution.py:703
  3.9 1.5 %shard_map.88 = (f32[12,12,8,128]{3,2,1,0:T(8,128)S(1)}, f32[12,12,8,128]{3,2,1,0:T(8,128)S(1)}, f32[11,12,8,128]{3,2,1,0:T(8,128)S(1)}, f32[1,12,8,128]{3,2,1,0...) custom-call(f32[24,3,64,128]{3,2,1,0:T(8,128)S(1)} %get-tuple-element.6, ...), custom_call_target="tpu_custom_call" | custom-call | tf_op jit(solution)/shard_map/pallas_call | solution.py:703
  5.4 1.5 %collective-permute-start.2 = (f32[24,4,8,128]{3,2,1,0:T(8,128)S(1)}, f32[24,4,8,128]{3,2,1,0:T(8,128)S(1)}, u32[]{:S(2)}, u32[]{:S(2)}) collective-permute-start(f32[24,4,8,128]{3,2,1,0:T(8,128)S(1)} %get-tuple-element.82), channel_id=1, source_target_pairs={{0,1},{1,0},{2,3},{3,2},{4,5},{5,4},{6,7},{7,6},{8,9},{9,8},{10,11... | collective-permute-start | bytes 1179656 | tf_op jit(solution)/shard_map/ppermute | solution.py:715
  6.9 3.1 %collective-permute-start = (f32[62,4,8,128]{3,2,1,0:T(8,128)S(1)}, f32[62,4,8,128]{3,2,1,0:T(8,128)S(1)}, u32[]{:S(2)}, u32[]{:S(2)}) collective-permute-start(f32[62,4,8,128]{3,2,1,0:T(8,128)S(1)} %get-tuple-element.61), channel_id=1, source_target_pairs={{1,2},{3,4},{5,6},{7,8},{9,10},{11,12},{13,14},{15,16},{17,18},{19... | collective-permute-start | bytes 3047432 | tf_op jit(solution)/shard_map/ppermute | solution.py:720
  10.0 1.3 %shard_map.89 = (f32[24,4,8,128]{3,2,1,0:T(8,128)S(1)}, f32[24,12,8,128]{3,2,1,0:T(8,128)S(1)}) custom-call(f32[24,12,8,128]{3,2,1,0:T(8,128)S(1)} %get-tuple-element.77.refs_0_.refs_1_, f32[24,4,8,128]{3,2,1,0:T(8,128)S(1)} %get-tuple-element.78.refs_1_.refs_2_, f32[24,8,8,128]{3,2,1,0:T(8,128)S(1)} %get-tuple-element.62.refs_0_.refs_2_.refs_6_.refs_3_, ...), custom_call_target="tpu_custom_call" | custom-call | tf_op jit(solution)/shard_map/pallas_call | solution.py:703
  11.3 0.0 collective-permute-done.2.refs_0_
  11.3 0.6 %shard_map.90 = (f32[24,4,8,128]{3,2,1,0:T(8,128)S(1)}, f32[24,16,8,128]{3,2,1,0:T(8,128)S(1)}, f32[24,4,8,128]{3,2,1,0:T(8,128)S(1)}) custom-call(f32[24,4,8,128]{3,2,1,0:T(8,128)S(1)} %collective-permute-done.2.refs_0_, f32[24,4,8,128]{3,2,1,0:T(8,128)S(1)} %get-tuple-element.83.refs_1_, ...), custom_call_target="tpu_custom_call" | custom-call | tf_op jit(solution)/shard_map/pallas_call | solution.py:703
  11.9 0.1 collective-permute-start.3
  12.0 1.8 %shard_map.91 = (f32[24,4,8,128]{3,2,1,0:T(8,128)S(1)}, f32[24,12,8,128]{3,2,1,0:T(8,128)S(1)}, f32[10,8,128]{2,1,0:T(8,128)S(1)}) custom-call(f32[24,16,8,128]{3,2,1,0:T(8,128)S(1)} %get-tuple-element.90.refs_0_.refs_10_.refs_4_, f32[24,4,8,128]{3,2,1,0:T(8,128)S(1)} %get-tuple-element.91.refs_1_.refs_11_.refs_5_, ...), custom_call_target="tpu_custom_call" | custom-call | tf_op jit(solution)/shard_map/pallas_call | solution.py:703
  13.8 0.0 collective-permute-done.3.refs_0_
  13.8 0.6 %shard_map.92 = (f32[24,4,8,128]{3,2,1,0:T(8,128)S(1)}, f32[24,16,8,128]{3,2,1,0:T(8,128)S(1)}, f32[24,4,8,128]{3,2,1,0:T(8,128)S(1)}) custom-call(f32[24,4,8,128]{3,2,1,0:T(8,128)S(1)} %collective-permute-done.3.refs_0_, f32[24,4,8,128]{3,2,1,0:T(8,128)S(1)} %get-tuple-element.95.refs_1_, ...), custom_call_target="tpu_custom_call" | custom-call | tf_op jit(solution)/shard_map/pallas_call | solution.py:703
  14.5 0.6 %collective-permute-start.4 = (f32[24,4,8,128]{3,2,1,0:T(8,128)S(1)}, f32[24,4,8,128]{3,2,1,0:T(8,128)S(1)}, u32[]{:S(2)}, u32[]{:S(2)}) collective-permute-start(f32[24,4,8,128]{3,2,1,0:T(8,128)S(1)} %get-tuple-element.100), channel_id=1, source_target_pairs={{0,1},{1,0},{2,3},{3,2},{4,5},{5,4},{6,7},{7,6},{8,9},{9,8},{10,11... | collective-permute-start | bytes 1179656 | tf_op jit(solution)/shard_map/ppermute | solution.py:715
  15.0 3.0 %collective-permute-start.1 = (f32[24,4,8,128]{3,2,1,0:T(8,128)S(1)}, f32[24,4,8,128]{3,2,1,0:T(8,128)S(1)}, u32[]{:S(2)}, u32[]{:S(2)}) collective-permute-start(f32[24,4,8,128]{3,2,1,0:T(8,128)S(1)} %get-tuple-element.74.refs_7_), channel_id=1, source_target_pairs={{1,2},{3,4},{5,6},{7,8},{9,10},{11,12},{13,14},{15,16},{17,18},{19... | collective-permute-start | bytes 1179656 | tf_op jit(solution)/shard_map/ppermute | solution.py:720
  18.1 1.2 %shard_map.93 = (f32[24,4,8,128]{3,2,1,0:T(8,128)S(1)}, f32[24,8,8,128]{3,2,1,0:T(8,128)S(1)}, f32[10,8,128]{2,1,0:T(8,128)S(1)}) custom-call(f32[24,16,8,128]{3,2,1,0:T(8,128)S(1)} %get-tuple-element.96.refs_0_.refs_13_.refs_7_, f32[1,12,8,128]{3,2,1,0:T(8,128)S(1)} %get-tuple-element.79.refs_3_.refs_9_.refs_2_.refs_1_, ...), custom_call_target="tpu_custom_call" | custom-call | tf_op jit(solution)/shard_map/pallas_call | solution.py:703
  19.3 0.0 collective-permute-done.4.refs_0_
  19.3 0.3 shard_map.94
  19.5 3.1 %collective-permute-done.refs_0_ = f32[62,4,8,128]{3,2,1,0:T(8,128)S(1)} collective-permute-done((f32[62,4,8,128]{3,2,1,0:T(8,128)S(1)}, f32[62,4,8,128]{3,2,1,0:T(8,128)S(1)}, u32[]{:S(2)}, u32[]{:S(2)}) %collective-permute-start) | collective-permute-done | bytes 1015840 | tf_op jit(solution)/shard_map/ppermute | solution.py:720
  22.6 3.9 %shard_map.95 = (f32[12,4,8,128]{3,2,1,0:T(8,128)S(1)}, f32[12,4,8,128]{3,2,1,0:T(8,128)S(1)}, f32[11,4,8,128]{3,2,1,0:T(8,128)S(1)}, f32[24,8,8,128]{3,2,1,0:T(...) custom-call(f32[62,4,8,128]{3,2,1,0:T(8,128)S(1)} %collective-permut, ...), custom_call_target="tpu_custom_call" | custom-call | tf_op jit(solution)/shard_map/pallas_call | solution.py:703
  26.6 0.3 collective-permute-done.1.refs_1_
  26.8 0.5 %shard_map.96 = (f32[24,4,8,128]{3,2,1,0:T(8,128)S(1)}, f32[128,128]{1,0:T(8,128)S(1)}) custom-call(f32[62,4,8,128]{3,2,1,0:T(8,128)S(1)} %collective-permute-done.refs_0_, f32[24,4,8,128]{3,2,1,0:T(8,128)S(1)} %collective-permute-done.1.refs_1_, f32[1,8,8,128]{3,2,1,0:T(8,128)S(1)} %get-tuple-element.63.refs_1_.refs_5_.refs_2_, ...), custom_call_target="tpu_custom_call" | custom-call | tf_op jit(solution)/shard_map/pallas_call | solution.py:703
  27.4 23.5 %all_to_all.11 = f32[128,1,128]{2,1,0:T(1,128)S(1)} all-to-all(f32[128,1,128]{2,1,0:T(1,128)S(1)} %bitcast.50), channel_id=1, replica_groups=mesh['flow_0'=4,'flow_1'=4,'flow_2'=4,'flow_3'=2] {'flow_0','flow_1','fl..., dimensions={0} | all-to-all | bytes 131072 | tf_op jit(solution)/shard_map/all_to_all | solution.py:864
  50.9 2.7 %shard_map.97 = (f32[24,3,64,128]{3,2,1,0:T(8,128)}, f32[24,3,64,128]{3,2,1,0:T(8,128)}) custom-call(f32[128,128]{1,0:T(8,128)S(1)} %bitcast.49, f32[24,12,8,128]{3,2,1,0:T(8,128)S(1)} %get-tuple-element.77.refs_0_.refs_1_, f32[24,4,8,128]{3,2,1,0:T(8,128)S(1)} %get-tuple-element.78.refs_1_.refs_2_, ...), custom_call_target="tpu_custom_call" | custom-call | tf_op jit(solution)/shard_map/pallas_call | solution.py:703
Async XLA Ops:
  5.4 5.9 %collective-permute-start.2 = (f32[24,4,8,128]{3,2,1,0:T(8,128)S(1)}, f32[24,4,8,128]{3,2,1,0:T(8,128)S(1)}, u32[]{:S(2)}, u32[]{:S(2)}) collective-permute-start(f32[24,4,8,128]{3,2,1,0:T(8,128)S(1)} %get-tuple-element.82), channel_id=1, source_target_pairs={{0,1},{1,0},{2,3},{3,2},{4,5},{5,4},{6,7},{7,6},{8,9},{9,8},{10,11... | collective-permute-start | bytes 1179656 | tf_op jit(solution)/shard_map/ppermute | solution.py:715
  6.9 15.8 %collective-permute-start = (f32[62,4,8,128]{3,2,1,0:T(8,128)S(1)}, f32[62,4,8,128]{3,2,1,0:T(8,128)S(1)}, u32[]{:S(2)}, u32[]{:S(2)}) collective-permute-start(f32[62,4,8,128]{3,2,1,0:T(8,128)S(1)} %get-tuple-element.61), channel_id=1, source_target_pairs={{1,2},{3,4},{5,6},{7,8},{9,10},{11,12},{13,14},{15,16},{17,18},{19... | collective-permute-start | bytes 3047432 | tf_op jit(solution)/shard_map/ppermute | solution.py:720
  11.9 1.9 %collective-permute-start.3 = (f32[24,4,8,128]{3,2,1,0:T(8,128)S(1)}, f32[24,4,8,128]{3,2,1,0:T(8,128)S(1)}, u32[]{:S(2)}, u32[]{:S(2)}) collective-permute-start(f32[24,4,8,128]{3,2,1,0:T(8,128)S(1)} %get-tuple-element.94), channel_id=1, source_target_pairs={{0,1},{1,0},{2,3},{3,2},{4,5},{5,4},{6,7},{7,6},{8,9},{9,8},{10,11... | collective-permute-start | bytes 1179656 | tf_op jit(solution)/shard_map/ppermute | solution.py:715
  14.5 4.8 %collective-permute-start.4 = (f32[24,4,8,128]{3,2,1,0:T(8,128)S(1)}, f32[24,4,8,128]{3,2,1,0:T(8,128)S(1)}, u32[]{:S(2)}, u32[]{:S(2)}) collective-permute-start(f32[24,4,8,128]{3,2,1,0:T(8,128)S(1)} %get-tuple-element.100), channel_id=1, source_target_pairs={{0,1},{1,0},{2,3},{3,2},{4,5},{5,4},{6,7},{7,6},{8,9},{9,8},{10,11... | collective-permute-start | bytes 1179656 | tf_op jit(solution)/shard_map/ppermute | solution.py:715
  15.0 11.8 %collective-permute-start.1 = (f32[24,4,8,128]{3,2,1,0:T(8,128)S(1)}, f32[24,4,8,128]{3,2,1,0:T(8,128)S(1)}, u32[]{:S(2)}, u32[]{:S(2)}) collective-permute-start(f32[24,4,8,128]{3,2,1,0:T(8,128)S(1)} %get-tuple-element.74.refs_7_), channel_id=1, source_target_pairs={{1,2},{3,4},{5,6},{7,8},{9,10},{11,12},{13,14},{15,16},{17,18},{19... | collective-permute-start | bytes 1179656 | tf_op jit(solution)/shard_map/ppermute | solution.py:720

commit v6 on v5

--- a/solution.py
+++ b/solution.py
@@ -150,15 +150,14 @@
     lane = lanes()
     sub = lax.broadcasted_iota(jnp.int32, TILE, 0)
     first, last = lane == 0, lane == 127
-    return first, last, first & (sub == 7), last & (sub == 0)
+    return first, last, (first & (sub == 0)) | (last & (sub == 7))
 
 
 def cross(s, masks):
-    first, last, first_end, last_end = masks
-    up = jnp.where(first, pltpu.roll(s, 7, 0), s)
-    up = jnp.where(first_end, 0.0, up)
-    down = jnp.where(last, pltpu.roll(s, 1, 0), s)
-    down = jnp.where(last_end, 0.0, down)
+    first, last, ends = masks
+    inside = jnp.where(ends, 0.0, s)
+    up = jnp.where(first, pltpu.roll(inside, 7, 0), s)
+    down = jnp.where(last, pltpu.roll(inside, 1, 0), s)
     return pltpu.roll(up, 127, 1) + pltpu.roll(down, 1, 1)
 
 
@@ -242,7 +241,7 @@
 def load_kernel(r):
     core = lax.axis_index(CORE)
     edge = jnp.where(core == 1, 2, 0)
-    names = ("nu", "fric", "rot", "ice", "ground", "v", "f")
+    names = ("f", "v", "nu", "fric", "rot", "ice", "ground")
     copies = {}
     for i, tile in enumerate((edge, 1, 2 - edge)):
         for j, n in enumerate(names):
@@ -250,7 +249,7 @@
                 getattr(r, n).at[:, tile], getattr(r, n + "raw").at[:, tile], r.sems.at[i, j]
             )
             copies[n, i].start()
-    for n in names[:-1]:
+    for n in names:
         copies[n, 0].wait()
     er, ei, link, nu = (Field(part(x, BAND, ROWS)) for x in (r.er, r.ei, r.link, r.nuh))
     packed = Field(mirrored(r.p1, 0, REACH), mirrored(r.p1, REACH, 2 * REACH, PLANES))
@@ -265,7 +264,6 @@
             packed.put(COEFS + L - 1, [t], jnp.where(active, nu_row, 0.0)[i : i + 1])
             packed.put(COEFS + L, [t], drag[i : i + 1])
             packed.put(COEFS + L + 1, [t], rot[i : i + 1])
-    copies["f", 0].wait()
     solve(ts, raw_source(r.fraw, core), er, ei, link, Field(part(r.s0, BAND, ROWS)), (packed, ts))
     for i in (1, 2):
         for n in names:
@@ -533,7 +531,7 @@
             r.u3[plane, t - 20] = value
             with_all(add, 3, value, plane, t, (u0, u1, u2))
 
-    sums = loop_sums(pairs_of(3), step, 6)
+    sums = loop_sums(pairs_of(3), step, 12)
     lane = lanes()
     out = jnp.zeros(TILE, F32)
     for i, pair in enumerate(GRAM):

time: 53.8 us -> 53.7 us (level)
  no operation moved by 1% of the time
where the time goes in v6:
time: 53.7 us; the launch traced here: 53.5 us
  blocking collectives  23.5 us (44%)
  Pallas kernels  17.5 us (33%)
  starting transfers between devices  8.27 us (15%)
  waiting for transfers between devices  3.47 us (6%)
  between operations  0.75 us (1%)
    all_to_all x1, blocking collectives, body(): lax.all_to_all(b2['payload'], FLOW, split_axis=0, concat_axis=0, tiled=True)  23.5 us
    pallas_call x12, Pallas kernels, call(): pl.pallas_call(run, out_shape=list(outs.values()), in_specs=[in_specs or...  17.5 us
    ppermute x2, starting transfers between devices, across(): return lax.ppermute(x, FLOW, pairs + [(b, a) for a, b in pairs])  6.15 us
    ppermute x2, waiting for transfers between devices, across(): return lax.ppermute(x, FLOW, pairs + [(b, a) for a, b in pairs])  3.46 us
    ppermute x3, starting transfers between devices, within(): return lax.ppermute(x, FLOW, [(i, i ^ 1) for i in range(128)])  2.12 us
  transfers between devices with their start and end apart: 5, of which 2 were waited for; matrix products, arithmetic and copies ran while one was open for 0% of the time, Pallas kernels for 18%

profile of v6, /device:TPU:1, one launch (start us, length us, event | category | flops | bytes accessed | tf_op | source)
XLA Modules:
  0.0 53.5 jit_solution(3438336292709565046)
XLA Ops:
  0.6 2.3 %shard_map.86 = (f32[12,8,8,128]{3,2,1,0:T(8,128)S(1)}, f32[12,8,8,128]{3,2,1,0:T(8,128)S(1)}, f32[11,8,8,128]{3,2,1,0:T(8,128)S(1)}, f32[1,8,8,128]{3,2,1,0:T(8...) custom-call(f32[24,3,64,128]{3,2,1,0:T(8,128)} %bitcast.51, ...), custom_call_target="tpu_custom_call" | custom-call | tf_op jit(solution)/shard_map/pallas_call | solution.py:701
  2.9 0.9 %shard_map.87 = (f32[12,4,8,128]{3,2,1,0:T(8,128)S(1)}, f32[12,4,8,128]{3,2,1,0:T(8,128)S(1)}, f32[11,4,8,128]{3,2,1,0:T(8,128)S(1)}, f32[1,4,8,128]{3,2,1,0:T(8...) custom-call(f32[24,8,8,128]{3,2,1,0:T(8,128)S(1)} %get-tuple-element, ...), custom_call_target="tpu_custom_call" | custom-call | tf_op jit(solution)/shard_map/pallas_call | solution.py:701
  3.8 1.5 %shard_map.88 = (f32[12,12,8,128]{3,2,1,0:T(8,128)S(1)}, f32[12,12,8,128]{3,2,1,0:T(8,128)S(1)}, f32[11,12,8,128]{3,2,1,0:T(8,128)S(1)}, f32[1,12,8,128]{3,2,1,0...) custom-call(f32[24,3,64,128]{3,2,1,0:T(8,128)S(1)} %get-tuple-element.6, ...), custom_call_target="tpu_custom_call" | custom-call | tf_op jit(solution)/shard_map/pallas_call | solution.py:701
  5.3 1.5 %collective-permute-start.2 = (f32[24,4,8,128]{3,2,1,0:T(8,128)S(1)}, f32[24,4,8,128]{3,2,1,0:T(8,128)S(1)}, u32[]{:S(2)}, u32[]{:S(2)}) collective-permute-start(f32[24,4,8,128]{3,2,1,0:T(8,128)S(1)} %get-tuple-element.82), channel_id=1, source_target_pairs={{0,1},{1,0},{2,3},{3,2},{4,5},{5,4},{6,7},{7,6},{8,9},{9,8},{10,11... | collective-permute-start | bytes 1179656 | tf_op jit(solution)/shard_map/ppermute | solution.py:713
  6.8 3.1 %collective-permute-start = (f32[62,4,8,128]{3,2,1,0:T(8,128)S(1)}, f32[62,4,8,128]{3,2,1,0:T(8,128)S(1)}, u32[]{:S(2)}, u32[]{:S(2)}) collective-permute-start(f32[62,4,8,128]{3,2,1,0:T(8,128)S(1)} %get-tuple-element.61), channel_id=1, source_target_pairs={{1,2},{3,4},{5,6},{7,8},{9,10},{11,12},{13,14},{15,16},{17,18},{19... | collective-permute-start | bytes 3047432 | tf_op jit(solution)/shard_map/ppermute | solution.py:718
  9.9 1.3 %shard_map.89 = (f32[24,4,8,128]{3,2,1,0:T(8,128)S(1)}, f32[24,12,8,128]{3,2,1,0:T(8,128)S(1)}) custom-call(f32[24,12,8,128]{3,2,1,0:T(8,128)S(1)} %get-tuple-element.77.refs_0_.refs_1_, f32[24,4,8,128]{3,2,1,0:T(8,128)S(1)} %get-tuple-element.78.refs_1_.refs_2_, f32[24,8,8,128]{3,2,1,0:T(8,128)S(1)} %get-tuple-element.62.refs_0_.refs_2_.refs_6_.refs_3_, ...), custom_call_target="tpu_custom_call" | custom-call | tf_op jit(solution)/shard_map/pallas_call | solution.py:701
  11.2 0.0 collective-permute-done.2.refs_0_
  11.2 0.6 %shard_map.90 = (f32[24,4,8,128]{3,2,1,0:T(8,128)S(1)}, f32[24,16,8,128]{3,2,1,0:T(8,128)S(1)}, f32[24,4,8,128]{3,2,1,0:T(8,128)S(1)}) custom-call(f32[24,4,8,128]{3,2,1,0:T(8,128)S(1)} %collective-permute-done.2.refs_0_, f32[24,4,8,128]{3,2,1,0:T(8,128)S(1)} %get-tuple-element.83.refs_1_, ...), custom_call_target="tpu_custom_call" | custom-call | tf_op jit(solution)/shard_map/pallas_call | solution.py:701
  11.9 0.1 collective-permute-start.3
  11.9 1.8 %shard_map.91 = (f32[24,4,8,128]{3,2,1,0:T(8,128)S(1)}, f32[24,12,8,128]{3,2,1,0:T(8,128)S(1)}, f32[10,8,128]{2,1,0:T(8,128)S(1)}) custom-call(f32[24,16,8,128]{3,2,1,0:T(8,128)S(1)} %get-tuple-element.90.refs_0_.refs_10_.refs_4_, f32[24,4,8,128]{3,2,1,0:T(8,128)S(1)} %get-tuple-element.91.refs_1_.refs_11_.refs_5_, ...), custom_call_target="tpu_custom_call" | custom-call | tf_op jit(solution)/shard_map/pallas_call | solution.py:701
  13.7 0.0 collective-permute-done.3.refs_0_
  13.7 0.6 %shard_map.92 = (f32[24,4,8,128]{3,2,1,0:T(8,128)S(1)}, f32[24,16,8,128]{3,2,1,0:T(8,128)S(1)}, f32[24,4,8,128]{3,2,1,0:T(8,128)S(1)}) custom-call(f32[24,4,8,128]{3,2,1,0:T(8,128)S(1)} %collective-permute-done.3.refs_0_, f32[24,4,8,128]{3,2,1,0:T(8,128)S(1)} %get-tuple-element.95.refs_1_, ...), custom_call_target="tpu_custom_call" | custom-call | tf_op jit(solution)/shard_map/pallas_call | solution.py:701
  14.4 0.6 %collective-permute-start.4 = (f32[24,4,8,128]{3,2,1,0:T(8,128)S(1)}, f32[24,4,8,128]{3,2,1,0:T(8,128)S(1)}, u32[]{:S(2)}, u32[]{:S(2)}) collective-permute-start(f32[24,4,8,128]{3,2,1,0:T(8,128)S(1)} %get-tuple-element.100), channel_id=1, source_target_pairs={{0,1},{1,0},{2,3},{3,2},{4,5},{5,4},{6,7},{7,6},{8,9},{9,8},{10,11... | collective-permute-start | bytes 1179656 | tf_op jit(solution)/shard_map/ppermute | solution.py:713
  14.9 3.0 %collective-permute-start.1 = (f32[24,4,8,128]{3,2,1,0:T(8,128)S(1)}, f32[24,4,8,128]{3,2,1,0:T(8,128)S(1)}, u32[]{:S(2)}, u32[]{:S(2)}) collective-permute-start(f32[24,4,8,128]{3,2,1,0:T(8,128)S(1)} %get-tuple-element.74.refs_7_), channel_id=1, source_target_pairs={{1,2},{3,4},{5,6},{7,8},{9,10},{11,12},{13,14},{15,16},{17,18},{19... | collective-permute-start | bytes 1179656 | tf_op jit(solution)/shard_map/ppermute | solution.py:718
  18.0 1.1 %shard_map.93 = (f32[24,4,8,128]{3,2,1,0:T(8,128)S(1)}, f32[24,8,8,128]{3,2,1,0:T(8,128)S(1)}, f32[10,8,128]{2,1,0:T(8,128)S(1)}) custom-call(f32[24,16,8,128]{3,2,1,0:T(8,128)S(1)} %get-tuple-element.96.refs_0_.refs_13_.refs_7_, f32[1,12,8,128]{3,2,1,0:T(8,128)S(1)} %get-tuple-element.79.refs_3_.refs_9_.refs_2_.refs_1_, ...), custom_call_target="tpu_custom_call" | custom-call | tf_op jit(solution)/shard_map/pallas_call | solution.py:701
  19.1 0.0 collective-permute-done.4.refs_0_
  19.1 0.3 shard_map.94
  19.4 3.1 %collective-permute-done.refs_0_ = f32[62,4,8,128]{3,2,1,0:T(8,128)S(1)} collective-permute-done((f32[62,4,8,128]{3,2,1,0:T(8,128)S(1)}, f32[62,4,8,128]{3,2,1,0:T(8,128)S(1)}, u32[]{:S(2)}, u32[]{:S(2)}) %collective-permute-start) | collective-permute-done | bytes 1015840 | tf_op jit(solution)/shard_map/ppermute | solution.py:718
  22.5 3.9 %shard_map.95 = (f32[12,4,8,128]{3,2,1,0:T(8,128)S(1)}, f32[12,4,8,128]{3,2,1,0:T(8,128)S(1)}, f32[11,4,8,128]{3,2,1,0:T(8,128)S(1)}, f32[24,8,8,128]{3,2,1,0:T(...) custom-call(f32[62,4,8,128]{3,2,1,0:T(8,128)S(1)} %collective-permut, ...), custom_call_target="tpu_custom_call" | custom-call | tf_op jit(solution)/shard_map/pallas_call | solution.py:701
  26.4 0.3 collective-permute-done.1.refs_1_
  26.8 0.5 shard_map.96
  27.3 23.5 %all_to_all.11 = f32[128,1,128]{2,1,0:T(1,128)S(1)} all-to-all(f32[128,1,128]{2,1,0:T(1,128)S(1)} %bitcast.50), channel_id=1, replica_groups=mesh['flow_0'=4,'flow_1'=4,'flow_2'=4,'flow_3'=2] {'flow_0','flow_1','fl..., dimensions={0} | all-to-all | bytes 131072 | tf_op jit(solution)/shard_map/all_to_all | solution.py:862
  50.8 2.7 %shard_map.97 = (f32[24,3,64,128]{3,2,1,0:T(8,128)}, f32[24,3,64,128]{3,2,1,0:T(8,128)}) custom-call(f32[128,128]{1,0:T(8,128)S(1)} %bitcast.49, f32[24,12,8,128]{3,2,1,0:T(8,128)S(1)} %get-tuple-element.77.refs_0_.refs_1_, f32[24,4,8,128]{3,2,1,0:T(8,128)S(1)} %get-tuple-element.78.refs_1_.refs_2_, ...), custom_call_target="tpu_custom_call" | custom-call | tf_op jit(solution)/shard_map/pallas_call | solution.py:701
Async XLA Ops:
  5.3 5.9 %collective-permute-start.2 = (f32[24,4,8,128]{3,2,1,0:T(8,128)S(1)}, f32[24,4,8,128]{3,2,1,0:T(8,128)S(1)}, u32[]{:S(2)}, u32[]{:S(2)}) collective-permute-start(f32[24,4,8,128]{3,2,1,0:T(8,128)S(1)} %get-tuple-element.82), channel_id=1, source_target_pairs={{0,1},{1,0},{2,3},{3,2},{4,5},{5,4},{6,7},{7,6},{8,9},{9,8},{10,11... | collective-permute-start | bytes 1179656 | tf_op jit(solution)/shard_map/ppermute | solution.py:713
  6.8 15.8 %collective-permute-start = (f32[62,4,8,128]{3,2,1,0:T(8,128)S(1)}, f32[62,4,8,128]{3,2,1,0:T(8,128)S(1)}, u32[]{:S(2)}, u32[]{:S(2)}) collective-permute-start(f32[62,4,8,128]{3,2,1,0:T(8,128)S(1)} %get-tuple-element.61), channel_id=1, source_target_pairs={{1,2},{3,4},{5,6},{7,8},{9,10},{11,12},{13,14},{15,16},{17,18},{19... | collective-permute-start | bytes 3047432 | tf_op jit(solution)/shard_map/ppermute | solution.py:718
  11.9 1.9 %collective-permute-start.3 = (f32[24,4,8,128]{3,2,1,0:T(8,128)S(1)}, f32[24,4,8,128]{3,2,1,0:T(8,128)S(1)}, u32[]{:S(2)}, u32[]{:S(2)}) collective-permute-start(f32[24,4,8,128]{3,2,1,0:T(8,128)S(1)} %get-tuple-element.94), channel_id=1, source_target_pairs={{0,1},{1,0},{2,3},{3,2},{4,5},{5,4},{6,7},{7,6},{8,9},{9,8},{10,11... | collective-permute-start | bytes 1179656 | tf_op jit(solution)/shard_map/ppermute | solution.py:713
  14.4 4.8 %collective-permute-start.4 = (f32[24,4,8,128]{3,2,1,0:T(8,128)S(1)}, f32[24,4,8,128]{3,2,1,0:T(8,128)S(1)}, u32[]{:S(2)}, u32[]{:S(2)}) collective-permute-start(f32[24,4,8,128]{3,2,1,0:T(8,128)S(1)} %get-tuple-element.100), channel_id=1, source_target_pairs={{0,1},{1,0},{2,3},{3,2},{4,5},{5,4},{6,7},{7,6},{8,9},{9,8},{10,11... | collective-permute-start | bytes 1179656 | tf_op jit(solution)/shard_map/ppermute | solution.py:713
  14.9 11.8 %collective-permute-start.1 = (f32[24,4,8,128]{3,2,1,0:T(8,128)S(1)}, f32[24,4,8,128]{3,2,1,0:T(8,128)S(1)}, u32[]{:S(2)}, u32[]{:S(2)}) collective-permute-start(f32[24,4,8,128]{3,2,1,0:T(8,128)S(1)} %get-tuple-element.74.refs_7_), channel_id=1, source_target_pairs={{1,2},{3,4},{5,6},{7,8},{9,10},{11,12},{13,14},{15,16},{17,18},{19... | collective-permute-start | bytes 1179656 | tf_op jit(solution)/shard_map/ppermute | solution.py:718

commit v7 on v6

--- a/solution.py
+++ b/solution.py
@@ -431,6 +431,11 @@
     write_sums(r.sums, loop_sums(pairs_of(3), step))
 
 
+def in_lane(out, i, value):
+    value = jnp.sum(jnp.sum(value, axis=0, keepdims=True), axis=1, keepdims=True)
+    return out + jnp.where(lanes() == i, value, 0.0)
+
+
 def band_kernel(r):
     masks = cross_masks()
     beyond = span(ROWS, ROWS + REACH)
@@ -499,9 +504,16 @@
                 r.nsum3[plane, t - 20] = total
 
     sums.update(loop_sums(pairs_of(3), third))
-    zero = jnp.zeros(TILE, F32)
+    out = jnp.zeros(TILE, F32)
     for i, pair in enumerate(GRAM):
-        r.sums[i] = r.sums2[i] + r.sums3[i] + r.sums4[i] + sums.get(pair, zero)
+        value = r.sums2[i] + r.sums3[i] + r.sums4[i]
+        if pair in sums:
+            value = value + sums[pair]
+        if pair[1] == 3:
+            r.sums[pair[0]] = value
+        else:
+            out = in_lane(out, i, value)
+    r.sums[4] = out
 
 
 def last_b_kernel(r):
@@ -531,15 +543,11 @@
             r.u3[plane, t - 20] = value
             with_all(add, 3, value, plane, t, (u0, u1, u2))
 
-    sums = loop_sums(pairs_of(3), step, 12)
-    lane = lanes()
-    out = jnp.zeros(TILE, F32)
+    sums = loop_sums(pairs_of(3), step, 6)
+    out = r.sums[4]
     for i, pair in enumerate(GRAM):
-        value = r.sums[i]
-        if pair in sums:
-            value = value + sums[pair]
-        value = jnp.sum(jnp.sum(value, axis=0, keepdims=True), axis=1, keepdims=True)
-        out = out + jnp.where(lane == i, value, 0.0)
+        if pair[1] == 3:
+            out = in_lane(out, i, r.sums[pair[0]] + sums[pair])
     for i in range(r.payload.shape[0] // 8):
         r.payload[pl.ds(8 * i, 8), :] = out
 
@@ -672,7 +680,7 @@
         pltpu.make_async_copy(r.buf_s.at[plane], r.out_s.at[plane], r.sem_s).start()
         pltpu.make_async_copy(r.buf_r.at[plane], r.out_r.at[plane], r.sem_r).start()
 
-    over_planes(step, 2)
+    over_planes(step, 4)
     pltpu.make_async_copy(r.buf_s, r.out_s, r.sem_s).wait()
     pltpu.make_async_copy(r.buf_r, r.out_r, r.sem_r).wait()
 
@@ -843,7 +851,7 @@
             "s2": vmem(PLANES, 8),
             "u3": vmem(PLANES, 8),
             "nsum3": edge,
-            "sums": vmem(10),
+            "sums": vmem(5),
         },
     )
     b2 = call(

time: 53.7 us -> 53.6 us (level)
  no operation moved by 1% of the time
where the time goes in v7:
time: 53.6 us; the launch traced here: 53.4 us
  blocking collectives  23.5 us (44%)
  Pallas kernels  17.6 us (33%)
  starting transfers between devices  8.27 us (15%)
  waiting for transfers between devices  3.38 us (6%)
  between operations  0.74 us (1%)
    all_to_all x1, blocking collectives, body(): lax.all_to_all(b2['payload'], FLOW, split_axis=0, concat_axis=0, tiled=True)  23.5 us
    pallas_call x12, Pallas kernels, call(): pl.pallas_call(run, out_shape=list(outs.values()), in_specs=[in_specs or...  17.6 us
    ppermute x2, starting transfers between devices, across(): return lax.ppermute(x, FLOW, pairs + [(b, a) for a, b in pairs])  6.15 us
    ppermute x2, waiting for transfers between devices, across(): return lax.ppermute(x, FLOW, pairs + [(b, a) for a, b in pairs])  3.37 us
    ppermute x3, starting transfers between devices, within(): return lax.ppermute(x, FLOW, [(i, i ^ 1) for i in range(128)])  2.12 us
  transfers between devices with their start and end apart: 5, of which 2 were waited for; matrix products, arithmetic and copies ran while one was open for 0% of the time, Pallas kernels for 18%

profile of v7, /device:TPU:1, one launch (start us, length us, event | category | flops | bytes accessed | tf_op | source)
XLA Modules:
  0.0 53.4 jit_solution(15500380459544641251)
XLA Ops:
  0.6 2.3 %shard_map.86 = (f32[12,8,8,128]{3,2,1,0:T(8,128)S(1)}, f32[12,8,8,128]{3,2,1,0:T(8,128)S(1)}, f32[11,8,8,128]{3,2,1,0:T(8,128)S(1)}, f32[1,8,8,128]{3,2,1,0:T(8...) custom-call(f32[24,3,64,128]{3,2,1,0:T(8,128)} %bitcast.51, ...), custom_call_target="tpu_custom_call" | custom-call | tf_op jit(solution)/shard_map/pallas_call | solution.py:709
  2.9 0.9 %shard_map.87 = (f32[12,4,8,128]{3,2,1,0:T(8,128)S(1)}, f32[12,4,8,128]{3,2,1,0:T(8,128)S(1)}, f32[11,4,8,128]{3,2,1,0:T(8,128)S(1)}, f32[1,4,8,128]{3,2,1,0:T(8...) custom-call(f32[24,8,8,128]{3,2,1,0:T(8,128)S(1)} %get-tuple-element, ...), custom_call_target="tpu_custom_call" | custom-call | tf_op jit(solution)/shard_map/pallas_call | solution.py:709
  3.8 1.5 %shard_map.88 = (f32[12,12,8,128]{3,2,1,0:T(8,128)S(1)}, f32[12,12,8,128]{3,2,1,0:T(8,128)S(1)}, f32[11,12,8,128]{3,2,1,0:T(8,128)S(1)}, f32[1,12,8,128]{3,2,1,0...) custom-call(f32[24,3,64,128]{3,2,1,0:T(8,128)S(1)} %get-tuple-element.6, ...), custom_call_target="tpu_custom_call" | custom-call | tf_op jit(solution)/shard_map/pallas_call | solution.py:709
  5.3 1.5 %collective-permute-start.2 = (f32[24,4,8,128]{3,2,1,0:T(8,128)S(1)}, f32[24,4,8,128]{3,2,1,0:T(8,128)S(1)}, u32[]{:S(2)}, u32[]{:S(2)}) collective-permute-start(f32[24,4,8,128]{3,2,1,0:T(8,128)S(1)} %get-tuple-element.82), channel_id=1, source_target_pairs={{0,1},{1,0},{2,3},{3,2},{4,5},{5,4},{6,7},{7,6},{8,9},{9,8},{10,11... | collective-permute-start | bytes 1179656 | tf_op jit(solution)/shard_map/ppermute | solution.py:721
  6.8 3.1 %collective-permute-start = (f32[62,4,8,128]{3,2,1,0:T(8,128)S(1)}, f32[62,4,8,128]{3,2,1,0:T(8,128)S(1)}, u32[]{:S(2)}, u32[]{:S(2)}) collective-permute-start(f32[62,4,8,128]{3,2,1,0:T(8,128)S(1)} %get-tuple-element.61), channel_id=1, source_target_pairs={{1,2},{3,4},{5,6},{7,8},{9,10},{11,12},{13,14},{15,16},{17,18},{19... | collective-permute-start | bytes 3047432 | tf_op jit(solution)/shard_map/ppermute | solution.py:726
  9.9 1.3 %shard_map.89 = (f32[24,4,8,128]{3,2,1,0:T(8,128)S(1)}, f32[24,12,8,128]{3,2,1,0:T(8,128)S(1)}) custom-call(f32[24,12,8,128]{3,2,1,0:T(8,128)S(1)} %get-tuple-element.77.refs_0_.refs_1_, f32[24,4,8,128]{3,2,1,0:T(8,128)S(1)} %get-tuple-element.78.refs_1_.refs_2_, f32[24,8,8,128]{3,2,1,0:T(8,128)S(1)} %get-tuple-element.62.refs_0_.refs_2_.refs_6_.refs_3_, ...), custom_call_target="tpu_custom_call" | custom-call | tf_op jit(solution)/shard_map/pallas_call | solution.py:709
  11.2 0.0 collective-permute-done.2.refs_0_
  11.2 0.6 %shard_map.90 = (f32[24,4,8,128]{3,2,1,0:T(8,128)S(1)}, f32[24,16,8,128]{3,2,1,0:T(8,128)S(1)}, f32[24,4,8,128]{3,2,1,0:T(8,128)S(1)}) custom-call(f32[24,4,8,128]{3,2,1,0:T(8,128)S(1)} %collective-permute-done.2.refs_0_, f32[24,4,8,128]{3,2,1,0:T(8,128)S(1)} %get-tuple-element.83.refs_1_, ...), custom_call_target="tpu_custom_call" | custom-call | tf_op jit(solution)/shard_map/pallas_call | solution.py:709
  11.9 0.1 collective-permute-start.3
  11.9 1.8 %shard_map.91 = (f32[24,4,8,128]{3,2,1,0:T(8,128)S(1)}, f32[24,12,8,128]{3,2,1,0:T(8,128)S(1)}, f32[10,8,128]{2,1,0:T(8,128)S(1)}) custom-call(f32[24,16,8,128]{3,2,1,0:T(8,128)S(1)} %get-tuple-element.90.refs_0_.refs_10_.refs_4_, f32[24,4,8,128]{3,2,1,0:T(8,128)S(1)} %get-tuple-element.91.refs_1_.refs_11_.refs_5_, ...), custom_call_target="tpu_custom_call" | custom-call | tf_op jit(solution)/shard_map/pallas_call | solution.py:709
  13.7 0.0 collective-permute-done.3.refs_0_
  13.7 0.6 %shard_map.92 = (f32[24,4,8,128]{3,2,1,0:T(8,128)S(1)}, f32[24,16,8,128]{3,2,1,0:T(8,128)S(1)}, f32[24,4,8,128]{3,2,1,0:T(8,128)S(1)}) custom-call(f32[24,4,8,128]{3,2,1,0:T(8,128)S(1)} %collective-permute-done.3.refs_0_, f32[24,4,8,128]{3,2,1,0:T(8,128)S(1)} %get-tuple-element.95.refs_1_, ...), custom_call_target="tpu_custom_call" | custom-call | tf_op jit(solution)/shard_map/pallas_call | solution.py:709
  14.4 0.6 %collective-permute-start.4 = (f32[24,4,8,128]{3,2,1,0:T(8,128)S(1)}, f32[24,4,8,128]{3,2,1,0:T(8,128)S(1)}, u32[]{:S(2)}, u32[]{:S(2)}) collective-permute-start(f32[24,4,8,128]{3,2,1,0:T(8,128)S(1)} %get-tuple-element.100), channel_id=1, source_target_pairs={{0,1},{1,0},{2,3},{3,2},{4,5},{5,4},{6,7},{7,6},{8,9},{9,8},{10,11... | collective-permute-start | bytes 1179656 | tf_op jit(solution)/shard_map/ppermute | solution.py:721
  14.9 3.0 %collective-permute-start.1 = (f32[24,4,8,128]{3,2,1,0:T(8,128)S(1)}, f32[24,4,8,128]{3,2,1,0:T(8,128)S(1)}, u32[]{:S(2)}, u32[]{:S(2)}) collective-permute-start(f32[24,4,8,128]{3,2,1,0:T(8,128)S(1)} %get-tuple-element.74.refs_7_), channel_id=1, source_target_pairs={{1,2},{3,4},{5,6},{7,8},{9,10},{11,12},{13,14},{15,16},{17,18},{19... | collective-permute-start | bytes 1179656 | tf_op jit(solution)/shard_map/ppermute | solution.py:726
  18.0 1.1 %shard_map.93 = (f32[24,4,8,128]{3,2,1,0:T(8,128)S(1)}, f32[24,8,8,128]{3,2,1,0:T(8,128)S(1)}, f32[10,8,128]{2,1,0:T(8,128)S(1)}) custom-call(f32[24,16,8,128]{3,2,1,0:T(8,128)S(1)} %get-tuple-element.96.refs_0_.refs_13_.refs_7_, f32[1,12,8,128]{3,2,1,0:T(8,128)S(1)} %get-tuple-element.79.refs_3_.refs_9_.refs_2_.refs_1_, ...), custom_call_target="tpu_custom_call" | custom-call | tf_op jit(solution)/shard_map/pallas_call | solution.py:709
  19.1 0.0 collective-permute-done.4.refs_0_
  19.1 0.3 shard_map.94
  19.4 3.1 %collective-permute-done.refs_0_ = f32[62,4,8,128]{3,2,1,0:T(8,128)S(1)} collective-permute-done((f32[62,4,8,128]{3,2,1,0:T(8,128)S(1)}, f32[62,4,8,128]{3,2,1,0:T(8,128)S(1)}, u32[]{:S(2)}, u32[]{:S(2)}) %collective-permute-start) | collective-permute-done | bytes 1015840 | tf_op jit(solution)/shard_map/ppermute | solution.py:726
  22.5 4.0 %shard_map.95 = (f32[12,4,8,128]{3,2,1,0:T(8,128)S(1)}, f32[12,4,8,128]{3,2,1,0:T(8,128)S(1)}, f32[11,4,8,128]{3,2,1,0:T(8,128)S(1)}, f32[24,8,8,128]{3,2,1,0:T(...) custom-call(f32[62,4,8,128]{3,2,1,0:T(8,128)S(1)} %collective-permut, ...), custom_call_target="tpu_custom_call" | custom-call | tf_op jit(solution)/shard_map/pallas_call | solution.py:709
  26.5 0.2 collective-permute-done.1.refs_1_
  26.8 0.5 %shard_map.96 = (f32[24,4,8,128]{3,2,1,0:T(8,128)S(1)}, f32[128,128]{1,0:T(8,128)S(1)}) custom-call(f32[62,4,8,128]{3,2,1,0:T(8,128)S(1)} %collective-permute-done.refs_0_, f32[24,4,8,128]{3,2,1,0:T(8,128)S(1)} %collective-permute-done.1.refs_1_, f32[1,8,8,128]{3,2,1,0:T(8,128)S(1)} %get-tuple-element.63.refs_1_.refs_5_.refs_2_, ...), custom_call_target="tpu_custom_call" | custom-call | tf_op jit(solution)/shard_map/pallas_call | solution.py:709
  27.3 23.5 %all_to_all.11 = f32[128,1,128]{2,1,0:T(1,128)S(1)} all-to-all(f32[128,1,128]{2,1,0:T(1,128)S(1)} %bitcast.50), channel_id=1, replica_groups=mesh['flow_0'=4,'flow_1'=4,'flow_2'=4,'flow_3'=2] {'flow_0','flow_1','fl..., dimensions={0} | all-to-all | bytes 131072 | tf_op jit(solution)/shard_map/all_to_all | solution.py:870
  50.8 2.7 %shard_map.97 = (f32[24,3,64,128]{3,2,1,0:T(8,128)}, f32[24,3,64,128]{3,2,1,0:T(8,128)}) custom-call(f32[128,128]{1,0:T(8,128)S(1)} %bitcast.49, f32[24,12,8,128]{3,2,1,0:T(8,128)S(1)} %get-tuple-element.77.refs_0_.refs_1_, f32[24,4,8,128]{3,2,1,0:T(8,128)S(1)} %get-tuple-element.78.refs_1_.refs_2_, ...), custom_call_target="tpu_custom_call" | custom-call | tf_op jit(solution)/shard_map/pallas_call | solution.py:709
Async XLA Ops:
  5.3 5.9 %collective-permute-start.2 = (f32[24,4,8,128]{3,2,1,0:T(8,128)S(1)}, f32[24,4,8,128]{3,2,1,0:T(8,128)S(1)}, u32[]{:S(2)}, u32[]{:S(2)}) collective-permute-start(f32[24,4,8,128]{3,2,1,0:T(8,128)S(1)} %get-tuple-element.82), channel_id=1, source_target_pairs={{0,1},{1,0},{2,3},{3,2},{4,5},{5,4},{6,7},{7,6},{8,9},{9,8},{10,11... | collective-permute-start | bytes 1179656 | tf_op jit(solution)/shard_map/ppermute | solution.py:721
  6.8 15.8 %collective-permute-start = (f32[62,4,8,128]{3,2,1,0:T(8,128)S(1)}, f32[62,4,8,128]{3,2,1,0:T(8,128)S(1)}, u32[]{:S(2)}, u32[]{:S(2)}) collective-permute-start(f32[62,4,8,128]{3,2,1,0:T(8,128)S(1)} %get-tuple-element.61), channel_id=1, source_target_pairs={{1,2},{3,4},{5,6},{7,8},{9,10},{11,12},{13,14},{15,16},{17,18},{19... | collective-permute-start | bytes 3047432 | tf_op jit(solution)/shard_map/ppermute | solution.py:726
  11.9 1.9 %collective-permute-start.3 = (f32[24,4,8,128]{3,2,1,0:T(8,128)S(1)}, f32[24,4,8,128]{3,2,1,0:T(8,128)S(1)}, u32[]{:S(2)}, u32[]{:S(2)}) collective-permute-start(f32[24,4,8,128]{3,2,1,0:T(8,128)S(1)} %get-tuple-element.94), channel_id=1, source_target_pairs={{0,1},{1,0},{2,3},{3,2},{4,5},{5,4},{6,7},{7,6},{8,9},{9,8},{10,11... | collective-permute-start | bytes 1179656 | tf_op jit(solution)/shard_map/ppermute | solution.py:721
  14.4 4.8 %collective-permute-start.4 = (f32[24,4,8,128]{3,2,1,0:T(8,128)S(1)}, f32[24,4,8,128]{3,2,1,0:T(8,128)S(1)}, u32[]{:S(2)}, u32[]{:S(2)}) collective-permute-start(f32[24,4,8,128]{3,2,1,0:T(8,128)S(1)} %get-tuple-element.100), channel_id=1, source_target_pairs={{0,1},{1,0},{2,3},{3,2},{4,5},{5,4},{6,7},{7,6},{8,9},{9,8},{10,11... | collective-permute-start | bytes 1179656 | tf_op jit(solution)/shard_map/ppermute | solution.py:721
  14.9 11.8 %collective-permute-start.1 = (f32[24,4,8,128]{3,2,1,0:T(8,128)S(1)}, f32[24,4,8,128]{3,2,1,0:T(8,128)S(1)}, u32[]{:S(2)}, u32[]{:S(2)}) collective-permute-start(f32[24,4,8,128]{3,2,1,0:T(8,128)S(1)} %get-tuple-element.74.refs_7_), channel_id=1, source_target_pairs={{1,2},{3,4},{5,6},{7,8},{9,10},{11,12},{13,14},{15,16},{17,18},{19... | collective-permute-start | bytes 1179656 | tf_op jit(solution)/shard_map/ppermute | solution.py:726
